TPU v7x, 256 devices: a whole 4x4x8 slice. The times are simulated.
256 devices in a mesh: gx: 8 (over z_hi, core), gy: 4 (over x), gz: 8 (over z_lo, y).
Axes of the slice: x: 4, y: 4, z: 8 (z_hi: 4, z_lo: 2; z = z_hi * 2 + z_lo), core: 2. Of those that a mesh axis runs over, the one named last changes fastest.
Arguments:
- right_side: float32 [3, 128, 64, 1024], P(None, 'gx', 'gy', 'gz'), may hold values from -64 to 64
- damage: int32 [128, 64, 1024], P('gx', 'gy', 'gz'), may hold values from 0 to 15
Outputs:
- displacement: float32 [3, 128, 64, 1024], P(None, 'gx', 'gy', 'gz')
- norms: float32 [2], replicated
All inputs are finite; a program needn't handle non-finite values.
Results may differ from a plain program's by a relative error of at most 0.0003.
Values sent between devices are 32-bit elements; how exact they have to be, the bound alone decides.
No kernel may reach another device: no remote copies, remote signals or barrier semaphores. Data moves between devices by JAX's collectives and lax.ppermute only.
A program may use at most 64 MiB of HBM per device.

v0:
```python
import functools

import jax
import jax.numpy as jnp
from jax import lax
from jax.sharding import Mesh
from jax.sharding import PartitionSpec as P

BLOCK = 16
COARSE = 8
GX = ("gx_0", "gx_1")
GZ = ("gz_0", "gz_1")
GY_GZ = ("gy", "gz_0", "gz_1")
GX_GY_GZ = ("gx_0", "gx_1", "gy", "gz_0", "gz_1")


FLOOR_STIFFNESS = 0.05
MASS_TERM = 0.001
COUPLING = 2.5
RELAXATION = 0.6


def from_everyone(value, axis):
    length = lax.axis_size(axis)
    return lax.all_to_all(
        jnp.broadcast_to(value[None], (length, *value.shape)), axis, 0, 0, tiled=True
    )


def in_order(parts, dim):
    lengths = list(parts.shape[1:])
    lengths[dim] *= parts.shape[0]
    return jnp.moveaxis(parts, 0, dim).reshape(lengths)


def gathered_copies(value, axis, dim):
    parts = from_everyone(value, axis)
    return in_order(parts, dim)


def padded_2(block, sides, width):
    for axis, dim in sides:
        count = lax.axis_size(axis)
        forward = [(i, i + 1) for i in range(count - 1)]
        backward = [(target, source) for source, target in forward]
        low = lax.ppermute(
            lax.slice_in_dim(block, block.shape[dim] - width, None, axis=dim), axis, forward
        )
        high = lax.ppermute(lax.slice_in_dim(block, 0, width, axis=dim), axis, backward)
        block = jnp.concatenate([low, block, high], axis=dim)
    return block


def by_axis(value, axes):
    return functools.reduce(lax.psum, axes, value)


def stiffness_of(damage):
    damage_level = damage.astype(jnp.float32) / 15.0
    return (1.0 - damage_level) ** 2 * (1.0 - FLOOR_STIFFNESS) + FLOOR_STIFFNESS


def diagonal_of(coefficient, mass_term):
    return coefficient * (6.0 + 2.0 * COUPLING) + mass_term


def stencil(padded, coefficient, mass_term):
    extent = (padded.shape[1] - 2, padded.shape[2] - 2, padded.shape[3] - 2)

    def neighbour(component, offset):
        return padded[
            component,
            1 + offset[0] : 1 + offset[0] + extent[0],
            1 + offset[1] : 1 + offset[1] + extent[1],
            1 + offset[2] : 1 + offset[2] + extent[2],
        ]

    def joined(first, second, factor):
        return tuple((first[number] + factor * second[number] for number in range(3)))

    unit_steps = ((1, 0, 0), (0, 1, 0), (0, 0, 1))
    images = []
    for component in range(3):
        centre = neighbour(component, (0, 0, 0))
        beside_all = jnp.zeros_like(centre)
        for partner in range(3):
            step_up = unit_steps[partner]
            step_down = joined((0, 0, 0), step_up, -1)
            beside_all = (
                beside_all + neighbour(component, step_up) + neighbour(component, step_down)
            )
        own_up = unit_steps[component]
        own_down = joined((0, 0, 0), own_up, -1)
        axial_part = 2.0 * centre - neighbour(component, own_up) - neighbour(component, own_down)
        mixed_part = jnp.zeros_like(centre)
        for partner in range(3):
            if partner != component:
                other_up = unit_steps[partner]
                mixed_part = (
                    mixed_part
                    + neighbour(partner, joined(own_up, other_up, 1))
                    - neighbour(partner, joined(own_up, other_up, -1))
                    - neighbour(partner, joined(own_down, other_up, 1))
                    + neighbour(partner, joined(own_down, other_up, -1))
                )
        images.append(
            coefficient * (6.0 * centre - beside_all + COUPLING * (axial_part - 0.25 * mixed_part))
            + mass_term * centre
        )
    return jnp.stack(images)


def crop_by(source, margin):
    return source[
        ...,
        margin : source.shape[-3] - margin,
        margin : source.shape[-2] - margin,
        margin : source.shape[-1] - margin,
    ]


def inside(margin, extent):
    position_x = (
        lax.axis_index(GX) * extent[0]
        + jnp.arange(extent[0] + 2 * margin, dtype=jnp.int32)
        - margin
    )
    position_y = (
        lax.axis_index("gy") * extent[1]
        + jnp.arange(extent[1] + 2 * margin, dtype=jnp.int32)
        - margin
    )
    position_z = (
        lax.axis_index(GZ) * extent[2]
        + jnp.arange(extent[2] + 2 * margin, dtype=jnp.int32)
        - margin
    )
    flag_x = ((position_x >= 0) & (position_x < extent[0] * lax.axis_size(GX))).astype(jnp.float32)
    flag_y = ((position_y >= 0) & (position_y < extent[1] * lax.axis_size("gy"))).astype(
        jnp.float32
    )
    flag_z = ((position_z >= 0) & (position_z < extent[2] * lax.axis_size(GZ))).astype(jnp.float32)
    return flag_x[:, None, None] * flag_y[None, :, None] * flag_z[None, None, :]


def block_sums(source):
    channels, size_x, size_y, size_z = source.shape
    return jnp.sum(
        source.reshape(
            channels, size_x // BLOCK, BLOCK, size_y // BLOCK, BLOCK, size_z // BLOCK, BLOCK
        ),
        axis=(2, 4, 6),
    )


def spread(block_field):
    channels, size_x, size_y, size_z = block_field.shape
    widened = jnp.broadcast_to(
        block_field[:, :, None, :, None, :, None],
        (channels, size_x, BLOCK, size_y, BLOCK, size_z, BLOCK),
    )
    return widened.reshape(channels, size_x * BLOCK, size_y * BLOCK, size_z * BLOCK)


def coarse_sweeps(coarse_load, mean_stiffness, padder):
    coarse_coefficient = BLOCK**2 * mean_stiffness
    coarse_mass = BLOCK**3 * MASS_TERM
    coarse_diagonal = diagonal_of(coarse_coefficient, coarse_mass)
    correction = RELAXATION * coarse_load / coarse_diagonal
    for repeat in range(COARSE - 1):
        coarse_image = stencil(padder(correction), coarse_coefficient, coarse_mass)
        correction = correction + RELAXATION * (coarse_load - coarse_image) / coarse_diagonal
    return correction


def coarse_correction(residual, coefficient):
    local_sums = jnp.concatenate(
        [block_sums(residual), block_sums(coefficient[None]) / BLOCK**3], axis=0
    )
    channels, size_x, size_y, size_z = local_sums.shape
    count_y = lax.axis_size("gy")
    count_z = lax.axis_size(GZ)
    gathered = gathered_copies(local_sums[None], GY_GZ, 0)
    coarse_slab = gathered.reshape(count_y, count_z, channels, size_x, size_y, size_z)
    coarse_slab = coarse_slab.transpose(2, 3, 0, 4, 1, 5).reshape(
        channels, size_x, count_y * size_y, count_z * size_z
    )

    def padder(coarse_field):
        widened = padded_2(coarse_field, ((GX, 1),), 1)
        return jnp.pad(widened, ((0, 0), (0, 0), (1, 1), (1, 1)))

    correction = coarse_sweeps(coarse_slab[:3], coarse_slab[3], padder)
    start_x = jnp.zeros((), jnp.int32)
    own_block = lax.dynamic_slice(
        correction,
        (
            jnp.zeros((), jnp.int32),
            start_x,
            lax.axis_index("gy") * size_y,
            lax.axis_index(GZ) * size_z,
        ),
        (3, size_x, size_y, size_z),
    )
    return spread(own_block)


def on_device(right_side, damage):
    coefficient = stiffness_of(damage)
    extent = coefficient.shape
    load_sum = by_axis(jnp.sum(right_side * right_side), GX_GY_GZ)
    stacked = jnp.concatenate([right_side, coefficient[None]], axis=0)
    widened = padded_2(stacked, ((GX, 1), ("gy", 2), (GZ, 3)), 2)
    load_wide = widened[:3]
    stiff_wide = widened[3]
    diag_wide = diagonal_of(stiff_wide, MASS_TERM)
    load_loop = crop_by(load_wide, 1)
    stiff_loop = crop_by(stiff_wide, 1)
    diag_loop = crop_by(diag_wide, 1)
    loop_mask = inside(1, extent)
    first_sweep = RELAXATION * load_wide / diag_wide
    second_sweep = (
        crop_by(first_sweep, 1)
        + RELAXATION * (load_loop - stencil(first_sweep, stiff_loop, MASS_TERM)) / diag_loop
    ) * loop_mask
    residual = right_side - stencil(second_sweep, coefficient, MASS_TERM)
    displacement = crop_by(second_sweep, 1) + coarse_correction(residual, coefficient)
    deep_field = padded_2(displacement, ((GX, 1), ("gy", 2), (GZ, 3)), 3)
    third_sweep = (
        crop_by(deep_field, 1)
        + RELAXATION * (load_wide - stencil(deep_field, stiff_wide, MASS_TERM)) / diag_wide
    ) * inside(2, extent)
    fourth_sweep = (
        crop_by(third_sweep, 1)
        + RELAXATION * (load_loop - stencil(third_sweep, stiff_loop, MASS_TERM)) / diag_loop
    ) * loop_mask
    displacement = crop_by(fourth_sweep, 1)
    residual = right_side - stencil(fourth_sweep, coefficient, MASS_TERM)
    total_count = (
        3
        * extent[0]
        * extent[1]
        * extent[2]
        * lax.axis_size(GX)
        * lax.axis_size("gy")
        * lax.axis_size(GZ)
    )
    residual_sum = by_axis(jnp.sum(residual * residual), GX_GY_GZ)
    norms = jnp.stack([jnp.sqrt(load_sum / total_count), jnp.sqrt(residual_sum / total_count)])
    return (displacement, norms)


def solution(mesh):
    torus = Mesh(
        mesh.devices.reshape(4, 2, mesh.shape["gy"], 2, 4), ("gx_0", "gx_1", "gy", "gz_0", "gz_1")
    )
    placed = (P(None, GX, "gy", GZ), P(GX, "gy", GZ))
    return jax.shard_map(
        on_device,
        mesh=torus,
        in_specs=placed,
        out_specs=(P(None, GX, "gy", GZ), P()),
        check_vma=False,
    )
```

profile of v0, /device:TPU:40, one launch (start us, length us, event | category | flops | bytes accessed | tf_op | source)
XLA Modules:
  0.0 239.6 jit_solution(8986494967420646442)
XLA Ops:
  5.6 4.8 %collective-permute-done.1 = f32[4,2,16,128]{3,2,1,0:T(8,128)S(1)} collective-permute-done((f32[4,2,16,128]{3,2,1,0:T(8,128)S(1)}, f32[4,2,16,128]{3,2,1,0:T(8,128)S(1)}, u32[]{:S(2)}, u32[]{:S(2)}) %collective-permute-start.1) | collective-permute-done | bytes 65568 | tf_op jit(solution)/shard_map/ppermute | solution.py:49
  12.9 4.6 %collective-permute-start.2 = (f32[4,20,2,128]{3,0,2,1:T(4,128)S(1)}, f32[4,20,2,128]{3,0,2,1:T(4,128)S(1)}, u32[]{:S(2)}, u32[]{:S(2)}) collective-permute-start(f32[4,20,2,128]{3,0,2,1:T(4,128)S(1)} %copy.326), channel_id=1, source_target_pairs={{0,8},{8,16},{16,24},{1,9},{9,17},{17,25},{2,10},{10,18},{18,26},{... | collective-permute-start | bytes 245768 | tf_op jit(solution)/shard_map/ppermute | solution.py:46
  21.4 2.4 collective-permute-start.5
  23.7 3.5 %collective-permute-start.4 = (f32[4,20,20,2]{2,0,3,1:T(4,128)S(1)}, f32[4,20,20,2]{2,0,3,1:T(4,128)S(1)}, u32[]{:S(2)}, u32[]{:S(2)}) collective-permute-start(f32[4,20,20,2]{2,0,3,1:T(4,128)S(1)} %copy.311), channel_id=1, source_target_pairs={{0,1},{1,2},{2,3},{3,4},{4,5},{5,6},{6,7},{8,9},{9,10},{10,11},{11... | collective-permute-start | bytes 38408 | tf_op jit(solution)/shard_map/ppermute | solution.py:46
  28.1 2.5 %collective-permute-done.4 = f32[4,20,20,2]{2,0,3,1:T(4,128)S(1)} collective-permute-done((f32[4,20,20,2]{2,0,3,1:T(4,128)S(1)}, f32[4,20,20,2]{2,0,3,1:T(4,128)S(1)}, u32[]{:S(2)}, u32[]{:S(2)}) %collective-permute-start.4) | collective-permute-done | bytes 12832 | tf_op jit(solution)/shard_map/ppermute | solution.py:46
  32.8 2.4 pad_maximum_fusion
  48.7 1.9 multiply_reduce_fusion
  52.1 16.7 %all_to_all.5 = f32[32,1,4,1,1,8]{5,2,4,3,1,0:T(4,128)S(1)} all-to-all(f32[32,1,4,1,1,8]{5,2,4,3,1,0:T(4,128)S(1)} %broadcast_in_dim.16), channel_id=1, replica_groups=mesh['gx_0'=4,'gx_1'=2,'gy'=4,'gz_0'=2,'gz_1'=4] {'gy','gz_0','gz_1'}, dimensions={0} | all-to-all | bytes 8192 | tf_op jit(solution)/shard_map/all_to_all | solution.py:25
  71.8 6.2 %collective-permute-done.6 = f32[3,1,4,64]{3,2,0,1:T(4,128)S(1)} collective-permute-done((f32[3,1,4,64]{3,2,0,1:T(4,128)S(1)}, f32[3,1,4,64]{3,2,0,1:T(4,128)S(1)}, u32[]{:S(2)}, u32[]{:S(2)}) %collective-permute-start.6) | collective-permute-done | bytes 3104 | tf_op jit(solution)/shard_map/ppermute | solution.py:49
  78.4 5.2 %collective-permute-start.9 = (f32[3,1,4,64]{3,2,0,1:T(4,128)S(1)}, f32[3,1,4,64]{3,2,0,1:T(4,128)S(1)}, u32[]{:S(2)}, u32[]{:S(2)}) collective-permute-start(f32[3,1,4,64]{3,2,0,1:T(4,128)S(1)} %divide_add_fusion.5), channel_id=1, source_target_pairs={{0,32},{32,64},{64,96},{96,128},{128,160},{160,192},{192,224},{1,3... | collective-permute-start | bytes 9224 | tf_op jit(solution)/shard_map/ppermute | solution.py:46
  85.0 3.8 %collective-permute-done.8 = f32[3,1,4,64]{3,2,0,1:T(4,128)S(1)} collective-permute-done((f32[3,1,4,64]{3,2,0,1:T(4,128)S(1)}, f32[3,1,4,64]{3,2,0,1:T(4,128)S(1)}, u32[]{:S(2)}, u32[]{:S(2)}) %collective-permute-start.8) | collective-permute-done | bytes 3104 | tf_op jit(solution)/shard_map/ppermute | solution.py:49
  89.1 7.0 %collective-permute-start.11 = (f32[3,1,4,64]{3,2,0,1:T(4,128)S(1)}, f32[3,1,4,64]{3,2,0,1:T(4,128)S(1)}, u32[]{:S(2)}, u32[]{:S(2)}) collective-permute-start(f32[3,1,4,64]{3,2,0,1:T(4,128)S(1)} %divide_add_fusion.4), channel_id=1, source_target_pairs={{0,32},{32,64},{64,96},{96,128},{128,160},{160,192},{192,224},{1,3... | collective-permute-start | bytes 9224 | tf_op jit(solution)/shard_map/ppermute | solution.py:46
  97.6 1.8 collective-permute-done.10
  99.8 5.9 %collective-permute-start.13 = (f32[3,1,4,64]{3,2,0,1:T(4,128)S(1)}, f32[3,1,4,64]{3,2,0,1:T(4,128)S(1)}, u32[]{:S(2)}, u32[]{:S(2)}) collective-permute-start(f32[3,1,4,64]{3,2,0,1:T(4,128)S(1)} %divide_add_fusion.3), channel_id=1, source_target_pairs={{0,32},{32,64},{64,96},{96,128},{128,160},{160,192},{192,224},{1,3... | collective-permute-start | bytes 9224 | tf_op jit(solution)/shard_map/ppermute | solution.py:46
  107.0 1.8 collective-permute-done.12
  109.1 5.9 %collective-permute-start.15 = (f32[3,1,4,64]{3,2,0,1:T(4,128)S(1)}, f32[3,1,4,64]{3,2,0,1:T(4,128)S(1)}, u32[]{:S(2)}, u32[]{:S(2)}) collective-permute-start(f32[3,1,4,64]{3,2,0,1:T(4,128)S(1)} %divide_add_fusion.2), channel_id=1, source_target_pairs={{0,32},{32,64},{64,96},{96,128},{128,160},{160,192},{192,224},{1,3... | collective-permute-start | bytes 9224 | tf_op jit(solution)/shard_map/ppermute | solution.py:46
  118.5 5.9 %collective-permute-start.17 = (f32[3,1,4,64]{3,2,0,1:T(4,128)S(1)}, f32[3,1,4,64]{3,2,0,1:T(4,128)S(1)}, u32[]{:S(2)}, u32[]{:S(2)}) collective-permute-start(f32[3,1,4,64]{3,2,0,1:T(4,128)S(1)} %divide_add_fusion.1), channel_id=1, source_target_pairs={{0,32},{32,64},{64,96},{96,128},{128,160},{160,192},{192,224},{1,3... | collective-permute-start | bytes 9224 | tf_op jit(solution)/shard_map/ppermute | solution.py:46
  127.9 5.9 %collective-permute-start.19 = (f32[3,1,4,64]{3,2,0,1:T(4,128)S(1)}, f32[3,1,4,64]{3,2,0,1:T(4,128)S(1)}, u32[]{:S(2)}, u32[]{:S(2)}) collective-permute-start(f32[3,1,4,64]{3,2,0,1:T(4,128)S(1)} %divide_add_fusion), channel_id=1, source_target_pairs={{0,32},{32,64},{64,96},{96,128},{128,160},{160,192},{192,224},{1,3... | collective-permute-start | bytes 9224 | tf_op jit(solution)/shard_map/ppermute | solution.py:46
  137.7 5.9 %collective-permute-start.20 = (f32[3,3,16,128]{3,2,1,0:T(8,128)S(1)}, f32[3,3,16,128]{3,2,1,0:T(8,128)S(1)}, u32[]{:S(2)}, u32[]{:S(2)}) collective-permute-start(f32[3,3,16,128]{3,2,1,0:T(8,128)S(1)} %get-tuple-element.34), channel_id=1, source_target_pairs={{0,32},{32,64},{64,96},{96,128},{128,160},{160,192},{192,224},{1,3... | collective-permute-start | bytes 221192 | tf_op jit(solution)/shard_map/ppermute | solution.py:46
  145.1 1.8 collective-permute-done.21
  148.2 4.6 %collective-permute-start.22 = (f32[3,22,3,128]{3,1,2,0:T(8,128)S(1)}, f32[3,22,3,128]{3,1,2,0:T(8,128)S(1)}, u32[]{:S(2)}, u32[]{:S(2)}) collective-permute-start(f32[3,22,3,128]{3,1,2,0:T(8,128)S(1)} %copy.317), channel_id=1, source_target_pairs={{0,8},{8,16},{16,24},{1,9},{9,17},{17,25},{2,10},{10,18},{18,26},{... | collective-permute-start | bytes 304136 | tf_op jit(solution)/shard_map/ppermute | solution.py:46
  157.1 2.3 copy.321
  160.6 3.4 %collective-permute-start.25 = (f32[3,22,22,3]{2,1,3,0:T(8,128)}, f32[3,22,22,3]{2,1,3,0:T(8,128)}, u32[]{:S(2)}, u32[]{:S(2)}) collective-permute-start(f32[3,22,22,3]{2,1,3,0:T(8,128)} %copy.322), channel_id=1, source_target_pairs={{1,0},{2,1},{3,2},{4,3},{5,4},{6,5},{7,6},{9,8},{10,9},{11,10},{12... | collective-permute-start | bytes 52280 | tf_op jit(solution)/shard_map/ppermute | solution.py:49
  164.0 2.5 %collective-permute-start.24 = (f32[3,22,22,3]{2,1,3,0:T(8,128)}, f32[3,22,22,3]{2,1,3,0:T(8,128)}, u32[]{:S(2)}, u32[]{:S(2)}) collective-permute-start(f32[3,22,22,3]{2,1,3,0:T(8,128)} %copy.321), channel_id=1, source_target_pairs={{0,1},{1,2},{2,3},{3,4},{4,5},{5,6},{6,7},{8,9},{9,10},{10,11},{11... | collective-permute-start | bytes 52280 | tf_op jit(solution)/shard_map/ppermute | solution.py:46
  167.4 3.6 %collective-permute-done.24 = f32[3,22,22,3]{2,1,3,0:T(8,128)} collective-permute-done((f32[3,22,22,3]{2,1,3,0:T(8,128)}, f32[3,22,22,3]{2,1,3,0:T(8,128)}, u32[]{:S(2)}, u32[]{:S(2)}) %collective-permute-start.24) | collective-permute-done | bytes 17456 | tf_op jit(solution)/shard_map/ppermute | solution.py:46
  172.4 2.3 copy.324
  174.7 2.2 pad_maximum_fusion.1
  191.1 14.4 %all-reduce.9 = (f32[]{:T(128)}, f32[]{:T(128)}) all-reduce(f32[]{:T(128)} %fusion.108, f32[]{:T(128)} %get-tuple-element.8), channel_id=1, replica_groups=mesh['gx_0'=4,'gx_1'=2,'gy'=4,'gz_0'=2,'gz_1'=4] {'gx_0'}, use_global_device_ids=true, to_apply=%region_11.12 | all-reduce | flops 2 | bytes 16 | tf_op jit(solution)/shard_map/psum | solution.py:55
  205.5 3.1 %all-reduce.11 = (f32[]{:T(128)}, f32[]{:T(128)}) all-reduce(f32[]{:T(128)} %get-tuple-element.14, f32[]{:T(128)} %get-tuple-element.15), channel_id=1, replica_groups=mesh['gx_0'=4,'gx_1'=2,'gy'=4,'gz_0'=2,'gz_1'=4] {'gx_1'}, use_global_device_ids=true, to_apply=%region_12.13 | all-reduce | flops 2 | bytes 16 | tf_op jit(solution)/shard_map/psum | solution.py:55
  208.6 10.8 %all-reduce.8 = (f32[]{:T(128)}, f32[]{:T(128)}) all-reduce(f32[]{:T(128)} %get-tuple-element.18, f32[]{:T(128)} %get-tuple-element.19), channel_id=1, replica_groups=mesh['gx_0'=4,'gx_1'=2,'gy'=4,'gz_0'=2,'gz_1'=4] {'gy'}, use_global_device_ids=true, to_apply=%region_13.14 | all-reduce | flops 2 | bytes 16 | tf_op jit(solution)/shard_map/psum | solution.py:55
  219.4 5.6 %all-reduce.10 = (f32[]{:T(128)}, f32[]{:T(128)}) all-reduce(f32[]{:T(128)} %get-tuple-element.12, f32[]{:T(128)} %get-tuple-element.13), channel_id=1, replica_groups=mesh['gx_0'=4,'gx_1'=2,'gy'=4,'gz_0'=2,'gz_1'=4] {'gz_0'}, use_global_device_ids=true, to_apply=%region_14.15 | all-reduce | flops 2 | bytes 16 | tf_op jit(solution)/shard_map/psum | solution.py:55
  225.0 12.5 %all-reduce.7 = (f32[]{:T(128)}, f32[]{:T(128)}) all-reduce(f32[]{:T(128)} %get-tuple-element.16, f32[]{:T(128)} %get-tuple-element.17), channel_id=1, replica_groups=mesh['gx_0'=4,'gx_1'=2,'gy'=4,'gz_0'=2,'gz_1'=4] {'gz_1'}, use_global_device_ids=true, to_apply=%region_15.16 | all-reduce | flops 2 | bytes 16 | tf_op jit(solution)/shard_map/psum | solution.py:55
  (177 shorter events, 73.5 us)
Async XLA Ops:
  0.6 18.9 %copy-start.2 = (f32[3,16,16,128]{3,2,1,0:T(8,128)S(1)}, f32[3,16,16,128]{3,2,1,0:T(8,128)}, u32[]{:S(2)}) copy-start(f32[3,16,16,128]{3,2,1,0:T(8,128)} %param.2) | copy-start | bytes 1179652
  2.5 3.1 %collective-permute-start = (f32[4,2,16,128]{3,2,1,0:T(8,128)S(1)}, f32[4,2,16,128]{3,2,1,0:T(8,128)S(1)}, u32[]{:S(2)}, u32[]{:S(2)}) collective-permute-start(f32[4,2,16,128]{3,2,1,0:T(8,128)S(1)} %get-tuple-element.30), channel_id=1, source_target_pairs={{0,32},{32,64},{64,96},{96,128},{128,160},{160,192},{192,224},{1,3... | collective-permute-start | bytes 196616 | tf_op jit(solution)/shard_map/ppermute | solution.py:46
  4.2 6.2 %collective-permute-start.1 = (f32[4,2,16,128]{3,2,1,0:T(8,128)S(1)}, f32[4,2,16,128]{3,2,1,0:T(8,128)S(1)}, u32[]{:S(2)}, u32[]{:S(2)}) collective-permute-start(f32[4,2,16,128]{3,2,1,0:T(8,128)S(1)} %get-tuple-element.31), channel_id=1, source_target_pairs={{32,0},{64,32},{96,64},{128,96},{160,128},{192,160},{224,192},{33,... | collective-permute-start | bytes 196616 | tf_op jit(solution)/shard_map/ppermute | solution.py:49
  5.6 14.1 %copy-start.17 = (f32[4,2,16,128]{3,2,1,0:T(8,128)}, f32[4,2,16,128]{3,2,1,0:T(8,128)S(1)}, u32[]{:S(2)}) copy-start(f32[4,2,16,128]{3,2,1,0:T(8,128)S(1)} %collective-permute-done) | copy-start | bytes 196612
  10.4 9.3 %copy-start.18 = (f32[4,2,16,128]{3,2,1,0:T(8,128)}, f32[4,2,16,128]{3,2,1,0:T(8,128)S(1)}, u32[]{:S(2)}) copy-start(f32[4,2,16,128]{3,2,1,0:T(8,128)S(1)} %collective-permute-done.1) | copy-start | bytes 196612
  11.6 6.3 %collective-permute-start.3 = (f32[4,20,2,128]{3,0,2,1:T(4,128)S(1)}, f32[4,20,2,128]{3,0,2,1:T(4,128)S(1)}, u32[]{:S(2)}, u32[]{:S(2)}) collective-permute-start(f32[4,20,2,128]{3,0,2,1:T(4,128)S(1)} %copy.327), channel_id=1, source_target_pairs={{8,0},{16,8},{24,16},{9,1},{17,9},{25,17},{10,2},{18,10},{26,18},{... | collective-permute-start | bytes 245768 | tf_op jit(solution)/shard_map/ppermute | solution.py:49
  12.9 6.6 %collective-permute-start.2 = (f32[4,20,2,128]{3,0,2,1:T(4,128)S(1)}, f32[4,20,2,128]{3,0,2,1:T(4,128)S(1)}, u32[]{:S(2)}, u32[]{:S(2)}) collective-permute-start(f32[4,20,2,128]{3,0,2,1:T(4,128)S(1)} %copy.326), channel_id=1, source_target_pairs={{0,8},{8,16},{16,24},{1,9},{9,17},{17,25},{2,10},{10,18},{18,26},{... | collective-permute-start | bytes 245768 | tf_op jit(solution)/shard_map/ppermute | solution.py:46
  21.4 9.8 %collective-permute-start.5 = (f32[4,20,20,2]{2,0,3,1:T(4,128)S(1)}, f32[4,20,20,2]{2,0,3,1:T(4,128)S(1)}, u32[]{:S(2)}, u32[]{:S(2)}) collective-permute-start(f32[4,20,20,2]{2,0,3,1:T(4,128)S(1)} %copy.312), channel_id=1, source_target_pairs={{1,0},{2,1},{3,2},{4,3},{5,4},{6,5},{7,6},{9,8},{10,9},{11,10},{12... | collective-permute-start | bytes 38408 | tf_op jit(solution)/shard_map/ppermute | solution.py:49
  23.7 6.9 %collective-permute-start.4 = (f32[4,20,20,2]{2,0,3,1:T(4,128)S(1)}, f32[4,20,20,2]{2,0,3,1:T(4,128)S(1)}, u32[]{:S(2)}, u32[]{:S(2)}) collective-permute-start(f32[4,20,20,2]{2,0,3,1:T(4,128)S(1)} %copy.311), channel_id=1, source_target_pairs={{0,1},{1,2},{2,3},{3,4},{4,5},{5,6},{6,7},{8,9},{9,10},{10,11},{11... | collective-permute-start | bytes 38408 | tf_op jit(solution)/shard_map/ppermute | solution.py:46
  69.0 2.8 %collective-permute-start.7 = (f32[3,1,4,64]{3,2,0,1:T(4,128)S(1)}, f32[3,1,4,64]{3,2,0,1:T(4,128)S(1)}, u32[]{:S(2)}, u32[]{:S(2)}) collective-permute-start(f32[3,1,4,64]{3,2,0,1:T(4,128)S(1)} %multiply_divide_fusion.1), channel_id=1, source_target_pairs={{0,32},{32,64},{64,96},{96,128},{128,160},{160,192},{192,224},{1,3... | collective-permute-start | bytes 9224 | tf_op jit(solution)/shard_map/ppermute | solution.py:46
  70.4 7.6 %collective-permute-start.6 = (f32[3,1,4,64]{3,2,0,1:T(4,128)S(1)}, f32[3,1,4,64]{3,2,0,1:T(4,128)S(1)}, u32[]{:S(2)}, u32[]{:S(2)}) collective-permute-start(f32[3,1,4,64]{3,2,0,1:T(4,128)S(1)} %multiply_divide_fusion.1), channel_id=1, source_target_pairs={{32,0},{64,32},{96,64},{128,96},{160,128},{192,160},{224,192},{33,... | collective-permute-start | bytes 9224 | tf_op jit(solution)/shard_map/ppermute | solution.py:49
  78.4 6.6 %collective-permute-start.9 = (f32[3,1,4,64]{3,2,0,1:T(4,128)S(1)}, f32[3,1,4,64]{3,2,0,1:T(4,128)S(1)}, u32[]{:S(2)}, u32[]{:S(2)}) collective-permute-start(f32[3,1,4,64]{3,2,0,1:T(4,128)S(1)} %divide_add_fusion.5), channel_id=1, source_target_pairs={{0,32},{32,64},{64,96},{96,128},{128,160},{160,192},{192,224},{1,3... | collective-permute-start | bytes 9224 | tf_op jit(solution)/shard_map/ppermute | solution.py:46
  83.6 5.1 %collective-permute-start.8 = (f32[3,1,4,64]{3,2,0,1:T(4,128)S(1)}, f32[3,1,4,64]{3,2,0,1:T(4,128)S(1)}, u32[]{:S(2)}, u32[]{:S(2)}) collective-permute-start(f32[3,1,4,64]{3,2,0,1:T(4,128)S(1)} %divide_add_fusion.5), channel_id=1, source_target_pairs={{32,0},{64,32},{96,64},{128,96},{160,128},{192,160},{224,192},{33,... | collective-permute-start | bytes 9224 | tf_op jit(solution)/shard_map/ppermute | solution.py:49
  89.1 8.5 %collective-permute-start.11 = (f32[3,1,4,64]{3,2,0,1:T(4,128)S(1)}, f32[3,1,4,64]{3,2,0,1:T(4,128)S(1)}, u32[]{:S(2)}, u32[]{:S(2)}) collective-permute-start(f32[3,1,4,64]{3,2,0,1:T(4,128)S(1)} %divide_add_fusion.4), channel_id=1, source_target_pairs={{0,32},{32,64},{64,96},{96,128},{128,160},{160,192},{192,224},{1,3... | collective-permute-start | bytes 9224 | tf_op jit(solution)/shard_map/ppermute | solution.py:46
  96.1 3.2 %collective-permute-start.10 = (f32[3,1,4,64]{3,2,0,1:T(4,128)S(1)}, f32[3,1,4,64]{3,2,0,1:T(4,128)S(1)}, u32[]{:S(2)}, u32[]{:S(2)}) collective-permute-start(f32[3,1,4,64]{3,2,0,1:T(4,128)S(1)} %divide_add_fusion.4), channel_id=1, source_target_pairs={{32,0},{64,32},{96,64},{128,96},{160,128},{192,160},{224,192},{33,... | collective-permute-start | bytes 9224 | tf_op jit(solution)/shard_map/ppermute | solution.py:49
  99.8 7.3 %collective-permute-start.13 = (f32[3,1,4,64]{3,2,0,1:T(4,128)S(1)}, f32[3,1,4,64]{3,2,0,1:T(4,128)S(1)}, u32[]{:S(2)}, u32[]{:S(2)}) collective-permute-start(f32[3,1,4,64]{3,2,0,1:T(4,128)S(1)} %divide_add_fusion.3), channel_id=1, source_target_pairs={{0,32},{32,64},{64,96},{96,128},{128,160},{160,192},{192,224},{1,3... | collective-permute-start | bytes 9224 | tf_op jit(solution)/shard_map/ppermute | solution.py:46
  105.7 3.1 %collective-permute-start.12 = (f32[3,1,4,64]{3,2,0,1:T(4,128)S(1)}, f32[3,1,4,64]{3,2,0,1:T(4,128)S(1)}, u32[]{:S(2)}, u32[]{:S(2)}) collective-permute-start(f32[3,1,4,64]{3,2,0,1:T(4,128)S(1)} %divide_add_fusion.3), channel_id=1, source_target_pairs={{32,0},{64,32},{96,64},{128,96},{160,128},{192,160},{224,192},{33,... | collective-permute-start | bytes 9224 | tf_op jit(solution)/shard_map/ppermute | solution.py:49
  109.1 7.3 %collective-permute-start.15 = (f32[3,1,4,64]{3,2,0,1:T(4,128)S(1)}, f32[3,1,4,64]{3,2,0,1:T(4,128)S(1)}, u32[]{:S(2)}, u32[]{:S(2)}) collective-permute-start(f32[3,1,4,64]{3,2,0,1:T(4,128)S(1)} %divide_add_fusion.2), channel_id=1, source_target_pairs={{0,32},{32,64},{64,96},{96,128},{128,160},{160,192},{192,224},{1,3... | collective-permute-start | bytes 9224 | tf_op jit(solution)/shard_map/ppermute | solution.py:46
  115.1 3.1 %collective-permute-start.14 = (f32[3,1,4,64]{3,2,0,1:T(4,128)S(1)}, f32[3,1,4,64]{3,2,0,1:T(4,128)S(1)}, u32[]{:S(2)}, u32[]{:S(2)}) collective-permute-start(f32[3,1,4,64]{3,2,0,1:T(4,128)S(1)} %divide_add_fusion.2), channel_id=1, source_target_pairs={{32,0},{64,32},{96,64},{128,96},{160,128},{192,160},{224,192},{33,... | collective-permute-start | bytes 9224 | tf_op jit(solution)/shard_map/ppermute | solution.py:49
  118.5 7.3 %collective-permute-start.17 = (f32[3,1,4,64]{3,2,0,1:T(4,128)S(1)}, f32[3,1,4,64]{3,2,0,1:T(4,128)S(1)}, u32[]{:S(2)}, u32[]{:S(2)}) collective-permute-start(f32[3,1,4,64]{3,2,0,1:T(4,128)S(1)} %divide_add_fusion.1), channel_id=1, source_target_pairs={{0,32},{32,64},{64,96},{96,128},{128,160},{160,192},{192,224},{1,3... | collective-permute-start | bytes 9224 | tf_op jit(solution)/shard_map/ppermute | solution.py:46
  124.5 3.1 %collective-permute-start.16 = (f32[3,1,4,64]{3,2,0,1:T(4,128)S(1)}, f32[3,1,4,64]{3,2,0,1:T(4,128)S(1)}, u32[]{:S(2)}, u32[]{:S(2)}) collective-permute-start(f32[3,1,4,64]{3,2,0,1:T(4,128)S(1)} %divide_add_fusion.1), channel_id=1, source_target_pairs={{32,0},{64,32},{96,64},{128,96},{160,128},{192,160},{224,192},{33,... | collective-permute-start | bytes 9224 | tf_op jit(solution)/shard_map/ppermute | solution.py:49
  127.9 7.3 %collective-permute-start.19 = (f32[3,1,4,64]{3,2,0,1:T(4,128)S(1)}, f32[3,1,4,64]{3,2,0,1:T(4,128)S(1)}, u32[]{:S(2)}, u32[]{:S(2)}) collective-permute-start(f32[3,1,4,64]{3,2,0,1:T(4,128)S(1)} %divide_add_fusion), channel_id=1, source_target_pairs={{0,32},{32,64},{64,96},{96,128},{128,160},{160,192},{192,224},{1,3... | collective-permute-start | bytes 9224 | tf_op jit(solution)/shard_map/ppermute | solution.py:46
  133.9 3.1 %collective-permute-start.18 = (f32[3,1,4,64]{3,2,0,1:T(4,128)S(1)}, f32[3,1,4,64]{3,2,0,1:T(4,128)S(1)}, u32[]{:S(2)}, u32[]{:S(2)}) collective-permute-start(f32[3,1,4,64]{3,2,0,1:T(4,128)S(1)} %divide_add_fusion), channel_id=1, source_target_pairs={{32,0},{64,32},{96,64},{128,96},{160,128},{192,160},{224,192},{33,... | collective-permute-start | bytes 9224 | tf_op jit(solution)/shard_map/ppermute | solution.py:49
  137.7 17.4 %copy-start.4 = (f32[3,16,16,128]{3,2,1,0:T(8,128)}, f32[3,16,16,128]{3,2,1,0:T(8,128)S(1)}, u32[]{:S(2)}) copy-start(f32[3,16,16,128]{3,2,1,0:T(8,128)S(1)} %slice_add_fusion.52) | copy-start | bytes 1179652
  137.7 7.3 %collective-permute-start.20 = (f32[3,3,16,128]{3,2,1,0:T(8,128)S(1)}, f32[3,3,16,128]{3,2,1,0:T(8,128)S(1)}, u32[]{:S(2)}, u32[]{:S(2)}) collective-permute-start(f32[3,3,16,128]{3,2,1,0:T(8,128)S(1)} %get-tuple-element.34), channel_id=1, source_target_pairs={{0,32},{32,64},{64,96},{96,128},{128,160},{160,192},{192,224},{1,3... | collective-permute-start | bytes 221192 | tf_op jit(solution)/shard_map/ppermute | solution.py:46
  143.7 3.2 %collective-permute-start.21 = (f32[3,3,16,128]{3,2,1,0:T(8,128)S(1)}, f32[3,3,16,128]{3,2,1,0:T(8,128)S(1)}, u32[]{:S(2)}, u32[]{:S(2)}) collective-permute-start(f32[3,3,16,128]{3,2,1,0:T(8,128)S(1)} %get-tuple-element.35), channel_id=1, source_target_pairs={{32,0},{64,32},{96,64},{128,96},{160,128},{192,160},{224,192},{33,... | collective-permute-start | bytes 221192 | tf_op jit(solution)/shard_map/ppermute | solution.py:49
  146.8 8.3 %copy-start.16 = (f32[3,3,16,128]{3,2,1,0:T(8,128)}, f32[3,3,16,128]{3,2,1,0:T(8,128)S(1)}, u32[]{:S(2)}) copy-start(f32[3,3,16,128]{3,2,1,0:T(8,128)S(1)} %collective-permute-done.21) | copy-start | bytes 221188
  146.9 6.6 %collective-permute-start.23 = (f32[3,22,3,128]{3,1,2,0:T(8,128)S(1)}, f32[3,22,3,128]{3,1,2,0:T(8,128)S(1)}, u32[]{:S(2)}, u32[]{:S(2)}) collective-permute-start(f32[3,22,3,128]{3,1,2,0:T(8,128)S(1)} %copy.318), channel_id=1, source_target_pairs={{8,0},{16,8},{24,16},{9,1},{17,9},{25,17},{10,2},{18,10},{26,18},{... | collective-permute-start | bytes 304136 | tf_op jit(solution)/shard_map/ppermute | solution.py:49
  148.2 6.9 %collective-permute-start.22 = (f32[3,22,3,128]{3,1,2,0:T(8,128)S(1)}, f32[3,22,3,128]{3,1,2,0:T(8,128)S(1)}, u32[]{:S(2)}, u32[]{:S(2)}) collective-permute-start(f32[3,22,3,128]{3,1,2,0:T(8,128)S(1)} %copy.317), channel_id=1, source_target_pairs={{0,8},{8,16},{16,24},{1,9},{9,17},{17,25},{2,10},{10,18},{18,26},{... | collective-permute-start | bytes 304136 | tf_op jit(solution)/shard_map/ppermute | solution.py:46
  159.4 15.2 %copy-start.5 = (f32[3,16,16,128]{3,2,1,0:T(8,128)S(1)}, f32[3,16,16,128]{3,2,1,0:T(8,128)}, u32[]{:S(2)}) copy-start(f32[3,16,16,128]{3,2,1,0:T(8,128)} %copy-done.4) | copy-start | bytes 1179652
  160.6 11.8 %collective-permute-start.25 = (f32[3,22,22,3]{2,1,3,0:T(8,128)}, f32[3,22,22,3]{2,1,3,0:T(8,128)}, u32[]{:S(2)}, u32[]{:S(2)}) collective-permute-start(f32[3,22,22,3]{2,1,3,0:T(8,128)} %copy.322), channel_id=1, source_target_pairs={{1,0},{2,1},{3,2},{4,3},{5,4},{6,5},{7,6},{9,8},{10,9},{11,10},{12... | collective-permute-start | bytes 52280 | tf_op jit(solution)/shard_map/ppermute | solution.py:49
  164.0 7.0 %collective-permute-start.24 = (f32[3,22,22,3]{2,1,3,0:T(8,128)}, f32[3,22,22,3]{2,1,3,0:T(8,128)}, u32[]{:S(2)}, u32[]{:S(2)}) collective-permute-start(f32[3,22,22,3]{2,1,3,0:T(8,128)} %copy.321), channel_id=1, source_target_pairs={{0,1},{1,2},{2,3},{3,4},{4,5},{5,6},{6,7},{8,9},{9,10},{10,11},{11... | collective-permute-start | bytes 52280 | tf_op jit(solution)/shard_map/ppermute | solution.py:46
  (13 other events, 17.3 us)
where the time goes:
time: 241 us; the launch traced here: 240 us
  starting transfers between devices  80.3 us (33%)
  blocking collectives  63.2 us (26%)
  other arithmetic  39.5 us (16%)
  waiting for transfers between devices  35.5 us (15%)
  local copies, waits for them, and re-layouts  18 us (7%)
  between operations  2.98 us (1%)
    ppermute x13, starting transfers between devices, padded_2(): lax.ppermute(lax.slice_in_dim(block, block.shape[dim] - width, None, axis...  60.2 us
    psum x5, blocking collectives, by_axis(): return functools.reduce(lax.psum, axes, value)  46.5 us
    ppermute x13, waiting for transfers between devices, padded_2(): lax.ppermute(lax.slice_in_dim(block, 0, width, axis=dim), axis, backward)  26.5 us
    ppermute x13, starting transfers between devices, padded_2(): lax.ppermute(lax.slice_in_dim(block, 0, width, axis=dim), axis, backward)  20.1 us
    all_to_all x1, blocking collectives, from_everyone(): lax.all_to_all(jnp.broadcast_to(value[None], (length, *value.shape)), axi...  16.7 us
    another operation x11, other arithmetic, stencil(): return jnp.stack(images)  12 us
    ppermute x13, waiting for transfers between devices, padded_2(): lax.ppermute(lax.slice_in_dim(block, block.shape[dim] - width, None, axis...  9.07 us
    add x24, other arithmetic, stencil(): coefficient * (6.0 * centre - beside_all + COUPLING * (axial_part - 0.25...  6.31 us
  transfers between devices with their start and end apart: 26, of which 15 were waited for; matrix products, arithmetic and copies ran while one was open for 2% of the time, Pallas kernels for 0%

commit v1 on v0

v1 whole, which is shorter than its diff:
```python
import functools

import jax
import jax.numpy as jnp
from jax import lax
from jax.experimental import pallas as pl
from jax.experimental.pallas import tpu as pltpu
from jax.sharding import Mesh
from jax.sharding import PartitionSpec as P

BLOCK = 16
COARSE = 8
GX = ("gx_0", "gx_1")
GZ = ("gz_0", "gz_1")
ALL = ("gx_0", "gx_1", "gy", "gz_0", "gz_1")

FLOOR_STIFFNESS = 0.05
MASS_TERM = 0.001
COUPLING = 2.5
RELAXATION = 0.6

W = 4
NP = 16 + 2 * W
ROWS = 32
Y0 = 8
DIAG = 6.0 + 2.0 * COUPLING
OWN = 1.0 + COUPLING
MIX = 0.25 * COUPLING
KEEP = 1.0 - RELAXATION


def lanes_of(shape):
    return lax.broadcasted_iota(jnp.int32, shape, 1)


def rows_of(shape):
    return lax.broadcasted_iota(jnp.int32, shape, 0)


def stiffness_of(damage):
    level = damage.astype(jnp.float32) / 15.0
    return (1.0 - level) ** 2 * (1.0 - FLOOR_STIFFNESS) + FLOOR_STIFFNESS


def z_up(main, tail, lane):
    a = pltpu.roll(main, 127, 1)
    b = pltpu.roll(tail, 127, 1)
    last = lane == 127
    return jnp.where(last, b, a), jnp.where(last, a, b)


def z_down(main, tail, lane):
    a = pltpu.roll(main, 1, 1)
    b = pltpu.roll(tail, 1, 1)
    first = lane == 0
    return jnp.where(first, b, a), jnp.where(first, a, b)


def neighbour_sum(ref, i, row, lane, both):
    def at(c, dx, dy, t):
        return ref[c, i + dx, t, pl.ds(row + dy, 8), :]

    ups, downs, rests, centres = [], [], [], []
    for t in range(2):
        v = [at(c, 0, 0, t) for c in range(3)]
        xp = [at(c, 1, 0, t) for c in range(3)]
        xm = [at(c, -1, 0, t) for c in range(3)]
        yp = [at(c, 0, 1, t) for c in range(3)]
        ym = [at(c, 0, -1, t) for c in range(3)]
        zx = MIX * (xp[2] - xm[2])
        zy = MIX * (yp[2] - ym[2])
        zz = MIX * ((xp[0] - xm[0]) + (yp[1] - ym[1]))
        own = OWN * v[2]
        ups.append((v[0] + zx, v[1] + zy, own + zz))
        downs.append((v[0] - zx, v[1] - zy, own - zz))
        centres.append(v)
        if t == 0 or both:
            mix_x = (at(1, 1, 1, t) - at(1, 1, -1, t)) - (at(1, -1, 1, t) - at(1, -1, -1, t))
            mix_y = (at(0, 1, 1, t) - at(0, 1, -1, t)) - (at(0, -1, 1, t) - at(0, -1, -1, t))
            rests.append(
                (
                    OWN * (xp[0] + xm[0]) + (yp[0] + ym[0]) + MIX * mix_x,
                    OWN * (yp[1] + ym[1]) + (xp[1] + xm[1]) + MIX * mix_y,
                    (xp[2] + xm[2]) + (yp[2] + ym[2]),
                )
            )
    sums = [[], []]
    for c in range(3):
        up = z_up(ups[0][c], ups[1][c], lane)
        down = z_down(downs[0][c], downs[1][c], lane)
        for t in range(2 if both else 1):
            sums[t].append(rests[t][c] + (up[t] + down[t]))
    return sums, centres


def sweep(source, target, p_ref, q_ref, first, last):
    lane = lanes_of((8, 128))

    def plane(i, carry):
        for row in (4, 12, 20):
            sums, centres = neighbour_sum(source, i, row, lane, True)
            for t in range(2):
                q = q_ref[i, t, pl.ds(row, 8), :]
                for c in range(3):
                    p = p_ref[c, i, t, pl.ds(row, 8), :]
                    target[c, i, t, pl.ds(row, 8), :] = KEEP * centres[t][c] + p + q * sums[t][c]
        return carry

    lax.fori_loop(first, last, plane, 0)


def first_kernel(at_ref, wide, zlo, zhi, x2, p_ref, q_ref, sums_out):
    lane24 = lanes_of((NP, 128))
    row24 = rows_of((NP, 128))
    lane = lanes_of((8, 128))
    gx, gy, gz = at_ref[0], at_ref[1], at_ref[2]
    y = gy * 16 + row24 - W
    y_in = (y >= 0) & (y < at_ref[4])
    tail_in = ((lane24 < W) & (gz < at_ref[5] - 1)) | ((lane24 >= 128 - W) & (gz > 0))

    def prepare(i, carry):
        x = gx * 16 + i - W
        x_in = (x >= 0) & (x < at_ref[3])
        for t in range(2):
            if t == 0:
                parts = [wide[c, i] for c in range(4)]
                inside = y_in & x_in
            else:
                parts = [
                    jnp.where(
                        lane24 < W,
                        pltpu.roll(zhi[c], (128 - W * i) % 128, 1),
                        pltpu.roll(zlo[c], 128 - W - W * i, 1),
                    )
                    for c in range(4)
                ]
                inside = y_in & x_in & tail_in
            g = stiffness_of(parts[3])
            scale = RELAXATION / (g * DIAG + MASS_TERM)
            for c in range(3):
                value = parts[c] * scale
                if t == 1:
                    value = jnp.where(tail_in, value, 0.0)
                p_ref[c, i, t, pl.ds(4, NP), :] = value
            q_ref[i, t, pl.ds(4, NP), :] = jnp.where(inside, g * scale, 0.0)
        return carry

    lax.fori_loop(0, NP, prepare, 0)
    sweep(p_ref, x2, p_ref, q_ref, 1, NP - 1)

    def residual(i, carry):
        totals = list(carry)
        for row in (8, 16):
            sums, centres = neighbour_sum(x2, i, row, lane, False)
            g = stiffness_of(wide[3, i, pl.ds(row - 4, 8), :])
            d = g * DIAG + MASS_TERM
            for c in range(3):
                f = wide[c, i, pl.ds(row - 4, 8), :]
                totals[c] += (f - d * centres[0][c]) + g * sums[0][c]
                totals[4] += f * f
            totals[3] += g
        return tuple(totals)

    zero = jnp.zeros((8, 128), jnp.float32)
    totals = lax.fori_loop(W, W + 16, residual, (zero,) * 5)
    row = rows_of((8, 128))
    stacked = zero
    for c in range(5):
        stacked = jnp.where(row == c, jnp.sum(totals[c], axis=0, keepdims=True), stacked)
    big = (128, 128)
    gather = (rows_of(big) // BLOCK == lanes_of(big) % 8).astype(jnp.float32)
    by_cell = jnp.dot(
        stacked, gather, precision=lax.Precision.HIGHEST, preferred_element_type=jnp.float32
    )
    slot = jnp.sum(jnp.where(lane // 8 == row, by_cell, 0.0), axis=0, keepdims=True)
    sums_out[...] = jnp.broadcast_to(slot, sums_out.shape)


def coarse_solve(load, mean, gx_n, gy_n, gz_n):
    shape = load[0].shape
    n = shape[1]
    lane = lanes_of(shape)
    row = rows_of(shape)
    sx, sy = gy_n * gz_n, gz_n
    x_at, y_at, z_at = lane // sx, lane // sy % gy_n, lane % gz_n

    def shift(v, step, at, count):
        up = jnp.where(at < count - 1, pltpu.roll(v, n - step, 1), 0.0)
        down = jnp.where(at > 0, pltpu.roll(v, step, 1), 0.0)
        return up, down

    def shift_z(v):
        up = pltpu.roll(v, 7, 0)
        down = pltpu.roll(v, 1, 0)
        next_up = jnp.where(z_at < gz_n - 1, pltpu.roll(up, n - 1, 1), 0.0)
        next_down = jnp.where(z_at > 0, pltpu.roll(down, 1, 1), 0.0)
        return jnp.where(row == 7, next_up, up), jnp.where(row == 0, next_down, down)

    shifts = (
        lambda v: shift(v, sx, x_at, gx_n),
        lambda v: shift(v, sy, y_at, gy_n),
        shift_z,
    )
    coefficient = BLOCK**2 * mean
    scale = RELAXATION / (coefficient * DIAG + BLOCK**3 * MASS_TERM)
    p = [scale * value for value in load]
    q = scale * coefficient

    def step(_, w):
        pairs = [[shifts[b](w[a]) for b in range(3)] for a in range(3)]
        diffs = [pairs[a][a][0] - pairs[a][a][1] for a in range(3)]
        out = []
        for a in range(3):
            total = 0.0
            for b in range(3):
                both = pairs[a][b][0] + pairs[a][b][1]
                total = total + (OWN * both if a == b else both)
            others = [diffs[b] for b in range(3) if b != a]
            up, down = shifts[a](others[0] + others[1])
            out.append(KEEP * w[a] + p[a] + q * (total + MIX * (up - down)))
        return tuple(out)

    return lax.fori_loop(0, COARSE - 1, step, tuple(p))


def second_kernel(
    counts, at_ref, every, x2, p_ref, q_ref, damage, out, sum_out, load_out, x3, x4, w_ref
):
    gx_n, gy_n, gz_n = counts
    lane = lanes_of((8, 128))
    row8 = rows_of((8, 128))
    cells = jnp.transpose(every[...])
    load = [cells[8 * c : 8 * c + 8] for c in range(3)]
    mean = cells[24:32] * (1.0 / BLOCK**3)
    load_out[...] = jnp.broadcast_to(jnp.sum(cells[32:40]), load_out.shape)
    w = coarse_solve(load, mean, gx_n, gy_n, gz_n)
    n = gx_n * gy_n * gz_n
    me = at_ref[6]
    centre = n // 2
    pick = (lane // BLOCK == row8).astype(jnp.float32)
    for c in range(3):
        turned = pltpu.roll(w[c], (centre + n - me) % n, 1)
        for dx in range(3):
            for dy in range(3):
                j = centre + (dx - 1) * gy_n * gz_n + (dy - 1) * gz_n
                main = jnp.sum(turned[:, j : j + 1] * pick, axis=0, keepdims=True)
                high = jnp.broadcast_to(turned[0:1, j + 1 : j + 2], (1, 128))
                low = jnp.broadcast_to(turned[7:8, j - 1 : j], (1, 128))
                tail = jnp.where(lane[:1] < W, high, low)
                first, size = ((4, 4), (8, 16), (24, 4))[dy]
                w_ref[c, dx, 0, pl.ds(first, size), :] = jnp.broadcast_to(main, (size, 128))
                w_ref[c, dx, 1, pl.ds(first, size), :] = jnp.broadcast_to(tail, (size, 128))

    def correct(i, carry):
        cell = (i >= W).astype(jnp.int32) + (i >= W + 16).astype(jnp.int32)
        for t in range(2):
            inside = q_ref[i, t, pl.ds(4, NP), :] > 0.0
            for c in range(3):
                value = w_ref[c, cell, t, pl.ds(4, NP), :]
                x3[c, i, t, pl.ds(4, NP), :] = x2[c, i, t, pl.ds(4, NP), :] + jnp.where(
                    inside, value, 0.0
                )
        return carry

    lax.fori_loop(1, NP - 1, correct, 0)
    sweep(x3, x4, p_ref, q_ref, 2, NP - 2)
    sweep(x4, x3, p_ref, q_ref, 3, NP - 3)

    def residual(i, total):
        for row in (8, 16):
            sums, centres = neighbour_sum(x3, i, row, lane, False)
            g = stiffness_of(damage[i - W, pl.ds(row - 8, 8), :])
            d = (g * DIAG + MASS_TERM) * (1.0 / RELAXATION)
            q = q_ref[i, 0, pl.ds(row, 8), :]
            for c in range(3):
                p = p_ref[c, i, 0, pl.ds(row, 8), :]
                out[c, i - W, pl.ds(row - 8, 8), :] = centres[0][c]
                r = d * ((p - RELAXATION * centres[0][c]) + q * sums[0][c])
                total += r * r
        return total

    total = lax.fori_loop(W, W + 16, residual, jnp.zeros((8, 128), jnp.float32))
    sum_out[...] = jnp.broadcast_to(jnp.sum(total), sum_out.shape)


def pack_kernel(wide, low_out, high_out):
    lane = lanes_of((NP, 128))
    for c in range(4):
        low = jnp.zeros((NP, 128), jnp.float32)
        high = low
        for i in range(NP):
            value = wide[c, i]
            here = (lane >= W * i) & (lane < W * i + W)
            low = jnp.where(here, pltpu.roll(value, W * i, 1), low)
            high = jnp.where(here, pltpu.roll(value, (W * i + W) % 128, 1), high)
        low_out[c] = low
        high_out[c] = high


def beside(block, axis, dim):
    count = lax.axis_size(axis)
    forward = [(i, i + 1) for i in range(count - 1)]
    backward = [(i + 1, i) for i in range(count - 1)]
    low = lax.ppermute(
        lax.slice_in_dim(block, block.shape[dim] - W, None, axis=dim), axis, forward
    )
    high = lax.ppermute(lax.slice_in_dim(block, 0, W, axis=dim), axis, backward)
    return jnp.concatenate([low, block, high], axis=dim)


VMEM = pl.BlockSpec(memory_space=pltpu.VMEM)
SMEM = pl.BlockSpec(memory_space=pltpu.SMEM)
F32 = jnp.float32


def on_device(right_side, damage):
    gx_n, gy_n, gz_n = lax.axis_size(GX), lax.axis_size("gy"), lax.axis_size(GZ)
    n = gx_n * gy_n * gz_n
    gx, gy, gz = lax.axis_index(GX), lax.axis_index("gy"), lax.axis_index(GZ)
    at = jnp.stack(
        [
            gx,
            gy,
            gz,
            jnp.int32(gx_n * 16),
            jnp.int32(gy_n * 16),
            jnp.int32(gz_n),
            (gx * gy_n + gy) * gz_n + gz,
        ]
    ).astype(jnp.int32)
    stacked = jnp.concatenate([right_side, damage.astype(F32)[None]], axis=0)
    wide = beside(beside(stacked, GX, 1), "gy", 2)
    side = jax.ShapeDtypeStruct((4, NP, 128), F32)
    low, high = pl.pallas_call(
        pack_kernel, out_shape=(side, side), in_specs=[VMEM], out_specs=(VMEM, VMEM)
    )(wide)
    zlo = lax.ppermute(high, GZ, [(i, i + 1) for i in range(gz_n - 1)])
    zhi = lax.ppermute(low, GZ, [(i + 1, i) for i in range(gz_n - 1)])
    field = (3, NP, 2, ROWS, 128)
    x2, p, q, sums = pl.pallas_call(
        first_kernel,
        out_shape=(
            jax.ShapeDtypeStruct(field, F32),
            jax.ShapeDtypeStruct(field, F32),
            jax.ShapeDtypeStruct(field[1:], F32),
            jax.ShapeDtypeStruct((n, 128), F32),
        ),
        in_specs=[SMEM, VMEM, VMEM, VMEM],
        out_specs=(VMEM,) * 4,
    )(at, wide, zlo, zhi)
    every = lax.all_to_all(sums, ALL, 0, 0, tiled=True)
    displacement, residual_sums, load_sum = pl.pallas_call(
        functools.partial(second_kernel, (gx_n, gy_n, gz_n)),
        out_shape=(
            jax.ShapeDtypeStruct(right_side.shape, F32),
            jax.ShapeDtypeStruct((n, 128), F32),
            jax.ShapeDtypeStruct((1, 128), F32),
        ),
        in_specs=[SMEM] + [VMEM] * 5,
        out_specs=(VMEM,) * 3,
        scratch_shapes=[
            pltpu.VMEM(field, F32),
            pltpu.VMEM(field, F32),
            pltpu.VMEM((3, 3, 2, ROWS, 128), F32),
        ],
    )(at, every, x2, p, q, damage)
    residual_sum = jnp.sum(lax.all_to_all(residual_sums[:, :1], ALL, 0, 0, tiled=True))
    total_count = right_side.size * n
    norms = jnp.sqrt(jnp.stack([load_sum[0, 0], residual_sum]) / total_count)
    return (displacement, norms)


def solution(mesh):
    torus = Mesh(mesh.devices.reshape(4, 2, mesh.shape["gy"], 2, 4), ALL)
    placed = (P(None, GX, "gy", GZ), P(GX, "gy", GZ))
    return jax.shard_map(
        on_device,
        mesh=torus,
        in_specs=placed,
        out_specs=(P(None, GX, "gy", GZ), P()),
        check_vma=False,
    )
```

time: 241 us -> 113 us (0.47)
  the two profiles are of different devices: /device:TPU:40 before, /device:TPU:1 now
where the time goes in v1:
time: 113 us
  blocking collectives  50 us (44%)
  Pallas kernels  24.4 us (22%)
  starting transfers between devices  17.1 us (15%)
  waiting for transfers between devices  13.5 us (12%)
  other arithmetic  5.95 us (5%)
  local copies, waits for them, and re-layouts  1.25 us (1%)
    all_to_all x1, blocking collectives, on_device(): every = lax.all_to_all(sums, ALL, 0, 0, tiled=True)  31.3 us
    all_to_all x1, blocking collectives, on_device(): lax.all_to_all(residual_sums[:, :1], ALL, 0, 0, tiled=True)  18.7 us
    pallas_call x1, Pallas kernels, on_device(): pl.pallas_call(functools.partial(second_kernel, (gx_n, gy_n, gz_n)), out_...  11.6 us
    pallas_call x1, Pallas kernels, on_device(): pl.pallas_call(first_kernel, out_shape=(jax.ShapeDtypeStruct(field, F32),...  10.3 us
    ppermute x2, starting transfers between devices, beside(): lax.ppermute(lax.slice_in_dim(block, block.shape[dim] - W, None, axis=dim...  9.4 us
    ppermute x2, waiting for transfers between devices, beside(): high = lax.ppermute(lax.slice_in_dim(block, 0, W, axis=dim), axis, backward)  9.09 us
    ppermute x2, starting transfers between devices, beside(): high = lax.ppermute(lax.slice_in_dim(block, 0, W, axis=dim), axis, backward)  3.21 us
    ppermute x1, starting transfers between devices, on_device(): zlo = lax.ppermute(high, GZ, [(i, i + 1) for i in range(gz_n - 1)])  3.19 us
  transfers between devices with their start and end apart: 6, of which 4 were waited for; matrix products, arithmetic and copies ran while one was open for 1% of the time, Pallas kernels for 0%

profile of v1, /device:TPU:1, one launch (start us, length us, event | category | flops | bytes accessed | tf_op | source)
XLA Modules:
  0.0 112.9 jit_solution(2135941310062182743)
XLA Ops:
  0.6 0.0 copy-start
  0.6 1.0 convert_bitcast_fusion
  1.6 1.0 pad_maximum_fusion.6
  2.6 6.3 %collective-permute-start = (f32[4,4,16,128]{3,2,1,0:T(8,128)S(1)}, f32[4,4,16,128]{3,2,1,0:T(8,128)S(1)}, u32[]{:S(2)}, u32[]{:S(2)}) collective-permute-start(f32[4,4,16,128]{3,2,1,0:T(8,128)S(1)} %get-tuple-element.22), channel_id=1, source_target_pairs={{0,32},{32,64},{64,96},{96,128},{128,160},{160,192},{192,224},{1,3... | collective-permute-start | bytes 393224 | tf_op jit(solution)/shard_map/ppermute | solution.py:304
  8.9 1.9 %collective-permute-start.1 = (f32[4,4,16,128]{3,2,1,0:T(8,128)S(1)}, f32[4,4,16,128]{3,2,1,0:T(8,128)S(1)}, u32[]{:S(2)}, u32[]{:S(2)}) collective-permute-start(f32[4,4,16,128]{3,2,1,0:T(8,128)S(1)} %get-tuple-element.23), channel_id=1, source_target_pairs={{32,0},{64,32},{96,64},{128,96},{160,128},{192,160},{224,192},{33,... | collective-permute-start | bytes 393224 | tf_op jit(solution)/shard_map/ppermute | solution.py:307
  10.8 0.0 collective-permute-done
  10.8 5.3 %collective-permute-done.1 = f32[4,4,16,128]{3,2,1,0:T(8,128)S(1)} collective-permute-done((f32[4,4,16,128]{3,2,1,0:T(8,128)S(1)}, f32[4,4,16,128]{3,2,1,0:T(8,128)S(1)}, u32[]{:S(2)}, u32[]{:S(2)}) %collective-permute-start.1) | collective-permute-done | bytes 131104 | tf_op jit(solution)/shard_map/ppermute | solution.py:307
  16.1 0.0 copy-done
  16.1 0.1 pad_maximum_fusion.4
  16.1 3.1 %collective-permute-start.2 = (f32[4,24,4,128]{3,2,1,0:T(4,128)S(1)}, f32[4,24,4,128]{3,2,1,0:T(4,128)S(1)}, u32[]{:S(2)}, u32[]{:S(2)}) collective-permute-start(f32[4,24,4,128]{3,2,1,0:T(4,128)S(1)} %get-tuple-element.20), channel_id=1, source_target_pairs={{0,8},{8,16},{16,24},{1,9},{9,17},{17,25},{2,10},{10,18},{18,26},{... | collective-permute-start | bytes 589832 | tf_op jit(solution)/shard_map/ppermute | solution.py:304
  19.3 1.3 %collective-permute-start.3 = (f32[4,24,4,128]{3,2,1,0:T(4,128)S(1)}, f32[4,24,4,128]{3,2,1,0:T(4,128)S(1)}, u32[]{:S(2)}, u32[]{:S(2)}) collective-permute-start(f32[4,24,4,128]{3,2,1,0:T(4,128)S(1)} %get-tuple-element.21), channel_id=1, source_target_pairs={{8,0},{16,8},{24,16},{9,1},{17,9},{25,17},{10,2},{18,10},{26,18},{... | collective-permute-start | bytes 589832 | tf_op jit(solution)/shard_map/ppermute | solution.py:307
  20.6 1.3 %collective-permute-done.2 = f32[4,24,4,128]{3,2,1,0:T(4,128)S(1)} collective-permute-done((f32[4,24,4,128]{3,2,1,0:T(4,128)S(1)}, f32[4,24,4,128]{3,2,1,0:T(4,128)S(1)}, u32[]{:S(2)}, u32[]{:S(2)}) %collective-permute-start.2) | collective-permute-done | bytes 196640 | tf_op jit(solution)/shard_map/ppermute | solution.py:304
  21.9 3.8 %collective-permute-done.3 = f32[4,24,4,128]{3,2,1,0:T(4,128)S(1)} collective-permute-done((f32[4,24,4,128]{3,2,1,0:T(4,128)S(1)}, f32[4,24,4,128]{3,2,1,0:T(4,128)S(1)}, u32[]{:S(2)}, u32[]{:S(2)}) %collective-permute-start.3) | collective-permute-done | bytes 196640 | tf_op jit(solution)/shard_map/ppermute | solution.py:307
  25.7 1.2 %pad_maximum_fusion.wide = f32[4,24,24,128]{3,2,1,0:T(8,128)} fusion(f32[4,24,4,128]{3,2,1,0:T(4,128)S(1)} %collective-permute-done.3, f32[4,4,16,128]{3,2,1,0:T(8,128)S(1)} %collective-permute-done.1, f32[1,16,16,128]{3,2,1,0:T(8,128)S(1)} %convert_bitcast_fusion, f32[3,16,16,128]{3,2,1,0:T(8,128)S(1)} %copy-done, ...), kind=kLoop, calls=%fused_computation | loop fusion | flops 1474560 | bytes 2359296 | tf_op jit(solution)/shard_map/concatenate | solution.py:308
  26.9 2.6 %shard_map.41 = (f32[4,24,128]{2,1,0:T(8,128)}, f32[4,24,128]{2,1,0:T(8,128)}) custom-call(f32[4,24,24,128]{3,2,1,0:T(8,128)} %pad_maximum_fusion.wide), custom_call_target="tpu_custom_call" | custom-call | tf_op jit(solution)/shard_map/pallas_call | solution.py:334
  29.5 3.2 %collective-permute-start.4 = (f32[4,24,128]{2,1,0:T(8,128)}, f32[4,24,128]{2,1,0:T(8,128)S(1)}, u32[]{:S(2)}, u32[]{:S(2)}) collective-permute-start(f32[4,24,128]{2,1,0:T(8,128)} %get-tuple-element.11), channel_id=1, source_target_pairs={{0,1},{1,2},{2,3},{3,4},{4,5},{5,6},{6,7},{8,9},{9,10},{10,11},{11... | collective-permute-start | bytes 147464 | tf_op jit(solution)/shard_map/ppermute | solution.py:337
  32.7 1.3 %collective-permute-start.5 = (f32[4,24,128]{2,1,0:T(8,128)}, f32[4,24,128]{2,1,0:T(8,128)S(1)}, u32[]{:S(2)}, u32[]{:S(2)}) collective-permute-start(f32[4,24,128]{2,1,0:T(8,128)} %get-tuple-element.12), channel_id=1, source_target_pairs={{1,0},{2,1},{3,2},{4,3},{5,4},{6,5},{7,6},{9,8},{10,9},{11,10},{12... | collective-permute-start | bytes 147464 | tf_op jit(solution)/shard_map/ppermute | solution.py:338
  34.0 0.6 stack.25.at_ref
  34.6 0.0 collective-permute-done.4.zlo
  34.6 0.0 copy-start.1
  34.6 3.1 %collective-permute-done.5.zhi = f32[4,24,128]{2,1,0:T(8,128)S(1)} collective-permute-done((f32[4,24,128]{2,1,0:T(8,128)}, f32[4,24,128]{2,1,0:T(8,128)S(1)}, u32[]{:S(2)}, u32[]{:S(2)}) %collective-permute-start.5) | collective-permute-done | bytes 49184 | tf_op jit(solution)/shard_map/ppermute | solution.py:338
  37.7 0.0 copy-done.1
  37.7 0.0 copy-start.2
  37.7 0.6 copy-done.2
  38.4 10.3 %shard_map.42 = (f32[3,24,2,32,128]{4,3,2,1,0:T(8,128)}, f32[3,24,2,32,128]{4,3,2,1,0:T(8,128)}, f32[24,2,32,128]{3,2,1,0:T(8,128)}, f32[256,128]{1,0:T(8,128)}) custom-call(s32[7]{0:T(128)} %stack.25.at_ref, f32[4,24,24,128]{3,2,1,0:T(8,128)} %pad_maximum_fusion.wide, f32[4,24,128]{2,1,0:T(8,128)} %copy-done.1, f32[4,24,128]{2,1,0:T(8,128)} %copy-done.2), custom_call_target="tpu_custom_call" | custom-call | tf_op jit(solution)/shard_map/pallas_call | solution.py:340
  48.6 31.3 %all_to_all.20 = f32[256,1,128]{2,1,0:T(1,128)} all-to-all(f32[256,1,128]{2,1,0:T(1,128)} %bitcast.17), channel_id=1, replica_groups=mesh['gx_0'=4,'gx_1'=2,'gy'=4,'gz_0'=2,'gz_1'=4] {'gx_0','gx_1','gy','gz..., dimensions={0} | all-to-all | bytes 262144 | tf_op jit(solution)/shard_map/all_to_all | solution.py:351
  80.0 11.6 %shard_map.43 = (f32[3,16,16,128]{3,2,1,0:T(8,128)}, f32[256,128]{1,0:T(8,128)}, f32[1,128]{1,0:T(1,128)}) custom-call(s32[7]{0:T(128)} %stack.25.at_ref, f32[256,128]{1,0:T(8,128)} %bitcast.15, f32[3,24,2,32,128]{4,3,2,1,0:T(8,128)} %get-tuple-element.14.x2, f32[3,24,2,32,128]{4,3,2,1,0:T(8,128)} %get-tuple-element.15.p_ref, ...), custom_call_target="tpu_custom_call" | custom-call | tf_op jit(solution)/shard_map/pallas_call | solution.py:352
  91.5 18.7 %all_to_all.21 = f32[256,1,1]{2,1,0:T(1,128)S(1)} all-to-all(f32[256,1,1]{2,1,0:T(1,128)} %bitcast.16), channel_id=1, replica_groups=mesh['gx_0'=4,'gx_1'=2,'gy'=4,'gz_0'=2,'gz_1'=4] {'gx_0','gx_1','gy','gz..., dimensions={0} | all-to-all | bytes 2048 | tf_op jit(solution)/shard_map/all_to_all | solution.py:367
  110.2 0.9 reduce_sum.9
  111.2 1.8 %fusion = f32[2]{0:T(128)} fusion(f32[1]{0:T(128)} %bitcast.10, f32[1]{0:T(128)} %bitcast.18), kind=kLoop, calls=%fused_computation.9 | loop fusion | flops 4 | bytes 16 | tf_op jit(solution)/shard_map/sqrt | solution.py:369
Async XLA Ops:
  0.6 15.4 %copy-start = (f32[3,16,16,128]{3,2,1,0:T(8,128)S(1)}, f32[3,16,16,128]{3,2,1,0:T(8,128)}, u32[]{:S(2)}) copy-start(f32[3,16,16,128]{3,2,1,0:T(8,128)} %param.2) | copy-start | bytes 1179652
  2.6 8.2 %collective-permute-start = (f32[4,4,16,128]{3,2,1,0:T(8,128)S(1)}, f32[4,4,16,128]{3,2,1,0:T(8,128)S(1)}, u32[]{:S(2)}, u32[]{:S(2)}) collective-permute-start(f32[4,4,16,128]{3,2,1,0:T(8,128)S(1)} %get-tuple-element.22), channel_id=1, source_target_pairs={{0,32},{32,64},{64,96},{96,128},{128,160},{160,192},{192,224},{1,3... | collective-permute-start | bytes 393224 | tf_op jit(solution)/shard_map/ppermute | solution.py:304
  8.9 7.2 %collective-permute-start.1 = (f32[4,4,16,128]{3,2,1,0:T(8,128)S(1)}, f32[4,4,16,128]{3,2,1,0:T(8,128)S(1)}, u32[]{:S(2)}, u32[]{:S(2)}) collective-permute-start(f32[4,4,16,128]{3,2,1,0:T(8,128)S(1)} %get-tuple-element.23), channel_id=1, source_target_pairs={{32,0},{64,32},{96,64},{128,96},{160,128},{192,160},{224,192},{33,... | collective-permute-start | bytes 393224 | tf_op jit(solution)/shard_map/ppermute | solution.py:307
  16.1 5.7 %collective-permute-start.2 = (f32[4,24,4,128]{3,2,1,0:T(4,128)S(1)}, f32[4,24,4,128]{3,2,1,0:T(4,128)S(1)}, u32[]{:S(2)}, u32[]{:S(2)}) collective-permute-start(f32[4,24,4,128]{3,2,1,0:T(4,128)S(1)} %get-tuple-element.20), channel_id=1, source_target_pairs={{0,8},{8,16},{16,24},{1,9},{9,17},{17,25},{2,10},{10,18},{18,26},{... | collective-permute-start | bytes 589832 | tf_op jit(solution)/shard_map/ppermute | solution.py:304
  19.3 6.4 %collective-permute-start.3 = (f32[4,24,4,128]{3,2,1,0:T(4,128)S(1)}, f32[4,24,4,128]{3,2,1,0:T(4,128)S(1)}, u32[]{:S(2)}, u32[]{:S(2)}) collective-permute-start(f32[4,24,4,128]{3,2,1,0:T(4,128)S(1)} %get-tuple-element.21), channel_id=1, source_target_pairs={{8,0},{16,8},{24,16},{9,1},{17,9},{25,17},{10,2},{18,10},{26,18},{... | collective-permute-start | bytes 589832 | tf_op jit(solution)/shard_map/ppermute | solution.py:307
  29.5 5.1 %collective-permute-start.4 = (f32[4,24,128]{2,1,0:T(8,128)}, f32[4,24,128]{2,1,0:T(8,128)S(1)}, u32[]{:S(2)}, u32[]{:S(2)}) collective-permute-start(f32[4,24,128]{2,1,0:T(8,128)} %get-tuple-element.11), channel_id=1, source_target_pairs={{0,1},{1,2},{2,3},{3,4},{4,5},{5,6},{6,7},{8,9},{9,10},{10,11},{11... | collective-permute-start | bytes 147464 | tf_op jit(solution)/shard_map/ppermute | solution.py:337
  32.7 5.0 %collective-permute-start.5 = (f32[4,24,128]{2,1,0:T(8,128)}, f32[4,24,128]{2,1,0:T(8,128)S(1)}, u32[]{:S(2)}, u32[]{:S(2)}) collective-permute-start(f32[4,24,128]{2,1,0:T(8,128)} %get-tuple-element.12), channel_id=1, source_target_pairs={{1,0},{2,1},{3,2},{4,3},{5,4},{6,5},{7,6},{9,8},{10,9},{11,10},{12... | collective-permute-start | bytes 147464 | tf_op jit(solution)/shard_map/ppermute | solution.py:338
  34.6 3.1 %copy-start.1 = (f32[4,24,128]{2,1,0:T(8,128)}, f32[4,24,128]{2,1,0:T(8,128)S(1)}, u32[]{:S(2)}) copy-start(f32[4,24,128]{2,1,0:T(8,128)S(1)} %collective-permute-done.4.zlo) | copy-start | bytes 147460
  37.7 0.6 copy-start.2

commit v2 on v1

v2 whole, which is shorter than its diff:
```python
import functools

import jax
import jax.numpy as jnp
from jax import lax
from jax.experimental import pallas as pl
from jax.experimental.pallas import tpu as pltpu
from jax.sharding import Mesh
from jax.sharding import PartitionSpec as P

BLOCK = 16
COARSE = 8
GX = ("gx_0", "gx_1")
GZ = ("gz_0", "gz_1")
ALL = ("gx_0", "gx_1", "gy", "gz_0", "gz_1")

FLOOR_STIFFNESS = 0.05
MASS_TERM = 0.001
COUPLING = 2.5
RELAXATION = 0.6

W = 4
NP = 16 + 2 * W
ROWS = 40
GROUPS = (4, 12, 20)
OWN_GROUPS = (8, 16)
DIAG = 6.0 + 2.0 * COUPLING
OWN = 1.0 + COUPLING
MIX = 0.25 * COUPLING
KEEP = 1.0 - RELAXATION
F32 = jnp.float32


def lanes_of(shape):
    return lax.broadcasted_iota(jnp.int32, shape, 1)


def rows_of(shape):
    return lax.broadcasted_iota(jnp.int32, shape, 0)


def stiffness_of(damage):
    level = damage.astype(F32) / 15.0
    return (1.0 - level) ** 2 * (1.0 - FLOOR_STIFFNESS) + FLOOR_STIFFNESS


def position(axis):
    at = lax.axis_index(axis)
    return at, lax.axis_size(axis), at % 2


def pick(odd, when_odd, when_even):
    return jnp.where(odd, when_odd, when_even)


def tail_edges(tail, row, page, up):
    parts = tail_parts(tail, row, page)
    return parts[0] if up else parts[1]


def tail_parts(tail, row, page):
    v = [tail[page, c, pl.ds(row, 8), :] for c in range(3)]
    yp = [tail[page, c, pl.ds(row + 1, 8), :] for c in range(3)]
    ym = [tail[page, c, pl.ds(row - 1, 8), :] for c in range(3)]
    xp = [pltpu.roll(v[c], 128 - W, 1) for c in range(3)]
    xm = [pltpu.roll(v[c], W, 1) for c in range(3)]
    zx = MIX * (xp[2] - xm[2])
    zy = MIX * (yp[2] - ym[2])
    zz = MIX * ((xp[0] - xm[0]) + (yp[1] - ym[1]))
    own = OWN * v[2]
    ups = (v[0] + zx, v[1] + zy, own + zz)
    downs = (v[0] - zx, v[1] - zy, own - zz)
    return ups, downs, v, xp, xm, yp, ym


def tail_sweep(source, target, pq, edges, outer_only=False):
    lane = lanes_of((8, 128))
    first = lane % W == 0
    last = lane % W == W - 1
    for row in GROUPS:
        for low in (0, 2):
            parts = [tail_parts(source, row, page) for page in (low, low + 1)]
            (up_a, down_a), (up_b, down_b) = (part[:2] for part in parts)
            for c in range(3):
                if low == 0:
                    edges[3 + c, pl.ds(row, 8), :] = down_a[c]
                else:
                    edges[c, pl.ds(row, 8), :] = up_b[c]
            sums = (
                [
                    jnp.where(last, pltpu.roll(up_b[c], W - 1, 1), pltpu.roll(up_a[c], 127, 1))
                    + pltpu.roll(down_a[c], 1, 1)
                    for c in range(3)
                ],
                [
                    jnp.where(first, pltpu.roll(down_a[c], 129 - W, 1), pltpu.roll(down_b[c], 1, 1))
                    + pltpu.roll(up_b[c], 127, 1)
                    for c in range(3)
                ],
            )
            for t in range(2):
                if outer_only and low + t in (1, 2):
                    continue
                _, _, v, xp, xm, yp, ym = parts[t]
                dy0 = MIX * (yp[0] - ym[0])
                dy1 = MIX * (yp[1] - ym[1])
                mix_x = pltpu.roll(dy1, 128 - W, 1) - pltpu.roll(dy1, W, 1)
                mix_y = pltpu.roll(dy0, 128 - W, 1) - pltpu.roll(dy0, W, 1)
                rest = (
                    OWN * (xp[0] + xm[0]) + (yp[0] + ym[0]) + mix_x,
                    OWN * (yp[1] + ym[1]) + (xp[1] + xm[1]) + mix_y,
                    (xp[2] + xm[2]) + (yp[2] + ym[2]),
                )
                q = pq[low + t, 3, pl.ds(row, 8), :]
                for c in range(3):
                    p = pq[low + t, c, pl.ds(row, 8), :]
                    target[low + t, c, pl.ds(row, 8), :] = (
                        KEEP * v[c] + p + q * (rest[c] + sums[t][c])
                    )


def edges_only(source, edges):
    for row in OWN_GROUPS:
        ups = tail_parts(source, row, 3)[0]
        downs = tail_parts(source, row, 0)[1]
        for c in range(3):
            edges[c, pl.ds(row, 8), :] = ups[c]
            edges[3 + c, pl.ds(row, 8), :] = downs[c]


def neighbour_sum(ref, edges, i, row, lane):
    def at(c, dx, dy):
        return ref[i + dx, c, pl.ds(row + dy, 8), :]

    v = [at(c, 0, 0) for c in range(3)]
    xp = [at(c, 1, 0) for c in range(3)]
    xm = [at(c, -1, 0) for c in range(3)]
    yp = [at(c, 0, 1) for c in range(3)]
    ym = [at(c, 0, -1) for c in range(3)]
    zx = MIX * (xp[2] - xm[2])
    zy = MIX * (yp[2] - ym[2])
    zz = MIX * ((xp[0] - xm[0]) + (yp[1] - ym[1]))
    own = OWN * v[2]
    ups = (v[0] + zx, v[1] + zy, own + zz)
    downs = (v[0] - zx, v[1] - zy, own - zz)
    mix_x = (at(1, 1, 1) - at(1, 1, -1)) - (at(1, -1, 1) - at(1, -1, -1))
    mix_y = (at(0, 1, 1) - at(0, 1, -1)) - (at(0, -1, 1) - at(0, -1, -1))
    rest = (
        OWN * (xp[0] + xm[0]) + (yp[0] + ym[0]) + MIX * mix_x,
        OWN * (yp[1] + ym[1]) + (xp[1] + xm[1]) + MIX * mix_y,
        (xp[2] + xm[2]) + (yp[2] + ym[2]),
    )
    sums = []
    for c in range(3):
        high = pltpu.roll(edges[c, pl.ds(row, 8), :], 127 - W * i, 1)
        low = pltpu.roll(edges[3 + c, pl.ds(row, 8), :], 129 - W - W * i, 1)
        up = jnp.where(lane == 127, high, pltpu.roll(ups[c], 127, 1))
        down = jnp.where(lane == 0, low, pltpu.roll(downs[c], 1, 1))
        sums.append(rest[c] + (up + down))
    return sums, v


def sweep(source, target, pq, edges, first, last):
    lane = lanes_of((8, 128))

    def plane(i, carry):
        for row in GROUPS:
            sums, v = neighbour_sum(source, edges, i, row, lane)
            q = pq[i, 3, pl.ds(row, 8), :]
            for c in range(3):
                p = pq[i, c, pl.ds(row, 8), :]
                target[i, c, pl.ds(row, 8), :] = KEEP * v[c] + p + q * sums[c]
        return carry

    lax.fori_loop(first, last, plane, 0, unroll=2)


def x_pack_kernel(load, damage, f_out, far_out, near_out, level, load_sem, level_sem):
    odd = position(GX)[2] == 1
    load_copy = pltpu.make_async_copy(load, f_out.at[pl.ds(0, 3)], load_sem)
    level_copy = pltpu.make_async_copy(damage, level, level_sem)
    load_copy.start()
    level_copy.start()
    level_copy.wait()
    f_out[3] = level[...].astype(F32)
    load_copy.wait()
    for c in range(4):
        for i in range(W):
            low, high = f_out[c, i], f_out[c, i + 16 - W]
            far_out[c, i] = pick(odd, high, low)
            near_out[c, i] = pick(odd, low, high)


def y_pack_kernel(f, xfar, xnear, far_out, near_out):
    odd_x, odd_y = position(GX)[2] == 1, position("gy")[2] == 1
    upper = rows_of((8, 128)) < 4

    def tile(c, i, k):
        rows = pl.ds(8 * k, 8)
        if i < W:
            return pick(odd_x, xnear[c, i, rows, :], xfar[c, i, rows, :])
        if i >= W + 16:
            return pick(odd_x, xfar[c, i - W - 16, rows, :], xnear[c, i - W - 16, rows, :])
        return f[c, i - W, rows, :]

    for c in range(4):
        for j in range(NP // 2):
            a, b = 2 * j, 2 * j + 1
            low = jnp.where(upper, tile(c, a, 0), pltpu.roll(tile(c, b, 0), 4, 0))
            high = jnp.where(upper, pltpu.roll(tile(c, a, 1), 4, 0), tile(c, b, 1))
            far_out[c, j] = pick(odd_y, high, low)
            near_out[c, j] = pick(odd_y, low, high)


def z_pack_kernel(f, xfar, xnear, yfar, ynear, far_out, near_out):
    odd_x, odd_y, odd_z = position(GX)[2] == 1, position("gy")[2] == 1, position(GZ)[2]
    lane = lanes_of((8, 128))
    upper = rows_of((8, 128)) < 4
    for c in range(4):
        for k in range(3):
            far = jnp.zeros((8, 128), F32)
            near = far
            for i in range(NP):
                if k == 2:
                    low = pick(odd_y, ynear[c, i // 2], yfar[c, i // 2])
                    high = pick(odd_y, yfar[c, i // 2], ynear[c, i // 2])
                    if i % 2:
                        value = jnp.where(upper, pltpu.roll(low, 4, 0), high)
                    else:
                        value = jnp.where(upper, low, pltpu.roll(high, 4, 0))
                else:
                    rows = pl.ds(8 * k, 8)
                    if i < W:
                        value = pick(odd_x, xnear[c, i, rows, :], xfar[c, i, rows, :])
                    elif i >= W + 16:
                        j = i - W - 16
                        value = pick(odd_x, xfar[c, j, rows, :], xnear[c, j, rows, :])
                    else:
                        value = f[c, i - W, rows, :]
                here = (lane >= W * i) & (lane < W * i + W)
                far = jnp.where(here, pltpu.roll(value, W * i + W * odd_z, 1), far)
                near = jnp.where(here, pltpu.roll(value, W * i + W * (1 - odd_z), 1), near)
            far_out[c, pl.ds(8 * k, 8), :] = far
            near_out[c, pl.ds(8 * k, 8), :] = near


def main_kernel(f, xfar, xnear, yfar, ynear, pq):
    gx, gx_n, odd_x = position(GX)
    gy, gy_n, odd_y = position("gy")
    odd_x, odd_y = odd_x == 1, odd_y == 1

    def x_inside(i):
        x = gx * 16 + i - W
        return (x >= 0) & (x < gx_n * 16)

    def values(parts, inside):
        g = stiffness_of(parts[3])
        scale = RELAXATION / (g * DIAG + MASS_TERM)
        out = [part * scale for part in parts[:3]] + [g * scale]
        return [jnp.where(inside, value, 0.0) for value in out]

    def fill(i, parts):
        for c, value in enumerate(values(parts, x_inside(i))):
            pq[i, c, pl.ds(8, 16), :] = value

    def own(i, carry):
        fill(i, [f[c, i - W] for c in range(4)])
        return carry

    lax.fori_loop(W, W + 16, own, 0)

    def beside_x(i, carry):
        fill(i, [pick(odd_x, xnear[c, i], xfar[c, i]) for c in range(4)])
        fill(i + W + 16, [pick(odd_x, xfar[c, i], xnear[c, i]) for c in range(4)])
        return carry

    lax.fori_loop(0, W, beside_x, 0)
    second = (rows_of((8, 128)) >= 4).astype(jnp.int32)
    low_in, high_in = gy > 0, gy < gy_n - 1

    def beside_y(j, carry):
        inside = x_inside(2 * j + second)
        low = values([pick(odd_y, ynear[c, j], yfar[c, j]) for c in range(4)], inside & low_in)
        high = values([pick(odd_y, yfar[c, j], ynear[c, j]) for c in range(4)], inside & high_in)
        for c in range(4):
            for t in range(2):
                pq[2 * j + t, c, pl.ds(4, 4), :] = low[c][4 * t : 4 * t + 4]
                pq[2 * j + t, c, pl.ds(24, 4), :] = high[c][4 * t : 4 * t + 4]
        return carry

    lax.fori_loop(0, NP // 2, beside_y, 0)


def first_kernel(
    pq, f, zfar_own, znear_own, zfar, znear, x2, tail, tail_pq, sums_out, edges
):
    lane = lanes_of((8, 128))
    row8 = rows_of((8, 128))
    gx, gx_n, _ = position(GX)
    gy, gy_n, _ = position("gy")
    gz, gz_n, odd_z = position(GZ)
    odd_z = odd_z == 1
    x = gx * 16 + lane // W - W
    x_in = (x >= 0) & (x < gx_n * 16)
    y_in = ((row8 >= 4) | (gy > 0)) & ((row8 < 4) | (gy < gy_n - 1))
    z_in = (gz > 0, True, True, gz < gz_n - 1)
    sides = (
        (znear, zfar),
        (znear_own, zfar_own),
        (zfar_own, znear_own),
        (zfar, znear),
    )
    for page in range(4):
        when_odd, when_even = sides[page]
        for k in range(3):
            rows = pl.ds(8 * k, 8)
            parts = [pick(odd_z, when_odd[c, rows, :], when_even[c, rows, :]) for c in range(4)]
            g = stiffness_of(parts[3])
            scale = RELAXATION / (g * DIAG + MASS_TERM)
            inside = x_in
            if page in (0, 3):
                inside = inside & z_in[page]
            if k == 2:
                inside = inside & y_in
            for c in range(4):
                value = jnp.where(inside, (parts[c] if c < 3 else g) * scale, 0.0)
                if k < 2:
                    tail_pq[page, c, pl.ds(8 + 8 * k, 8), :] = value
                else:
                    tail_pq[page, c, pl.ds(4, 4), :] = value[:4]
                    tail_pq[page, c, pl.ds(24, 4), :] = value[4:]
    tail_sweep(tail_pq, tail, tail_pq, edges)
    sweep(pq, x2, pq, edges, 1, NP - 1)
    edges_only(tail, edges)

    def residual(i, carry):
        totals = list(carry)
        for row in OWN_GROUPS:
            sums, v = neighbour_sum(x2, edges, i, row, lane)
            rows = pl.ds(row - 8, 8)
            g = stiffness_of(f[3, i - W, rows, :])
            d = g * DIAG + MASS_TERM
            for c in range(3):
                load = f[c, i - W, rows, :]
                totals[c] += (load - d * v[c]) + g * sums[c]
                totals[4] += load * load
            totals[3] += g
        return tuple(totals)

    zero = jnp.zeros((8, 128), F32)
    totals = lax.fori_loop(W, W + 16, residual, (zero,) * 5, unroll=2)
    stacked = zero
    for c in range(5):
        stacked = jnp.where(row8 == c, jnp.sum(totals[c], axis=0, keepdims=True), stacked)
    big = (128, 128)
    gather = (rows_of(big) // BLOCK == lanes_of(big) % 8).astype(F32)
    by_cell = jnp.dot(
        stacked, gather, precision=lax.Precision.HIGHEST, preferred_element_type=F32
    )
    slot = jnp.sum(jnp.where(lane // 8 == row8, by_cell, 0.0), axis=0, keepdims=True)
    sums_out[...] = jnp.broadcast_to(slot, sums_out.shape)


def coarse_solve(load, mean, gx_n, gy_n, gz_n):
    shape = load[0].shape
    n = shape[1]
    lane = lanes_of(shape)
    row = rows_of(shape)
    sx, sy = gy_n * gz_n, gz_n
    x_at, y_at, z_at = lane // sx, lane // sy % gy_n, lane % gz_n

    def shift(v, step, at, count):
        up = jnp.where(at < count - 1, pltpu.roll(v, n - step, 1), 0.0)
        down = jnp.where(at > 0, pltpu.roll(v, step, 1), 0.0)
        return up, down

    def shift_z(v):
        up = pltpu.roll(v, 7, 0)
        down = pltpu.roll(v, 1, 0)
        next_up = jnp.where(z_at < gz_n - 1, pltpu.roll(up, n - 1, 1), 0.0)
        next_down = jnp.where(z_at > 0, pltpu.roll(down, 1, 1), 0.0)
        return jnp.where(row == 7, next_up, up), jnp.where(row == 0, next_down, down)

    shifts = (
        lambda v: shift(v, sx, x_at, gx_n),
        lambda v: shift(v, sy, y_at, gy_n),
        shift_z,
    )
    coefficient = BLOCK**2 * mean
    scale = RELAXATION / (coefficient * DIAG + BLOCK**3 * MASS_TERM)
    p = [scale * value for value in load]
    q = scale * coefficient

    def step(_, w):
        pairs = [[shifts[b](w[a]) for b in range(3)] for a in range(3)]
        diffs = [pairs[a][a][0] - pairs[a][a][1] for a in range(3)]
        out = []
        for a in range(3):
            total = 0.0
            for b in range(3):
                both = pairs[a][b][0] + pairs[a][b][1]
                total = total + (OWN * both if a == b else both)
            others = [diffs[b] for b in range(3) if b != a]
            up, down = shifts[a](others[0] + others[1])
            out.append(KEEP * w[a] + p[a] + q * (total + MIX * (up - down)))
        return tuple(out)

    return lax.fori_loop(0, COARSE - 1, step, tuple(p))


def second_kernel(
    every,
    x2,
    tail2,
    pq,
    tail_pq,
    f,
    out,
    sum_out,
    x3,
    x4,
    tail3,
    tail4,
    w_ref,
    edges,
    out_sem,
):
    gx, gx_n, _ = position(GX)
    gy, gy_n, _ = position("gy")
    gz, gz_n, _ = position(GZ)
    me = (gx * gy_n + gy) * gz_n + gz
    lane = lanes_of((8, 128))
    row8 = rows_of((8, 128))
    cells = jnp.transpose(every[...])
    load = [cells[8 * c : 8 * c + 8] for c in range(3)]
    mean = cells[24:32] * (1.0 / BLOCK**3)
    load_sum = jnp.sum(cells[32:40])
    w = coarse_solve(load, mean, gx_n, gy_n, gz_n)
    n = gx_n * gy_n * gz_n
    centre = n // 2
    own_cells = (lane // BLOCK == row8).astype(F32)
    line = lane[:1]
    cell_of = ((7, -1), (0, 0), (7, 0), (0, 1))
    spans = ((4, 4), (8, 16), (24, 4))
    for c in range(3):
        turned = pltpu.roll(w[c], (centre + n - me) % n, 1)

        def column(dx, dy):
            return centre + (dx - 1) * gy_n * gz_n + (dy - 1) * gz_n

        for dy in range(3):
            first, size = spans[dy]
            for dx in range(3):
                j = column(dx, dy)
                main = jnp.sum(turned[:, j : j + 1] * own_cells, axis=0, keepdims=True)
                w_ref[dx, c, pl.ds(first, size), :] = jnp.broadcast_to(main, (size, 128))
            for page in range(4):
                k, dz = cell_of[page]
                here = [
                    jnp.broadcast_to(
                        turned[k : k + 1, column(dx, dy) + dz : column(dx, dy) + dz + 1], (1, 128)
                    )
                    for dx in range(3)
                ]
                value = jnp.where(
                    line < W * W, here[0], jnp.where(line < W * (W + 16), here[1], here[2])
                )
                rows = pl.ds(first, size)
                inside = tail_pq[page, 3, rows, :] > 0.0
                tail3[page, c, rows, :] = tail2[page, c, rows, :] + jnp.where(inside, value, 0.0)

    def correct(i, carry):
        cell = (i >= W).astype(jnp.int32) + (i >= W + 16).astype(jnp.int32)
        for row in GROUPS:
            rows = pl.ds(row, 8)
            inside = pq[i, 3, rows, :] > 0.0
            for c in range(3):
                x3[i, c, rows, :] = x2[i, c, rows, :] + jnp.where(
                    inside, w_ref[cell, c, rows, :], 0.0
                )
        return carry

    lax.fori_loop(1, NP - 1, correct, 0)
    tail_sweep(tail3, tail4, tail_pq, edges)
    sweep(x3, x4, pq, edges, 2, NP - 2)
    tail_sweep(tail4, tail3, tail_pq, edges, True)
    sweep(x4, x3, pq, edges, 3, NP - 3)
    copies = [
        pltpu.make_async_copy(
            x3.at[pl.ds(W, 16), c, pl.ds(8, 16), :], out.at[c], out_sem.at[c]
        )
        for c in range(3)
    ]
    for copy in copies:
        copy.start()
    edges_only(tail3, edges)

    def residual(i, total):
        for row in OWN_GROUPS:
            sums, v = neighbour_sum(x3, edges, i, row, lane)
            rows = pl.ds(row - 8, 8)
            g = stiffness_of(f[3, i - W, rows, :])
            d = (g * DIAG + MASS_TERM) * (1.0 / RELAXATION)
            q = pq[i, 3, pl.ds(row, 8), :]
            for c in range(3):
                p = pq[i, c, pl.ds(row, 8), :]
                r = d * ((p - RELAXATION * v[c]) + q * sums[c])
                total += r * r
        return total

    total = jnp.sum(lax.fori_loop(W, W + 16, residual, jnp.zeros((8, 128), F32), unroll=2))
    both = jnp.where(line == 0, load_sum * (1.0 / n), total)
    sum_out[...] = jnp.broadcast_to(both, sum_out.shape)
    for copy in copies:
        copy.wait()


def swaps(far_send, near_send, axis):
    count = lax.axis_size(axis)
    near = [(i, i ^ 1) for i in range(count)]
    far = [(i, ((i ^ 1) + (2 if i % 2 else -2)) % count) for i in range(count)]
    return lax.ppermute(far_send, axis, far), lax.ppermute(near_send, axis, near)


VMEM = pl.BlockSpec(memory_space=pltpu.VMEM)
SMEM = pl.BlockSpec(memory_space=pltpu.SMEM)
HBM = pl.BlockSpec(memory_space=pltpu.HBM)


def call(kernel, shapes, arguments, mib, scratch=(), source=VMEM, target=VMEM):
    shapes = [jax.ShapeDtypeStruct(shape, F32) for shape in shapes]
    return pl.pallas_call(
        kernel,
        out_shape=tuple(shapes),
        in_specs=[source] * len(arguments),
        out_specs=target if isinstance(target, tuple) else (target,) * len(shapes),
        scratch_shapes=[pltpu.VMEM(s, F32) if isinstance(s, tuple) else s for s in scratch],
        compiler_params=pltpu.CompilerParams(vmem_limit_bytes=mib << 20),
    )(*arguments)


def norms_kernel(count, parts, out):
    root = jnp.sqrt(jnp.sum(parts[...], axis=0, keepdims=True) * (1.0 / count))
    out[0] = root[0, 0]
    out[1] = root[0, 1]


def on_device(right_side, damage):
    n = lax.axis_size(ALL)
    slab = (4, W, 16, 128)
    f, *x_sends = call(
        x_pack_kernel,
        ((4, 16, 16, 128), slab, slab),
        tuple(pltpu.with_memory_space_constraint(x, pltpu.HBM) for x in (right_side, damage)),
        8,
        (
            pltpu.VMEM((16, 16, 128), jnp.int32),
            pltpu.SemaphoreType.DMA(()),
            pltpu.SemaphoreType.DMA(()),
        ),
        source=HBM,
    )
    x_pieces = swaps(*x_sends, GX)
    slab = (4, NP // 2, 8, 128)
    y_sends = call(y_pack_kernel, (slab, slab), (f, *x_pieces), 8)
    y_pieces = swaps(*y_sends, "gy")
    pieces = (f, *x_pieces, *y_pieces)
    side = (4, NP, 128)
    z_sends = call(z_pack_kernel, (side, side), pieces, 8)
    z_pieces = swaps(*z_sends, GZ)
    field = (NP, 4, ROWS, 128)
    tails = (4, 4, ROWS, 128)
    edges = (6, ROWS, 128)
    (pq,) = call(main_kernel, (field,), pieces, 8)
    x2, tail, tail_pq, sums = call(
        first_kernel,
        (field, tails, tails, (n, 128)),
        (pq, f, *z_sends, *z_pieces),
        12,
        (edges,),
    )
    every = lax.all_to_all(sums, ALL, 0, 0, tiled=True)
    displacement, partial_sums = call(
        second_kernel,
        (right_side.shape, (n, 128)),
        (every, x2, tail, pq, tail_pq, f),
        20,
        (field, field, tails, tails, (3, 3, ROWS, 128), edges, pltpu.SemaphoreType.DMA((3,))),
        target=(HBM, VMEM),
    )
    partial_sums = lax.all_to_all(partial_sums, ALL, 0, 0, tiled=True)
    (norms,) = call(
        functools.partial(norms_kernel, right_side.size * n), ((2,),), (partial_sums,), 2, target=SMEM
    )
    return (displacement, norms)


def solution(mesh):
    torus = Mesh(mesh.devices.reshape(4, 2, mesh.shape["gy"], 2, 4), ALL)
    placed = (P(None, GX, "gy", GZ), P(GX, "gy", GZ))
    return jax.shard_map(
        on_device,
        mesh=torus,
        in_specs=placed,
        out_specs=(P(None, GX, "gy", GZ), P()),
        check_vma=False,
    )
```

time: 113 us -> 81 us (0.72)
  Pallas kernels: 24.4 us -> 13.4 us
  other arithmetic: 5.95 us -> 0 us
  waiting for transfers between devices: 13.5 us -> 7.77 us
  blocking collectives: 50 us -> 45.8 us
  starting transfers between devices: 17.1 us -> 13.2 us
  local copies, waits for them, and re-layouts: 1.25 us -> 0 us
    pallas_call x3 -> x7, Pallas kernels: 24.4 us -> 13.4 us  [call(): pl.pallas_call(kernel, out_shape=tuple(shapes), in_specs=[source] * len(a...]
    ppermute x6, waiting for transfers between devices: 13.5 us -> 7.77 us  [the longest x3 4.44 us: swaps(): lax.ppermute(far_send, axis, far)]
    ppermute x6, starting transfers between devices: 17.1 us -> 13.2 us  [the longest x3 10.3 us: swaps(): lax.ppermute(far_send, axis, far)]
    all_to_all x1, blocking collectives: 31.3 us -> 27.5 us  [on_device(): every = lax.all_to_all(sums, ALL, 0, 0, tiled=True)]
    sqrt x1 -> x0, other arithmetic: 1.77 us -> none  [on_device(): norms = jnp.sqrt(jnp.stack([load_sum[0, 0], residual_sum]) / total_count)]
    concatenate x1 -> x0, other arithmetic: 1.25 us -> none  [beside(): return jnp.concatenate([low, block, high], axis=dim)]
  transfers between devices with their start and end apart: 6 -> 6, of which waited for: 4 -> 5; matrix products, arithmetic and copies ran while one was open for 1% -> 0% of each run, Pallas kernels for 0% -> 1%
where the time goes in v2:
time: 81 us; the launch traced here: 80.9 us
  blocking collectives  45.8 us (57%)
  Pallas kernels  13.4 us (17%)
  starting transfers between devices  13.2 us (16%)
  waiting for transfers between devices  7.77 us (10%)
    all_to_all x1, blocking collectives, on_device(): every = lax.all_to_all(sums, ALL, 0, 0, tiled=True)  27.5 us
    all_to_all x1, blocking collectives, on_device(): partial_sums = lax.all_to_all(partial_sums, ALL, 0, 0, tiled=True)  18.3 us
    pallas_call x7, Pallas kernels, call(): pl.pallas_call(kernel, out_shape=tuple(shapes), in_specs=[source] * len(a...  13.4 us
    ppermute x3, starting transfers between devices, swaps(): lax.ppermute(far_send, axis, far)  10.3 us
    ppermute x3, waiting for transfers between devices, swaps(): lax.ppermute(far_send, axis, far)  4.44 us
    ppermute x3, waiting for transfers between devices, swaps(): lax.ppermute(near_send, axis, near)  3.33 us
    ppermute x3, starting transfers between devices, swaps(): lax.ppermute(near_send, axis, near)  2.87 us
  transfers between devices with their start and end apart: 6, of which 5 were waited for; matrix products, arithmetic and copies ran while one was open for 0% of the time, Pallas kernels for 1%

profile of v2, /device:TPU:1, one launch (start us, length us, event | category | flops | bytes accessed | tf_op | source)
XLA Modules:
  0.0 80.9 jit_solution(12421278776290938337)
XLA Ops:
  0.6 1.1 %shard_map.41 = (f32[4,16,16,128]{3,2,1,0:T(8,128)S(1)}, f32[4,4,16,128]{3,2,1,0:T(8,128)S(1)}, f32[4,4,16,128]{3,2,1,0:T(8,128)S(1)}) custom-call(f32[3,16,16,128]{3,2,1,0:T(8,128)} %load.1, s32[16,16,128]{2,1,0:T(8,128)} %damage.1), custom_call_target="tpu_custom_call" | custom-call | tf_op jit(solution)/shard_map/pallas_call | solution.py:532
  1.7 4.5 %collective-permute-start = (f32[4,4,16,128]{3,2,1,0:T(8,128)S(1)}, f32[4,4,16,128]{3,2,1,0:T(8,128)S(1)}, u32[]{:S(2)}, u32[]{:S(2)}) collective-permute-start(f32[4,4,16,128]{3,2,1,0:T(8,128)S(1)} %get-tuple-element.16), channel_id=1, source_target_pairs={{0,224},{32,64},{64,32},{96,128},{128,96},{160,192},{192,160},{224... | collective-permute-start | bytes 393224 | tf_op jit(solution)/shard_map/ppermute | solution.py:522
  6.2 2.9 %collective-permute-start.1 = (f32[4,4,16,128]{3,2,1,0:T(8,128)S(1)}, f32[4,4,16,128]{3,2,1,0:T(8,128)S(1)}, u32[]{:S(2)}, u32[]{:S(2)}) collective-permute-start(f32[4,4,16,128]{3,2,1,0:T(8,128)S(1)} %get-tuple-element.17), channel_id=1, source_target_pairs={{0,32},{32,0},{64,96},{96,64},{128,160},{160,128},{192,224},{224,1... | collective-permute-start | bytes 393224 | tf_op jit(solution)/shard_map/ppermute | solution.py:522
  9.0 0.0 collective-permute-done.xfar
  9.0 1.0 %collective-permute-done.1.xnear = f32[4,4,16,128]{3,2,1,0:T(8,128)S(1)} collective-permute-done((f32[4,4,16,128]{3,2,1,0:T(8,128)S(1)}, f32[4,4,16,128]{3,2,1,0:T(8,128)S(1)}, u32[]{:S(2)}, u32[]{:S(2)}) %collective-permute-start.1) | collective-permute-done | bytes 131104 | tf_op jit(solution)/shard_map/ppermute | solution.py:522
  10.0 0.1 shard_map.42
  10.1 2.6 %collective-permute-start.2 = (f32[4,12,8,128]{3,2,1,0:T(8,128)S(1)}, f32[4,12,8,128]{3,2,1,0:T(8,128)S(1)}, u32[]{:S(2)}, u32[]{:S(2)}) collective-permute-start(f32[4,12,8,128]{3,2,1,0:T(8,128)S(1)} %get-tuple-element.18), channel_id=1, source_target_pairs={{0,24},{8,16},{16,8},{24,0},{1,25},{9,17},{17,9},{25,1},{2,26},{10... | collective-permute-start | bytes 589832 | tf_op jit(solution)/shard_map/ppermute | solution.py:522
  12.6 0.0 collective-permute-start.3
  12.7 3.2 %collective-permute-done.2.yfar = f32[4,12,8,128]{3,2,1,0:T(8,128)S(1)} collective-permute-done((f32[4,12,8,128]{3,2,1,0:T(8,128)S(1)}, f32[4,12,8,128]{3,2,1,0:T(8,128)S(1)}, u32[]{:S(2)}, u32[]{:S(2)}) %collective-permute-start.2) | collective-permute-done | bytes 196640 | tf_op jit(solution)/shard_map/ppermute | solution.py:522
  15.9 1.3 %collective-permute-done.3.ynear = f32[4,12,8,128]{3,2,1,0:T(8,128)S(1)} collective-permute-done((f32[4,12,8,128]{3,2,1,0:T(8,128)S(1)}, f32[4,12,8,128]{3,2,1,0:T(8,128)S(1)}, u32[]{:S(2)}, u32[]{:S(2)}) %collective-permute-start.3) | collective-permute-done | bytes 196640 | tf_op jit(solution)/shard_map/ppermute | solution.py:522
  17.2 0.7 shard_map.44
  17.9 3.3 %collective-permute-start.4 = (f32[4,24,128]{2,1,0:T(8,128)S(1)}, f32[4,24,128]{2,1,0:T(8,128)S(1)}, u32[]{:S(2)}, u32[]{:S(2)}) collective-permute-start(f32[4,24,128]{2,1,0:T(8,128)S(1)} %get-tuple-element.20.zfar_own), channel_id=1, source_target_pairs={{0,7},{1,2},{2,1},{3,4},{4,3},{5,6},{6,5},{7,0},{8,15},{9,10},{10,... | collective-permute-start | bytes 147464 | tf_op jit(solution)/shard_map/ppermute | solution.py:522
  21.1 0.0 collective-permute-start.5
  21.2 0.7 shard_map.43.pq
  21.8 1.2 %collective-permute-done.4.zfar = f32[4,24,128]{2,1,0:T(8,128)S(1)} collective-permute-done((f32[4,24,128]{2,1,0:T(8,128)S(1)}, f32[4,24,128]{2,1,0:T(8,128)S(1)}, u32[]{:S(2)}, u32[]{:S(2)}) %collective-permute-start.4) | collective-permute-done | bytes 49184 | tf_op jit(solution)/shard_map/ppermute | solution.py:522
  23.0 1.1 %collective-permute-done.5.znear = f32[4,24,128]{2,1,0:T(8,128)S(1)} collective-permute-done((f32[4,24,128]{2,1,0:T(8,128)S(1)}, f32[4,24,128]{2,1,0:T(8,128)S(1)}, u32[]{:S(2)}, u32[]{:S(2)}) %collective-permute-start.5) | collective-permute-done | bytes 49184 | tf_op jit(solution)/shard_map/ppermute | solution.py:522
  24.1 3.4 %shard_map.45 = (f32[24,4,40,128]{3,2,1,0:T(8,128)S(1)}, f32[4,4,40,128]{3,2,1,0:T(8,128)S(1)}, f32[4,4,40,128]{3,2,1,0:T(8,128)S(1)}, f32[256,128]{1,0:T(8,128)S(1)}) custom-call(f32[24,4,40,128]{3,2,1,0:T(8,128)S(1)} %shard_map.43.pq, f32[4,16,16,128]{3,2,1,0:T(8,128)S(1)} %get-tuple-element.15.f, f32[4,24,128]{2,1,0:T(8,128)S(1)} %get-tuple-element.20.zfar_own, ...), custom_call_target="tpu_custom_call" | custom-call | tf_op jit(solution)/shard_map/pallas_call | solution.py:532
  27.5 27.5 %all_to_all.22 = f32[256,1,128]{2,1,0:T(1,128)S(1)} all-to-all(f32[256,1,128]{2,1,0:T(1,128)S(1)} %bitcast.10), channel_id=1, replica_groups=mesh['gx_0'=4,'gx_1'=2,'gy'=4,'gz_0'=2,'gz_1'=4] {'gx_0','gx_1','gy','gz..., dimensions={0} | all-to-all | bytes 262144 | tf_op jit(solution)/shard_map/all_to_all | solution.py:582
  55.1 6.8 %shard_map.46 = (f32[3,16,16,128]{3,2,1,0:T(8,128)}, f32[256,128]{1,0:T(8,128)S(1)}) custom-call(f32[256,128]{1,0:T(8,128)S(1)} %bitcast.8, f32[24,4,40,128]{3,2,1,0:T(8,128)S(1)} %get-tuple-element.23.x2, f32[4,4,40,128]{3,2,1,0:T(8,128)S(1)} %get-tuple-element.24.tail2, f32[24,4,40,128]{3,2,1,0:T(8,128)S(1)} %shard_map.43.pq, ...), custom_call_target="tpu_custom_call" | custom-call | tf_op jit(solution)/shard_map/pallas_call | solution.py:532
  61.9 18.3 %all_to_all.23 = f32[256,1,128]{2,1,0:T(1,128)S(1)} all-to-all(f32[256,1,128]{2,1,0:T(1,128)S(1)} %bitcast.11), channel_id=1, replica_groups=mesh['gx_0'=4,'gx_1'=2,'gy'=4,'gz_0'=2,'gz_1'=4] {'gx_0','gx_1','gy','gz..., dimensions={0} | all-to-all | bytes 262144 | tf_op jit(solution)/shard_map/all_to_all | solution.py:591
  80.2 0.7 shard_map.47
Async XLA Ops:
  1.7 7.3 %collective-permute-start = (f32[4,4,16,128]{3,2,1,0:T(8,128)S(1)}, f32[4,4,16,128]{3,2,1,0:T(8,128)S(1)}, u32[]{:S(2)}, u32[]{:S(2)}) collective-permute-start(f32[4,4,16,128]{3,2,1,0:T(8,128)S(1)} %get-tuple-element.16), channel_id=1, source_target_pairs={{0,224},{32,64},{64,32},{96,128},{128,96},{160,192},{192,160},{224... | collective-permute-start | bytes 393224 | tf_op jit(solution)/shard_map/ppermute | solution.py:522
  6.2 3.9 %collective-permute-start.1 = (f32[4,4,16,128]{3,2,1,0:T(8,128)S(1)}, f32[4,4,16,128]{3,2,1,0:T(8,128)S(1)}, u32[]{:S(2)}, u32[]{:S(2)}) collective-permute-start(f32[4,4,16,128]{3,2,1,0:T(8,128)S(1)} %get-tuple-element.17), channel_id=1, source_target_pairs={{0,32},{32,0},{64,96},{96,64},{128,160},{160,128},{192,224},{224,1... | collective-permute-start | bytes 393224 | tf_op jit(solution)/shard_map/ppermute | solution.py:522
  10.1 5.8 %collective-permute-start.2 = (f32[4,12,8,128]{3,2,1,0:T(8,128)S(1)}, f32[4,12,8,128]{3,2,1,0:T(8,128)S(1)}, u32[]{:S(2)}, u32[]{:S(2)}) collective-permute-start(f32[4,12,8,128]{3,2,1,0:T(8,128)S(1)} %get-tuple-element.18), channel_id=1, source_target_pairs={{0,24},{8,16},{16,8},{24,0},{1,25},{9,17},{17,9},{25,1},{2,26},{10... | collective-permute-start | bytes 589832 | tf_op jit(solution)/shard_map/ppermute | solution.py:522
  12.6 4.5 %collective-permute-start.3 = (f32[4,12,8,128]{3,2,1,0:T(8,128)S(1)}, f32[4,12,8,128]{3,2,1,0:T(8,128)S(1)}, u32[]{:S(2)}, u32[]{:S(2)}) collective-permute-start(f32[4,12,8,128]{3,2,1,0:T(8,128)S(1)} %get-tuple-element.19), channel_id=1, source_target_pairs={{0,8},{8,0},{16,24},{24,16},{1,9},{9,1},{17,25},{25,17},{2,10},{10... | collective-permute-start | bytes 589832 | tf_op jit(solution)/shard_map/ppermute | solution.py:522
  17.9 5.1 %collective-permute-start.4 = (f32[4,24,128]{2,1,0:T(8,128)S(1)}, f32[4,24,128]{2,1,0:T(8,128)S(1)}, u32[]{:S(2)}, u32[]{:S(2)}) collective-permute-start(f32[4,24,128]{2,1,0:T(8,128)S(1)} %get-tuple-element.20.zfar_own), channel_id=1, source_target_pairs={{0,7},{1,2},{2,1},{3,4},{4,3},{5,6},{6,5},{7,0},{8,15},{9,10},{10,... | collective-permute-start | bytes 147464 | tf_op jit(solution)/shard_map/ppermute | solution.py:522
  21.1 2.9 %collective-permute-start.5 = (f32[4,24,128]{2,1,0:T(8,128)S(1)}, f32[4,24,128]{2,1,0:T(8,128)S(1)}, u32[]{:S(2)}, u32[]{:S(2)}) collective-permute-start(f32[4,24,128]{2,1,0:T(8,128)S(1)} %get-tuple-element.21.znear_own), channel_id=1, source_target_pairs={{0,1},{1,0},{2,3},{3,2},{4,5},{5,4},{6,7},{7,6},{8,9},{9,8},{10,11... | collective-permute-start | bytes 147464 | tf_op jit(solution)/shard_map/ppermute | solution.py:522

commit v3 on v2

--- a/solution.py
+++ b/solution.py
@@ -51,11 +51,6 @@
 
 def pick(odd, when_odd, when_even):
     return jnp.where(odd, when_odd, when_even)
-
-
-def tail_edges(tail, row, page, up):
-    parts = tail_parts(tail, row, page)
-    return parts[0] if up else parts[1]
 
 
 def tail_parts(tail, row, page):
@@ -73,59 +68,70 @@
     return ups, downs, v, xp, xm, yp, ym
 
 
-def tail_sweep(source, target, pq, edges, outer_only=False):
+def tail_sums(source, row, low):
     lane = lanes_of((8, 128))
+    parts = [tail_parts(source, row, page) for page in (low, low + 1)]
+    (up_a, down_a), (up_b, down_b) = (part[:2] for part in parts)
     first = lane % W == 0
     last = lane % W == W - 1
+    beside_z = (
+        [
+            jnp.where(last, pltpu.roll(up_b[c], W - 1, 1), pltpu.roll(up_a[c], 127, 1))
+            + pltpu.roll(down_a[c], 1, 1)
+            for c in range(3)
+        ],
+        [
+            jnp.where(first, pltpu.roll(down_a[c], 129 - W, 1), pltpu.roll(down_b[c], 1, 1))
+            + pltpu.roll(up_b[c], 127, 1)
+            for c in range(3)
+        ],
+    )
+    sums = []
+    for t in range(2):
+        _, _, v, xp, xm, yp, ym = parts[t]
+        dy0 = MIX * (yp[0] - ym[0])
+        dy1 = MIX * (yp[1] - ym[1])
+        mix_x = pltpu.roll(dy1, 128 - W, 1) - pltpu.roll(dy1, W, 1)
+        mix_y = pltpu.roll(dy0, 128 - W, 1) - pltpu.roll(dy0, W, 1)
+        rest = (
+            OWN * (xp[0] + xm[0]) + (yp[0] + ym[0]) + mix_x,
+            OWN * (yp[1] + ym[1]) + (xp[1] + xm[1]) + mix_y,
+            (xp[2] + xm[2]) + (yp[2] + ym[2]),
+        )
+        sums.append([rest[c] + beside_z[t][c] for c in range(3)])
+    return sums, [part[2] for part in parts], up_b, down_a
+
+
+def put_edges(edges, row, ups, downs):
+    last = lanes_of((8, 128)) % W == W - 1
+    for c in range(3):
+        edges[c, pl.ds(row, 8), :] = jnp.where(
+            last, pltpu.roll(ups[c], 127, 1), pltpu.roll(downs[c], 129 - W, 1)
+        )
+
+
+def tail_sweep(source, target, pq, edges=None, outer_only=False):
     for row in GROUPS:
+        kept = {}
         for low in (0, 2):
-            parts = [tail_parts(source, row, page) for page in (low, low + 1)]
-            (up_a, down_a), (up_b, down_b) = (part[:2] for part in parts)
-            for c in range(3):
-                if low == 0:
-                    edges[3 + c, pl.ds(row, 8), :] = down_a[c]
-                else:
-                    edges[c, pl.ds(row, 8), :] = up_b[c]
-            sums = (
-                [
-                    jnp.where(last, pltpu.roll(up_b[c], W - 1, 1), pltpu.roll(up_a[c], 127, 1))
-                    + pltpu.roll(down_a[c], 1, 1)
-                    for c in range(3)
-                ],
-                [
-                    jnp.where(first, pltpu.roll(down_a[c], 129 - W, 1), pltpu.roll(down_b[c], 1, 1))
-                    + pltpu.roll(up_b[c], 127, 1)
-                    for c in range(3)
-                ],
-            )
+            sums, v, up_b, down_a = tail_sums(source, row, low)
+            kept[low] = up_b, down_a
             for t in range(2):
                 if outer_only and low + t in (1, 2):
                     continue
-                _, _, v, xp, xm, yp, ym = parts[t]
-                dy0 = MIX * (yp[0] - ym[0])
-                dy1 = MIX * (yp[1] - ym[1])
-                mix_x = pltpu.roll(dy1, 128 - W, 1) - pltpu.roll(dy1, W, 1)
-                mix_y = pltpu.roll(dy0, 128 - W, 1) - pltpu.roll(dy0, W, 1)
-                rest = (
-                    OWN * (xp[0] + xm[0]) + (yp[0] + ym[0]) + mix_x,
-                    OWN * (yp[1] + ym[1]) + (xp[1] + xm[1]) + mix_y,
-                    (xp[2] + xm[2]) + (yp[2] + ym[2]),
-                )
                 q = pq[low + t, 3, pl.ds(row, 8), :]
                 for c in range(3):
                     p = pq[low + t, c, pl.ds(row, 8), :]
-                    target[low + t, c, pl.ds(row, 8), :] = (
-                        KEEP * v[c] + p + q * (rest[c] + sums[t][c])
-                    )
+                    target[low + t, c, pl.ds(row, 8), :] = KEEP * v[t][c] + p + q * sums[t][c]
+        if edges is not None:
+            put_edges(edges, row, kept[2][0], kept[0][1])
 
 
 def edges_only(source, edges):
     for row in OWN_GROUPS:
-        ups = tail_parts(source, row, 3)[0]
-        downs = tail_parts(source, row, 0)[1]
-        for c in range(3):
-            edges[c, pl.ds(row, 8), :] = ups[c]
-            edges[3 + c, pl.ds(row, 8), :] = downs[c]
+        put_edges(
+            edges, row, tail_parts(source, row, 3)[0], tail_parts(source, row, 0)[1]
+        )
 
 
 def neighbour_sum(ref, edges, i, row, lane):
@@ -152,12 +158,27 @@
     )
     sums = []
     for c in range(3):
-        high = pltpu.roll(edges[c, pl.ds(row, 8), :], 127 - W * i, 1)
-        low = pltpu.roll(edges[3 + c, pl.ds(row, 8), :], 129 - W - W * i, 1)
-        up = jnp.where(lane == 127, high, pltpu.roll(ups[c], 127, 1))
-        down = jnp.where(lane == 0, low, pltpu.roll(downs[c], 1, 1))
+        up, down = pltpu.roll(ups[c], 127, 1), pltpu.roll(downs[c], 1, 1)
+        if edges is not None:
+            edge = pltpu.roll(edges[c, pl.ds(row, 8), :], 128 - W * i, 1)
+            up = jnp.where(lane == 127, edge, up)
+            down = jnp.where(lane == 0, edge, down)
         sums.append(rest[c] + (up + down))
     return sums, v
+
+
+def planes(first, last, body, carry=0):
+    whole = first + (last - first) // 4 * 4
+
+    def four(k, carry):
+        for j in range(4):
+            carry = body(first + 4 * k + j, carry)
+        return carry
+
+    carry = lax.fori_loop(0, (last - first) // 4, four, carry)
+    for i in range(whole, last):
+        carry = body(i, carry)
+    return carry
 
 
 def sweep(source, target, pq, edges, first, last):
@@ -172,7 +193,7 @@
                 target[i, c, pl.ds(row, 8), :] = KEEP * v[c] + p + q * sums[c]
         return carry
 
-    lax.fori_loop(first, last, plane, 0, unroll=2)
+    planes(first, last, plane)
 
 
 def x_pack_kernel(load, damage, f_out, far_out, near_out, level, load_sem, level_sem):
@@ -244,7 +265,7 @@
             near_out[c, pl.ds(8 * k, 8), :] = near
 
 
-def main_kernel(f, xfar, xnear, yfar, ynear, pq):
+def main_kernel(f, xfar, xnear, yfar, ynear, pq, x2, columns):
     gx, gx_n, odd_x = position(GX)
     gy, gy_n, odd_y = position("gy")
     odd_x, odd_y = odd_x == 1, odd_y == 1
@@ -289,11 +310,35 @@
         return carry
 
     lax.fori_loop(0, NP // 2, beside_y, 0)
-
-
-def first_kernel(
-    pq, f, zfar_own, znear_own, zfar, znear, x2, tail, tail_pq, sums_out, edges
-):
+    sweep(pq, x2, pq, None, 1, NP - 1)
+    lane = lanes_of((8, 128))
+    row8 = rows_of((8, 128))
+
+    def residual(i, carry):
+        totals = list(carry)
+        for row in OWN_GROUPS:
+            sums, v = neighbour_sum(x2, None, i, row, lane)
+            rows = pl.ds(row - 8, 8)
+            g = stiffness_of(f[3, i - W, rows, :])
+            d = g * DIAG + MASS_TERM
+            for c in range(3):
+                load = f[c, i - W, rows, :]
+                totals[c] += (load - d * v[c]) + g * sums[c]
+                totals[4] += load * load
+            totals[3] += g
+        return tuple(totals)
+
+    zero = jnp.zeros((8, 128), F32)
+    totals = planes(W, W + 16, residual, (zero,) * 5)
+    stacked = zero
+    inner = (lane >= 2) & (lane < 126)
+    for c in range(5):
+        total = jnp.where(inner, totals[c], 0.0) if c < 3 else totals[c]
+        stacked = jnp.where(row8 == c, jnp.sum(total, axis=0, keepdims=True), stacked)
+    columns[...] = stacked
+
+
+def first_kernel(columns, zfar_own, znear_own, zfar, znear, tail, tail_pq, sums_out):
     lane = lanes_of((8, 128))
     row8 = rows_of((8, 128))
     gx, gx_n, _ = position(GX)
@@ -310,12 +355,15 @@
         (zfar_own, znear_own),
         (zfar, znear),
     )
+
+    def part(page, c, k):
+        when_odd, when_even = sides[page]
+        rows = pl.ds(8 * k, 8)
+        return pick(odd_z, when_odd[c, rows, :], when_even[c, rows, :])
+
     for page in range(4):
-        when_odd, when_even = sides[page]
         for k in range(3):
-            rows = pl.ds(8 * k, 8)
-            parts = [pick(odd_z, when_odd[c, rows, :], when_even[c, rows, :]) for c in range(4)]
-            g = stiffness_of(parts[3])
+            g = stiffness_of(part(page, 3, k))
             scale = RELAXATION / (g * DIAG + MASS_TERM)
             inside = x_in
             if page in (0, 3):
@@ -323,42 +371,45 @@
             if k == 2:
                 inside = inside & y_in
             for c in range(4):
-                value = jnp.where(inside, (parts[c] if c < 3 else g) * scale, 0.0)
+                value = jnp.where(inside, (part(page, c, k) if c < 3 else g) * scale, 0.0)
                 if k < 2:
                     tail_pq[page, c, pl.ds(8 + 8 * k, 8), :] = value
                 else:
                     tail_pq[page, c, pl.ds(4, 4), :] = value[:4]
                     tail_pq[page, c, pl.ds(24, 4), :] = value[4:]
-    tail_sweep(tail_pq, tail, tail_pq, edges)
-    sweep(pq, x2, pq, edges, 1, NP - 1)
-    edges_only(tail, edges)
-
-    def residual(i, carry):
-        totals = list(carry)
+    tail_sweep(tail_pq, tail, tail_pq)
+    zero = jnp.zeros((8, 128), F32)
+    ends = zero
+    for side in range(2):
+        page = 1 + side
+        here = (lane % W < 2) if side == 0 else (lane % W >= 2)
+        totals = [zero] * 3
         for row in OWN_GROUPS:
-            sums, v = neighbour_sum(x2, edges, i, row, lane)
-            rows = pl.ds(row - 8, 8)
-            g = stiffness_of(f[3, i - W, rows, :])
+            sums, v, _, _ = tail_sums(tail, row, 2 * side)
+            k = row // 8 - 1
+            g = stiffness_of(part(page, 3, k))
             d = g * DIAG + MASS_TERM
             for c in range(3):
-                load = f[c, i - W, rows, :]
-                totals[c] += (load - d * v[c]) + g * sums[c]
-                totals[4] += load * load
-            totals[3] += g
-        return tuple(totals)
-
-    zero = jnp.zeros((8, 128), F32)
-    totals = lax.fori_loop(W, W + 16, residual, (zero,) * 5, unroll=2)
-    stacked = zero
-    for c in range(5):
-        stacked = jnp.where(row8 == c, jnp.sum(totals[c], axis=0, keepdims=True), stacked)
+                totals[c] += (part(page, c, k) - d * v[1 - side][c]) + g * sums[1 - side][c]
+        for c in range(3):
+            total = jnp.sum(jnp.where(here, totals[c], 0.0), axis=0, keepdims=True)
+            ends = jnp.where(row8 == 3 * side + c, total, ends)
     big = (128, 128)
     gather = (rows_of(big) // BLOCK == lanes_of(big) % 8).astype(F32)
-    by_cell = jnp.dot(
-        stacked, gather, precision=lax.Precision.HIGHEST, preferred_element_type=F32
-    )
-    slot = jnp.sum(jnp.where(lane // 8 == row8, by_cell, 0.0), axis=0, keepdims=True)
-    sums_out[...] = jnp.broadcast_to(slot, sums_out.shape)
+    own = ((rows_of(big) >= W * W) & (rows_of(big) < W * (W + 16))).astype(F32)
+
+    def dot(a, b):
+        return jnp.dot(a, b, precision=lax.Precision.HIGHEST, preferred_element_type=F32)
+
+    ends = jnp.where((lane >= W * W) & (lane < W * (W + 16)), ends, 0.0)
+    by_cell = dot(columns[...], gather)
+    by_end = dot(ends, own)
+    low_end = (lane % 8 == 0) & (lane // 8 == row8) & (row8 < 3)
+    high_end = (lane % 8 == 7) & (lane // 8 + 3 == row8) & (row8 < 6)
+    slot = jnp.where(lane // 8 == row8, by_cell, 0.0) + jnp.where(
+        low_end | high_end, by_end, 0.0
+    )
+    sums_out[...] = jnp.broadcast_to(jnp.sum(slot, axis=0, keepdims=True), sums_out.shape)
 
 
 def coarse_solve(load, mean, gx_n, gy_n, gz_n):
@@ -469,18 +520,26 @@
                 inside = tail_pq[page, 3, rows, :] > 0.0
                 tail3[page, c, rows, :] = tail2[page, c, rows, :] + jnp.where(inside, value, 0.0)
 
+    ends = (lane == 0) | (lane == 127)
+    for row in GROUPS:
+        for c in range(3):
+            rows = pl.ds(row, 8)
+            edges[c, rows, :] = jnp.where(
+                lane % W == W - 1, pltpu.roll(tail3[2, c, rows, :], 128 - W, 1), tail3[1, c, rows, :]
+            )
+
     def correct(i, carry):
-        cell = (i >= W).astype(jnp.int32) + (i >= W + 16).astype(jnp.int32)
+        cell = (i >= W) * 1 + (i >= W + 16) * 1
         for row in GROUPS:
             rows = pl.ds(row, 8)
             inside = pq[i, 3, rows, :] > 0.0
             for c in range(3):
-                x3[i, c, rows, :] = x2[i, c, rows, :] + jnp.where(
-                    inside, w_ref[cell, c, rows, :], 0.0
-                )
+                edge = pltpu.roll(edges[c, rows, :], 128 - W * i, 1)
+                value = x2[i, c, rows, :] + jnp.where(inside, w_ref[cell, c, rows, :], 0.0)
+                x3[i, c, rows, :] = jnp.where(ends, edge, value)
         return carry
 
-    lax.fori_loop(1, NP - 1, correct, 0)
+    planes(1, NP - 1, correct)
     tail_sweep(tail3, tail4, tail_pq, edges)
     sweep(x3, x4, pq, edges, 2, NP - 2)
     tail_sweep(tail4, tail3, tail_pq, edges, True)
@@ -508,7 +567,7 @@
                 total += r * r
         return total
 
-    total = jnp.sum(lax.fori_loop(W, W + 16, residual, jnp.zeros((8, 128), F32), unroll=2))
+    total = jnp.sum(planes(W, W + 16, residual, jnp.zeros((8, 128), F32)))
     both = jnp.where(line == 0, load_sum * (1.0 / n), total)
     sum_out[...] = jnp.broadcast_to(both, sum_out.shape)
     for copy in copies:
@@ -570,14 +629,10 @@
     z_pieces = swaps(*z_sends, GZ)
     field = (NP, 4, ROWS, 128)
     tails = (4, 4, ROWS, 128)
-    edges = (6, ROWS, 128)
-    (pq,) = call(main_kernel, (field,), pieces, 8)
-    x2, tail, tail_pq, sums = call(
-        first_kernel,
-        (field, tails, tails, (n, 128)),
-        (pq, f, *z_sends, *z_pieces),
-        12,
-        (edges,),
+    edges = (3, ROWS, 128)
+    pq, x2, columns = call(main_kernel, (field, field, (8, 128)), pieces, 12)
+    tail, tail_pq, sums = call(
+        first_kernel, (tails, tails, (n, 128)), (columns, *z_sends, *z_pieces), 8
     )
     every = lax.all_to_all(sums, ALL, 0, 0, tiled=True)
     displacement, partial_sums = call(

time: 81 us -> 77.2 us (0.953)
  Pallas kernels: 13.4 us -> 11 us
  waiting for transfers between devices: 7.77 us -> 6.36 us
    pallas_call x7, Pallas kernels: 13.4 us -> 11 us  [call(): pl.pallas_call(kernel, out_shape=tuple(shapes), in_specs=[source] * len(a...]
    ppermute x3, waiting for transfers between devices: 4.44 us -> 3.25 us  [swaps(): lax.ppermute(far_send, axis, far)]
  transfers between devices with their start and end apart: 6 -> 6, of which waited for: 5 -> 4; matrix products, arithmetic and copies ran while one was open for 0% -> 0% of each run, Pallas kernels for 1% -> 3%
where the time goes in v3:
time: 77.2 us; the launch traced here: 77 us
  blocking collectives  45.8 us (59%)
  starting transfers between devices  13.2 us (17%)
  Pallas kernels  11 us (14%)
  waiting for transfers between devices  6.36 us (8%)
    all_to_all x1, blocking collectives, on_device(): every = lax.all_to_all(sums, ALL, 0, 0, tiled=True)  27.5 us
    all_to_all x1, blocking collectives, on_device(): partial_sums = lax.all_to_all(partial_sums, ALL, 0, 0, tiled=True)  18.3 us
    pallas_call x7, Pallas kernels, call(): pl.pallas_call(kernel, out_shape=tuple(shapes), in_specs=[source] * len(a...  11 us
    ppermute x3, starting transfers between devices, swaps(): lax.ppermute(far_send, axis, far)  10.3 us
    ppermute x3, waiting for transfers between devices, swaps(): lax.ppermute(far_send, axis, far)  3.25 us
    ppermute x3, waiting for transfers between devices, swaps(): lax.ppermute(near_send, axis, near)  3.11 us
    ppermute x3, starting transfers between devices, swaps(): lax.ppermute(near_send, axis, near)  2.87 us
  transfers between devices with their start and end apart: 6, of which 4 were waited for; matrix products, arithmetic and copies ran while one was open for 0% of the time, Pallas kernels for 3%

profile of v3, /device:TPU:1, one launch (start us, length us, event | category | flops | bytes accessed | tf_op | source)
XLA Modules:
  0.0 77.0 jit_solution(5348477650130452399)
XLA Ops:
  0.6 1.1 %shard_map.41 = (f32[4,16,16,128]{3,2,1,0:T(8,128)S(1)}, f32[4,4,16,128]{3,2,1,0:T(8,128)S(1)}, f32[4,4,16,128]{3,2,1,0:T(8,128)S(1)}) custom-call(f32[3,16,16,128]{3,2,1,0:T(8,128)} %load.1, s32[16,16,128]{2,1,0:T(8,128)} %damage.1), custom_call_target="tpu_custom_call" | custom-call | tf_op jit(solution)/shard_map/pallas_call | solution.py:591
  1.7 4.5 %collective-permute-start = (f32[4,4,16,128]{3,2,1,0:T(8,128)S(1)}, f32[4,4,16,128]{3,2,1,0:T(8,128)S(1)}, u32[]{:S(2)}, u32[]{:S(2)}) collective-permute-start(f32[4,4,16,128]{3,2,1,0:T(8,128)S(1)} %get-tuple-element.18), channel_id=1, source_target_pairs={{0,224},{32,64},{64,32},{96,128},{128,96},{160,192},{192,160},{224... | collective-permute-start | bytes 393224 | tf_op jit(solution)/shard_map/ppermute | solution.py:581
  6.2 2.9 %collective-permute-start.1 = (f32[4,4,16,128]{3,2,1,0:T(8,128)S(1)}, f32[4,4,16,128]{3,2,1,0:T(8,128)S(1)}, u32[]{:S(2)}, u32[]{:S(2)}) collective-permute-start(f32[4,4,16,128]{3,2,1,0:T(8,128)S(1)} %get-tuple-element.19), channel_id=1, source_target_pairs={{0,32},{32,0},{64,96},{96,64},{128,160},{160,128},{192,224},{224,1... | collective-permute-start | bytes 393224 | tf_op jit(solution)/shard_map/ppermute | solution.py:581
  9.0 0.0 collective-permute-done.xfar
  9.0 1.0 %collective-permute-done.1.xnear = f32[4,4,16,128]{3,2,1,0:T(8,128)S(1)} collective-permute-done((f32[4,4,16,128]{3,2,1,0:T(8,128)S(1)}, f32[4,4,16,128]{3,2,1,0:T(8,128)S(1)}, u32[]{:S(2)}, u32[]{:S(2)}) %collective-permute-start.1) | collective-permute-done | bytes 131104 | tf_op jit(solution)/shard_map/ppermute | solution.py:581
  10.0 0.1 shard_map.42
  10.1 2.6 %collective-permute-start.2 = (f32[4,12,8,128]{3,2,1,0:T(8,128)S(1)}, f32[4,12,8,128]{3,2,1,0:T(8,128)S(1)}, u32[]{:S(2)}, u32[]{:S(2)}) collective-permute-start(f32[4,12,8,128]{3,2,1,0:T(8,128)S(1)} %get-tuple-element.20), channel_id=1, source_target_pairs={{0,24},{8,16},{16,8},{24,0},{1,25},{9,17},{17,9},{25,1},{2,26},{10... | collective-permute-start | bytes 589832 | tf_op jit(solution)/shard_map/ppermute | solution.py:581
  12.6 0.0 collective-permute-start.3
  12.7 3.2 %collective-permute-done.2.yfar = f32[4,12,8,128]{3,2,1,0:T(8,128)S(1)} collective-permute-done((f32[4,12,8,128]{3,2,1,0:T(8,128)S(1)}, f32[4,12,8,128]{3,2,1,0:T(8,128)S(1)}, u32[]{:S(2)}, u32[]{:S(2)}) %collective-permute-start.2) | collective-permute-done | bytes 196640 | tf_op jit(solution)/shard_map/ppermute | solution.py:581
  15.9 1.3 %collective-permute-done.3.ynear = f32[4,12,8,128]{3,2,1,0:T(8,128)S(1)} collective-permute-done((f32[4,12,8,128]{3,2,1,0:T(8,128)S(1)}, f32[4,12,8,128]{3,2,1,0:T(8,128)S(1)}, u32[]{:S(2)}, u32[]{:S(2)}) %collective-permute-start.3) | collective-permute-done | bytes 196640 | tf_op jit(solution)/shard_map/ppermute | solution.py:581
  17.2 0.7 shard_map.44
  17.9 3.3 %collective-permute-start.4 = (f32[4,24,128]{2,1,0:T(8,128)S(1)}, f32[4,24,128]{2,1,0:T(8,128)S(1)}, u32[]{:S(2)}, u32[]{:S(2)}) collective-permute-start(f32[4,24,128]{2,1,0:T(8,128)S(1)} %get-tuple-element.23.zfar_own), channel_id=1, source_target_pairs={{0,7},{1,2},{2,1},{3,4},{4,3},{5,6},{6,5},{7,0},{8,15},{9,10},{10,... | collective-permute-start | bytes 147464 | tf_op jit(solution)/shard_map/ppermute | solution.py:581
  21.1 0.0 collective-permute-start.5
  21.2 2.1 %shard_map.43 = (f32[24,4,40,128]{3,2,1,0:T(8,128)S(1)}, f32[24,4,40,128]{3,2,1,0:T(8,128)S(1)}, f32[8,128]{1,0:T(8,128)S(1)}) custom-call(f32[4,16,16,128]{3,2,1,0:T(8,128)S(1)} %get-tuple-element.17.f, f32[4,4,16,128]{3,2,1,0:T(8,128)S(1)} %collective-permute-done.xfar, f32[4,4,16,128]{3,2,1,0:T(8,128)S(1)} %collective-permute-done.1.xnear, ...), custom_call_target="tpu_custom_call" | custom-call | tf_op jit(solution)/shard_map/pallas_call | solution.py:591
  23.2 0.0 collective-permute-done.4.zfar
  23.2 0.9 %collective-permute-done.5.znear = f32[4,24,128]{2,1,0:T(8,128)S(1)} collective-permute-done((f32[4,24,128]{2,1,0:T(8,128)S(1)}, f32[4,24,128]{2,1,0:T(8,128)S(1)}, u32[]{:S(2)}, u32[]{:S(2)}) %collective-permute-start.5) | collective-permute-done | bytes 49184 | tf_op jit(solution)/shard_map/ppermute | solution.py:581
  24.1 0.7 shard_map.45
  24.8 27.5 %all_to_all.22 = f32[256,1,128]{2,1,0:T(1,128)S(1)} all-to-all(f32[256,1,128]{2,1,0:T(1,128)S(1)} %bitcast.10), channel_id=1, replica_groups=mesh['gx_0'=4,'gx_1'=2,'gy'=4,'gz_0'=2,'gz_1'=4] {'gx_0','gx_1','gy','gz..., dimensions={0} | all-to-all | bytes 262144 | tf_op jit(solution)/shard_map/all_to_all | solution.py:637
  52.3 5.8 %shard_map.46 = (f32[3,16,16,128]{3,2,1,0:T(8,128)}, f32[256,128]{1,0:T(8,128)S(1)}) custom-call(f32[256,128]{1,0:T(8,128)S(1)} %bitcast.8, f32[24,4,40,128]{3,2,1,0:T(8,128)S(1)} %get-tuple-element.26.x2, f32[4,4,40,128]{3,2,1,0:T(8,128)S(1)} %get-tuple-element.27.tail2, f32[24,4,40,128]{3,2,1,0:T(8,128)S(1)} %get-tuple-element.28.pq, ...), custom_call_target="tpu_custom_call" | custom-call | tf_op jit(solution)/shard_map/pallas_call | solution.py:591
  58.1 18.3 %all_to_all.23 = f32[256,1,128]{2,1,0:T(1,128)S(1)} all-to-all(f32[256,1,128]{2,1,0:T(1,128)S(1)} %bitcast.11), channel_id=1, replica_groups=mesh['gx_0'=4,'gx_1'=2,'gy'=4,'gz_0'=2,'gz_1'=4] {'gx_0','gx_1','gy','gz..., dimensions={0} | all-to-all | bytes 262144 | tf_op jit(solution)/shard_map/all_to_all | solution.py:646
  76.4 0.7 shard_map.47
Async XLA Ops:
  1.7 7.3 %collective-permute-start = (f32[4,4,16,128]{3,2,1,0:T(8,128)S(1)}, f32[4,4,16,128]{3,2,1,0:T(8,128)S(1)}, u32[]{:S(2)}, u32[]{:S(2)}) collective-permute-start(f32[4,4,16,128]{3,2,1,0:T(8,128)S(1)} %get-tuple-element.18), channel_id=1, source_target_pairs={{0,224},{32,64},{64,32},{96,128},{128,96},{160,192},{192,160},{224... | collective-permute-start | bytes 393224 | tf_op jit(solution)/shard_map/ppermute | solution.py:581
  6.2 3.9 %collective-permute-start.1 = (f32[4,4,16,128]{3,2,1,0:T(8,128)S(1)}, f32[4,4,16,128]{3,2,1,0:T(8,128)S(1)}, u32[]{:S(2)}, u32[]{:S(2)}) collective-permute-start(f32[4,4,16,128]{3,2,1,0:T(8,128)S(1)} %get-tuple-element.19), channel_id=1, source_target_pairs={{0,32},{32,0},{64,96},{96,64},{128,160},{160,128},{192,224},{224,1... | collective-permute-start | bytes 393224 | tf_op jit(solution)/shard_map/ppermute | solution.py:581
  10.1 5.8 %collective-permute-start.2 = (f32[4,12,8,128]{3,2,1,0:T(8,128)S(1)}, f32[4,12,8,128]{3,2,1,0:T(8,128)S(1)}, u32[]{:S(2)}, u32[]{:S(2)}) collective-permute-start(f32[4,12,8,128]{3,2,1,0:T(8,128)S(1)} %get-tuple-element.20), channel_id=1, source_target_pairs={{0,24},{8,16},{16,8},{24,0},{1,25},{9,17},{17,9},{25,1},{2,26},{10... | collective-permute-start | bytes 589832 | tf_op jit(solution)/shard_map/ppermute | solution.py:581
  12.6 4.5 %collective-permute-start.3 = (f32[4,12,8,128]{3,2,1,0:T(8,128)S(1)}, f32[4,12,8,128]{3,2,1,0:T(8,128)S(1)}, u32[]{:S(2)}, u32[]{:S(2)}) collective-permute-start(f32[4,12,8,128]{3,2,1,0:T(8,128)S(1)} %get-tuple-element.21), channel_id=1, source_target_pairs={{0,8},{8,0},{16,24},{24,16},{1,9},{9,1},{17,25},{25,17},{2,10},{10... | collective-permute-start | bytes 589832 | tf_op jit(solution)/shard_map/ppermute | solution.py:581
  17.9 5.4 %collective-permute-start.4 = (f32[4,24,128]{2,1,0:T(8,128)S(1)}, f32[4,24,128]{2,1,0:T(8,128)S(1)}, u32[]{:S(2)}, u32[]{:S(2)}) collective-permute-start(f32[4,24,128]{2,1,0:T(8,128)S(1)} %get-tuple-element.23.zfar_own), channel_id=1, source_target_pairs={{0,7},{1,2},{2,1},{3,4},{4,3},{5,6},{6,5},{7,0},{8,15},{9,10},{10,... | collective-permute-start | bytes 147464 | tf_op jit(solution)/shard_map/ppermute | solution.py:581
  21.1 2.9 %collective-permute-start.5 = (f32[4,24,128]{2,1,0:T(8,128)S(1)}, f32[4,24,128]{2,1,0:T(8,128)S(1)}, u32[]{:S(2)}, u32[]{:S(2)}) collective-permute-start(f32[4,24,128]{2,1,0:T(8,128)S(1)} %get-tuple-element.24.znear_own), channel_id=1, source_target_pairs={{0,1},{1,0},{2,3},{3,2},{4,5},{5,4},{6,7},{7,6},{8,9},{9,8},{10,11... | collective-permute-start | bytes 147464 | tf_op jit(solution)/shard_map/ppermute | solution.py:581

commit v4 on v3

--- a/solution.py
+++ b/solution.py
@@ -233,39 +233,54 @@
             near_out[c, j] = pick(odd_y, low, high)
 
 
-def z_pack_kernel(f, xfar, xnear, yfar, ynear, far_out, near_out):
-    odd_x, odd_y, odd_z = position(GX)[2] == 1, position("gy")[2] == 1, position(GZ)[2]
+def put_z_pack(values, rows, odd_z, far_out, near_out):
     lane = lanes_of((8, 128))
+    for c in range(4):
+        far = jnp.zeros((8, 128), F32)
+        near = far
+        for i in range(NP):
+            value = values(c, i)
+            here = (lane >= W * i) & (lane < W * i + W)
+            far = jnp.where(here, pltpu.roll(value, W * i + W * odd_z, 1), far)
+            near = jnp.where(here, pltpu.roll(value, W * i + W * (1 - odd_z), 1), near)
+        far_out[c, rows, :] = far
+        near_out[c, rows, :] = near
+
+
+def z_pack_own_kernel(f, xfar, xnear, far_out, near_out):
+    odd_x = position(GX)[2] == 1
+    for k in range(2):
+        rows = pl.ds(8 * k, 8)
+
+        def values(c, i):
+            if i < W:
+                return pick(odd_x, xnear[c, i, rows, :], xfar[c, i, rows, :])
+            if i >= W + 16:
+                j = i - W - 16
+                return pick(odd_x, xfar[c, j, rows, :], xnear[c, j, rows, :])
+            return f[c, i - W, rows, :]
+
+        put_z_pack(values, rows, position(GZ)[2], far_out, near_out)
+
+
+def z_pack_kernel(yfar, ynear, far_own, near_own, far_out, near_out):
+    odd_y = position("gy")[2] == 1
     upper = rows_of((8, 128)) < 4
     for c in range(4):
-        for k in range(3):
-            far = jnp.zeros((8, 128), F32)
-            near = far
-            for i in range(NP):
-                if k == 2:
-                    low = pick(odd_y, ynear[c, i // 2], yfar[c, i // 2])
-                    high = pick(odd_y, yfar[c, i // 2], ynear[c, i // 2])
-                    if i % 2:
-                        value = jnp.where(upper, pltpu.roll(low, 4, 0), high)
-                    else:
-                        value = jnp.where(upper, low, pltpu.roll(high, 4, 0))
-                else:
-                    rows = pl.ds(8 * k, 8)
-                    if i < W:
-                        value = pick(odd_x, xnear[c, i, rows, :], xfar[c, i, rows, :])
-                    elif i >= W + 16:
-                        j = i - W - 16
-                        value = pick(odd_x, xfar[c, j, rows, :], xnear[c, j, rows, :])
-                    else:
-                        value = f[c, i - W, rows, :]
-                here = (lane >= W * i) & (lane < W * i + W)
-                far = jnp.where(here, pltpu.roll(value, W * i + W * odd_z, 1), far)
-                near = jnp.where(here, pltpu.roll(value, W * i + W * (1 - odd_z), 1), near)
-            far_out[c, pl.ds(8 * k, 8), :] = far
-            near_out[c, pl.ds(8 * k, 8), :] = near
-
-
-def main_kernel(f, xfar, xnear, yfar, ynear, pq, x2, columns):
+        far_out[c, pl.ds(0, 16), :] = far_own[c]
+        near_out[c, pl.ds(0, 16), :] = near_own[c]
+
+    def values(c, i):
+        low = pick(odd_y, ynear[c, i // 2], yfar[c, i // 2])
+        high = pick(odd_y, yfar[c, i // 2], ynear[c, i // 2])
+        if i % 2:
+            return jnp.where(upper, pltpu.roll(low, 4, 0), high)
+        return jnp.where(upper, low, pltpu.roll(high, 4, 0))
+
+    put_z_pack(values, pl.ds(16, 8), position(GZ)[2], far_out, near_out)
+
+
+def main_kernel(f, xfar, xnear, yfar, ynear, pq, y3, columns, x2):
     gx, gx_n, odd_x = position(GX)
     gy, gy_n, odd_y = position("gy")
     odd_x, odd_y = odd_x == 1, odd_y == 1
@@ -336,6 +351,7 @@
         total = jnp.where(inner, totals[c], 0.0) if c < 3 else totals[c]
         stacked = jnp.where(row8 == c, jnp.sum(total, axis=0, keepdims=True), stacked)
     columns[...] = stacked
+    sweep(x2, y3, pq, None, 2, NP - 2)
 
 
 def first_kernel(columns, zfar_own, znear_own, zfar, znear, tail, tail_pq, sums_out):
@@ -461,7 +477,7 @@
 
 def second_kernel(
     every,
-    x2,
+    y3,
     tail2,
     pq,
     tail_pq,
@@ -473,6 +489,7 @@
     tail3,
     tail4,
     w_ref,
+    n_ref,
     edges,
     out_sem,
 ):
@@ -493,6 +510,8 @@
     line = lane[:1]
     cell_of = ((7, -1), (0, 0), (7, 0), (0, 1))
     spans = ((4, 4), (8, 16), (24, 4))
+    x_cell_in = (gx > 0, True, gx < gx_n - 1)
+    y_cell_in = (gy > 0, True, gy < gy_n - 1)
     for c in range(3):
         turned = pltpu.roll(w[c], (centre + n - me) % n, 1)
 
@@ -504,7 +523,9 @@
             for dx in range(3):
                 j = column(dx, dy)
                 main = jnp.sum(turned[:, j : j + 1] * own_cells, axis=0, keepdims=True)
-                w_ref[dx, c, pl.ds(first, size), :] = jnp.broadcast_to(main, (size, 128))
+                main = jnp.where(x_cell_in[dx] & y_cell_in[dy], main, 0.0)
+                for k in range(3 * dx, 3 * dx + 3):
+                    w_ref[k, c, pl.ds(first, size), :] = jnp.broadcast_to(main, (size, 128))
             for page in range(4):
                 k, dz = cell_of[page]
                 here = [
@@ -520,28 +541,32 @@
                 inside = tail_pq[page, 3, rows, :] > 0.0
                 tail3[page, c, rows, :] = tail2[page, c, rows, :] + jnp.where(inside, value, 0.0)
 
-    ends = (lane == 0) | (lane == 127)
+    tail_sweep(tail3, tail4, tail_pq)
+    for k in range(1, 8):
+        for row in GROUPS:
+            sums, _ = neighbour_sum(w_ref, None, k, row, lane)
+            for c in range(3):
+                n_ref[k, c, pl.ds(row, 8), :] = sums[c]
+    ends = (lane < 2) | (lane >= 126)
     for row in GROUPS:
         for c in range(3):
             rows = pl.ds(row, 8)
             edges[c, rows, :] = jnp.where(
-                lane % W == W - 1, pltpu.roll(tail3[2, c, rows, :], 128 - W, 1), tail3[1, c, rows, :]
+                lane % W < 2, tail4[1, c, rows, :], pltpu.roll(tail4[2, c, rows, :], 128 - W, 1)
             )
 
     def correct(i, carry):
-        cell = (i >= W) * 1 + (i >= W + 16) * 1
+        k = jnp.minimum(i - 1, W) + jnp.maximum(i - W - 14, 0)
         for row in GROUPS:
             rows = pl.ds(row, 8)
-            inside = pq[i, 3, rows, :] > 0.0
+            q = pq[i, 3, rows, :]
             for c in range(3):
                 edge = pltpu.roll(edges[c, rows, :], 128 - W * i, 1)
-                value = x2[i, c, rows, :] + jnp.where(inside, w_ref[cell, c, rows, :], 0.0)
-                x3[i, c, rows, :] = jnp.where(ends, edge, value)
+                value = y3[i, c, rows, :] + KEEP * w_ref[k, c, rows, :] + q * n_ref[k, c, rows, :]
+                x4[i, c, rows, :] = jnp.where(ends, edge, value)
         return carry
 
-    planes(1, NP - 1, correct)
-    tail_sweep(tail3, tail4, tail_pq, edges)
-    sweep(x3, x4, pq, edges, 2, NP - 2)
+    planes(2, NP - 2, correct)
     tail_sweep(tail4, tail3, tail_pq, edges, True)
     sweep(x4, x3, pq, edges, 3, NP - 3)
     copies = [
@@ -625,12 +650,14 @@
     y_pieces = swaps(*y_sends, "gy")
     pieces = (f, *x_pieces, *y_pieces)
     side = (4, NP, 128)
-    z_sends = call(z_pack_kernel, (side, side), pieces, 8)
+    own_side = (4, 16, 128)
+    own_sends = call(z_pack_own_kernel, (own_side, own_side), (f, *x_pieces), 8)
+    z_sends = call(z_pack_kernel, (side, side), (*y_pieces, *own_sends), 8)
     z_pieces = swaps(*z_sends, GZ)
     field = (NP, 4, ROWS, 128)
     tails = (4, 4, ROWS, 128)
     edges = (3, ROWS, 128)
-    pq, x2, columns = call(main_kernel, (field, field, (8, 128)), pieces, 12)
+    pq, y3, columns = call(main_kernel, (field, field, (8, 128)), pieces, 12, (field,))
     tail, tail_pq, sums = call(
         first_kernel, (tails, tails, (n, 128)), (columns, *z_sends, *z_pieces), 8
     )
@@ -638,9 +665,13 @@
     displacement, partial_sums = call(
         second_kernel,
         (right_side.shape, (n, 128)),
-        (every, x2, tail, pq, tail_pq, f),
+        (every, y3, tail, pq, tail_pq, f),
         20,
-        (field, field, tails, tails, (3, 3, ROWS, 128), edges, pltpu.SemaphoreType.DMA((3,))),
+        (
+            *(field, field, tails, tails),
+            *((9, 4, ROWS, 128), (9, 4, ROWS, 128), edges),
+            pltpu.SemaphoreType.DMA((3,)),
+        ),
         target=(HBM, VMEM),
     )
     partial_sums = lax.all_to_all(partial_sums, ALL, 0, 0, tiled=True)

time: 77.2 us -> 76 us (0.984)
  waiting for transfers between devices: 6.36 us -> 5.12 us
    pallas_call x7 -> x8, Pallas kernels: 11 us -> 11 us  [call(): pl.pallas_call(kernel, out_shape=tuple(shapes), in_specs=[source] * len(a...]
  transfers between devices with their start and end apart: 6 -> 6, of which waited for: 4 -> 4; matrix products, arithmetic and copies ran while one was open for 0% -> 0% of each run, Pallas kernels for 3% -> 4%
where the time goes in v4:
time: 76 us; the launch traced here: 75.8 us
  blocking collectives  45.8 us (60%)
  starting transfers between devices  13.2 us (17%)
  Pallas kernels  11 us (14%)
  waiting for transfers between devices  5.12 us (7%)
    all_to_all x1, blocking collectives, on_device(): every = lax.all_to_all(sums, ALL, 0, 0, tiled=True)  27.5 us
    all_to_all x1, blocking collectives, on_device(): partial_sums = lax.all_to_all(partial_sums, ALL, 0, 0, tiled=True)  18.3 us
    pallas_call x8, Pallas kernels, call(): pl.pallas_call(kernel, out_shape=tuple(shapes), in_specs=[source] * len(a...  11 us
    ppermute x3, starting transfers between devices, swaps(): lax.ppermute(far_send, axis, far)  10.3 us
    ppermute x3, starting transfers between devices, swaps(): lax.ppermute(near_send, axis, near)  2.87 us
    ppermute x3, waiting for transfers between devices, swaps(): lax.ppermute(far_send, axis, far)  2.76 us
    ppermute x3, waiting for transfers between devices, swaps(): lax.ppermute(near_send, axis, near)  2.36 us
  transfers between devices with their start and end apart: 6, of which 4 were waited for; matrix products, arithmetic and copies ran while one was open for 0% of the time, Pallas kernels for 4%

profile of v4, /device:TPU:1, one launch (start us, length us, event | category | flops | bytes accessed | tf_op | source)
XLA Modules:
  0.0 75.8 jit_solution(8720441605867079764)
XLA Ops:
  0.6 1.1 %shard_map.41 = (f32[4,16,16,128]{3,2,1,0:T(8,128)S(1)}, f32[4,4,16,128]{3,2,1,0:T(8,128)S(1)}, f32[4,4,16,128]{3,2,1,0:T(8,128)S(1)}) custom-call(f32[3,16,16,128]{3,2,1,0:T(8,128)} %load.1, s32[16,16,128]{2,1,0:T(8,128)} %damage.1), custom_call_target="tpu_custom_call" | custom-call | tf_op jit(solution)/shard_map/pallas_call | solution.py:616
  1.7 4.5 %collective-permute-start = (f32[4,4,16,128]{3,2,1,0:T(8,128)S(1)}, f32[4,4,16,128]{3,2,1,0:T(8,128)S(1)}, u32[]{:S(2)}, u32[]{:S(2)}) collective-permute-start(f32[4,4,16,128]{3,2,1,0:T(8,128)S(1)} %get-tuple-element.20), channel_id=1, source_target_pairs={{0,224},{32,64},{64,32},{96,128},{128,96},{160,192},{192,160},{224... | collective-permute-start | bytes 393224 | tf_op jit(solution)/shard_map/ppermute | solution.py:606
  6.2 2.9 %collective-permute-start.1 = (f32[4,4,16,128]{3,2,1,0:T(8,128)S(1)}, f32[4,4,16,128]{3,2,1,0:T(8,128)S(1)}, u32[]{:S(2)}, u32[]{:S(2)}) collective-permute-start(f32[4,4,16,128]{3,2,1,0:T(8,128)S(1)} %get-tuple-element.21), channel_id=1, source_target_pairs={{0,32},{32,0},{64,96},{96,64},{128,160},{160,128},{192,224},{224,1... | collective-permute-start | bytes 393224 | tf_op jit(solution)/shard_map/ppermute | solution.py:606
  9.0 0.0 collective-permute-done.xfar
  9.0 1.0 %collective-permute-done.1.xnear = f32[4,4,16,128]{3,2,1,0:T(8,128)S(1)} collective-permute-done((f32[4,4,16,128]{3,2,1,0:T(8,128)S(1)}, f32[4,4,16,128]{3,2,1,0:T(8,128)S(1)}, u32[]{:S(2)}, u32[]{:S(2)}) %collective-permute-start.1) | collective-permute-done | bytes 131104 | tf_op jit(solution)/shard_map/ppermute | solution.py:606
  10.0 0.1 shard_map.42
  10.1 2.6 %collective-permute-start.2 = (f32[4,12,8,128]{3,2,1,0:T(8,128)S(1)}, f32[4,12,8,128]{3,2,1,0:T(8,128)S(1)}, u32[]{:S(2)}, u32[]{:S(2)}) collective-permute-start(f32[4,12,8,128]{3,2,1,0:T(8,128)S(1)} %get-tuple-element.22), channel_id=1, source_target_pairs={{0,24},{8,16},{16,8},{24,0},{1,25},{9,17},{17,9},{25,1},{2,26},{10... | collective-permute-start | bytes 589832 | tf_op jit(solution)/shard_map/ppermute | solution.py:606
  12.6 0.0 collective-permute-start.3
  12.7 0.5 shard_map.44
  13.1 2.8 %collective-permute-done.2.yfar = f32[4,12,8,128]{3,2,1,0:T(8,128)S(1)} collective-permute-done((f32[4,12,8,128]{3,2,1,0:T(8,128)S(1)}, f32[4,12,8,128]{3,2,1,0:T(8,128)S(1)}, u32[]{:S(2)}, u32[]{:S(2)}) %collective-permute-start.2) | collective-permute-done | bytes 196640 | tf_op jit(solution)/shard_map/ppermute | solution.py:606
  15.9 1.3 %collective-permute-done.3.ynear = f32[4,12,8,128]{3,2,1,0:T(8,128)S(1)} collective-permute-done((f32[4,12,8,128]{3,2,1,0:T(8,128)S(1)}, f32[4,12,8,128]{3,2,1,0:T(8,128)S(1)}, u32[]{:S(2)}, u32[]{:S(2)}) %collective-permute-start.3) | collective-permute-done | bytes 196640 | tf_op jit(solution)/shard_map/ppermute | solution.py:606
  17.2 0.3 shard_map.45
  17.4 3.3 %collective-permute-start.4 = (f32[4,24,128]{2,1,0:T(8,128)S(1)}, f32[4,24,128]{2,1,0:T(8,128)S(1)}, u32[]{:S(2)}, u32[]{:S(2)}) collective-permute-start(f32[4,24,128]{2,1,0:T(8,128)S(1)} %get-tuple-element.27.zfar_own), channel_id=1, source_target_pairs={{0,7},{1,2},{2,1},{3,4},{4,3},{5,6},{6,5},{7,0},{8,15},{9,10},{10,... | collective-permute-start | bytes 147464 | tf_op jit(solution)/shard_map/ppermute | solution.py:606
  20.7 0.0 collective-permute-start.5
  20.7 2.8 %shard_map.43 = (f32[24,4,40,128]{3,2,1,0:T(8,128)S(1)}, f32[24,4,40,128]{3,2,1,0:T(8,128)S(1)}, f32[8,128]{1,0:T(8,128)S(1)}) custom-call(f32[4,16,16,128]{3,2,1,0:T(8,128)S(1)} %get-tuple-element.19.f, f32[4,4,16,128]{3,2,1,0:T(8,128)S(1)} %collective-permute-done.xfar, f32[4,4,16,128]{3,2,1,0:T(8,128)S(1)} %collective-permute-done.1.xnear, ...), custom_call_target="tpu_custom_call" | custom-call | tf_op jit(solution)/shard_map/pallas_call | solution.py:616
  23.5 0.0 collective-permute-done.4.zfar
  23.6 0.1 collective-permute-done.5.znear
  23.7 0.7 shard_map.46
  24.4 27.5 %all_to_all.22 = f32[256,1,128]{2,1,0:T(1,128)S(1)} all-to-all(f32[256,1,128]{2,1,0:T(1,128)S(1)} %bitcast.10), channel_id=1, replica_groups=mesh['gx_0'=4,'gx_1'=2,'gy'=4,'gz_0'=2,'gz_1'=4] {'gx_0','gx_1','gy','gz..., dimensions={0} | all-to-all | bytes 262144 | tf_op jit(solution)/shard_map/all_to_all | solution.py:664
  51.9 5.0 %shard_map.47 = (f32[3,16,16,128]{3,2,1,0:T(8,128)}, f32[256,128]{1,0:T(8,128)S(1)}) custom-call(f32[256,128]{1,0:T(8,128)S(1)} %bitcast.8, f32[24,4,40,128]{3,2,1,0:T(8,128)S(1)} %get-tuple-element.30.y3, f32[4,4,40,128]{3,2,1,0:T(8,128)S(1)} %get-tuple-element.31.tail2, f32[24,4,40,128]{3,2,1,0:T(8,128)S(1)} %get-tuple-element.32.pq, ...), custom_call_target="tpu_custom_call" | custom-call | tf_op jit(solution)/shard_map/pallas_call | solution.py:616
  56.9 18.3 %all_to_all.23 = f32[256,1,128]{2,1,0:T(1,128)S(1)} all-to-all(f32[256,1,128]{2,1,0:T(1,128)S(1)} %bitcast.11), channel_id=1, replica_groups=mesh['gx_0'=4,'gx_1'=2,'gy'=4,'gz_0'=2,'gz_1'=4] {'gx_0','gx_1','gy','gz..., dimensions={0} | all-to-all | bytes 262144 | tf_op jit(solution)/shard_map/all_to_all | solution.py:677
  75.2 0.7 shard_map.48
Async XLA Ops:
  1.7 7.3 %collective-permute-start = (f32[4,4,16,128]{3,2,1,0:T(8,128)S(1)}, f32[4,4,16,128]{3,2,1,0:T(8,128)S(1)}, u32[]{:S(2)}, u32[]{:S(2)}) collective-permute-start(f32[4,4,16,128]{3,2,1,0:T(8,128)S(1)} %get-tuple-element.20), channel_id=1, source_target_pairs={{0,224},{32,64},{64,32},{96,128},{128,96},{160,192},{192,160},{224... | collective-permute-start | bytes 393224 | tf_op jit(solution)/shard_map/ppermute | solution.py:606
  6.2 3.9 %collective-permute-start.1 = (f32[4,4,16,128]{3,2,1,0:T(8,128)S(1)}, f32[4,4,16,128]{3,2,1,0:T(8,128)S(1)}, u32[]{:S(2)}, u32[]{:S(2)}) collective-permute-start(f32[4,4,16,128]{3,2,1,0:T(8,128)S(1)} %get-tuple-element.21), channel_id=1, source_target_pairs={{0,32},{32,0},{64,96},{96,64},{128,160},{160,128},{192,224},{224,1... | collective-permute-start | bytes 393224 | tf_op jit(solution)/shard_map/ppermute | solution.py:606
  10.1 5.8 %collective-permute-start.2 = (f32[4,12,8,128]{3,2,1,0:T(8,128)S(1)}, f32[4,12,8,128]{3,2,1,0:T(8,128)S(1)}, u32[]{:S(2)}, u32[]{:S(2)}) collective-permute-start(f32[4,12,8,128]{3,2,1,0:T(8,128)S(1)} %get-tuple-element.22), channel_id=1, source_target_pairs={{0,24},{8,16},{16,8},{24,0},{1,25},{9,17},{17,9},{25,1},{2,26},{10... | collective-permute-start | bytes 589832 | tf_op jit(solution)/shard_map/ppermute | solution.py:606
  12.6 4.5 %collective-permute-start.3 = (f32[4,12,8,128]{3,2,1,0:T(8,128)S(1)}, f32[4,12,8,128]{3,2,1,0:T(8,128)S(1)}, u32[]{:S(2)}, u32[]{:S(2)}) collective-permute-start(f32[4,12,8,128]{3,2,1,0:T(8,128)S(1)} %get-tuple-element.23), channel_id=1, source_target_pairs={{0,8},{8,0},{16,24},{24,16},{1,9},{9,1},{17,25},{25,17},{2,10},{10... | collective-permute-start | bytes 589832 | tf_op jit(solution)/shard_map/ppermute | solution.py:606
  17.4 6.1 %collective-permute-start.4 = (f32[4,24,128]{2,1,0:T(8,128)S(1)}, f32[4,24,128]{2,1,0:T(8,128)S(1)}, u32[]{:S(2)}, u32[]{:S(2)}) collective-permute-start(f32[4,24,128]{2,1,0:T(8,128)S(1)} %get-tuple-element.27.zfar_own), channel_id=1, source_target_pairs={{0,7},{1,2},{2,1},{3,4},{4,3},{5,6},{6,5},{7,0},{8,15},{9,10},{10,... | collective-permute-start | bytes 147464 | tf_op jit(solution)/shard_map/ppermute | solution.py:606
  20.7 2.9 %collective-permute-start.5 = (f32[4,24,128]{2,1,0:T(8,128)S(1)}, f32[4,24,128]{2,1,0:T(8,128)S(1)}, u32[]{:S(2)}, u32[]{:S(2)}) collective-permute-start(f32[4,24,128]{2,1,0:T(8,128)S(1)} %get-tuple-element.28.znear_own), channel_id=1, source_target_pairs={{0,1},{1,0},{2,3},{3,2},{4,5},{5,4},{6,7},{7,6},{8,9},{9,8},{10,11... | collective-permute-start | bytes 147464 | tf_op jit(solution)/shard_map/ppermute | solution.py:606

commit v5 on v4

--- a/solution.py
+++ b/solution.py
@@ -167,21 +167,21 @@
     return sums, v
 
 
-def planes(first, last, body, carry=0):
-    whole = first + (last - first) // 4 * 4
-
-    def four(k, carry):
-        for j in range(4):
-            carry = body(first + 4 * k + j, carry)
+def planes(first, last, body, carry=0, step=4):
+    whole = first + (last - first) // step * step
+
+    def some(k, carry):
+        for j in range(step):
+            carry = body(first + step * k + j, carry)
         return carry
 
-    carry = lax.fori_loop(0, (last - first) // 4, four, carry)
+    carry = lax.fori_loop(0, (last - first) // step, some, carry)
     for i in range(whole, last):
         carry = body(i, carry)
     return carry
 
 
-def sweep(source, target, pq, edges, first, last):
+def sweep(source, target, pq, edges, first, last, step=4):
     lane = lanes_of((8, 128))
 
     def plane(i, carry):
@@ -193,7 +193,7 @@
                 target[i, c, pl.ds(row, 8), :] = KEEP * v[c] + p + q * sums[c]
         return carry
 
-    planes(first, last, plane)
+    planes(first, last, plane, step=step)
 
 
 def x_pack_kernel(load, damage, f_out, far_out, near_out, level, load_sem, level_sem):
@@ -280,7 +280,7 @@
     put_z_pack(values, pl.ds(16, 8), position(GZ)[2], far_out, near_out)
 
 
-def main_kernel(f, xfar, xnear, yfar, ynear, pq, y3, columns, x2):
+def main_kernel(f, xfar, xnear, yfar, ynear, pq, y3, by_cell, x2):
     gx, gx_n, odd_x = position(GX)
     gy, gy_n, odd_y = position("gy")
     odd_x, odd_y = odd_x == 1, odd_y == 1
@@ -350,11 +350,15 @@
     for c in range(5):
         total = jnp.where(inner, totals[c], 0.0) if c < 3 else totals[c]
         stacked = jnp.where(row8 == c, jnp.sum(total, axis=0, keepdims=True), stacked)
-    columns[...] = stacked
+    big = (128, 128)
+    gather = (rows_of(big) // BLOCK == lanes_of(big) % 8).astype(F32)
+    by_cell[...] = jnp.dot(
+        stacked, gather, precision=lax.Precision.HIGHEST, preferred_element_type=F32
+    )
     sweep(x2, y3, pq, None, 2, NP - 2)
 
 
-def first_kernel(columns, zfar_own, znear_own, zfar, znear, tail, tail_pq, sums_out):
+def first_kernel(by_cell, zfar_own, znear_own, zfar, znear, tail, tail_pq, sums_out):
     lane = lanes_of((8, 128))
     row8 = rows_of((8, 128))
     gx, gx_n, _ = position(GX)
@@ -410,19 +414,11 @@
         for c in range(3):
             total = jnp.sum(jnp.where(here, totals[c], 0.0), axis=0, keepdims=True)
             ends = jnp.where(row8 == 3 * side + c, total, ends)
-    big = (128, 128)
-    gather = (rows_of(big) // BLOCK == lanes_of(big) % 8).astype(F32)
-    own = ((rows_of(big) >= W * W) & (rows_of(big) < W * (W + 16))).astype(F32)
-
-    def dot(a, b):
-        return jnp.dot(a, b, precision=lax.Precision.HIGHEST, preferred_element_type=F32)
-
     ends = jnp.where((lane >= W * W) & (lane < W * (W + 16)), ends, 0.0)
-    by_cell = dot(columns[...], gather)
-    by_end = dot(ends, own)
+    by_end = jnp.sum(ends, axis=1, keepdims=True)
     low_end = (lane % 8 == 0) & (lane // 8 == row8) & (row8 < 3)
     high_end = (lane % 8 == 7) & (lane // 8 + 3 == row8) & (row8 < 6)
-    slot = jnp.where(lane // 8 == row8, by_cell, 0.0) + jnp.where(
+    slot = jnp.where(lane // 8 == row8, by_cell[...], 0.0) + jnp.where(
         low_end | high_end, by_end, 0.0
     )
     sums_out[...] = jnp.broadcast_to(jnp.sum(slot, axis=0, keepdims=True), sums_out.shape)
@@ -484,6 +480,7 @@
     f,
     out,
     sum_out,
+    load_out,
     x3,
     x4,
     tail3,
@@ -502,7 +499,7 @@
     cells = jnp.transpose(every[...])
     load = [cells[8 * c : 8 * c + 8] for c in range(3)]
     mean = cells[24:32] * (1.0 / BLOCK**3)
-    load_sum = jnp.sum(cells[32:40])
+    load_out[...] = cells[32:40]
     w = coarse_solve(load, mean, gx_n, gy_n, gz_n)
     n = gx_n * gy_n * gz_n
     centre = n // 2
@@ -568,7 +565,7 @@
 
     planes(2, NP - 2, correct)
     tail_sweep(tail4, tail3, tail_pq, edges, True)
-    sweep(x4, x3, pq, edges, 3, NP - 3)
+    sweep(x4, x3, pq, edges, 3, NP - 3, 6)
     copies = [
         pltpu.make_async_copy(
             x3.at[pl.ds(W, 16), c, pl.ds(8, 16), :], out.at[c], out_sem.at[c]
@@ -592,9 +589,8 @@
                 total += r * r
         return total
 
-    total = jnp.sum(planes(W, W + 16, residual, jnp.zeros((8, 128), F32)))
-    both = jnp.where(line == 0, load_sum * (1.0 / n), total)
-    sum_out[...] = jnp.broadcast_to(both, sum_out.shape)
+    total = planes(W, W + 16, residual, jnp.zeros((8, 128), F32))
+    sum_out[...] = jnp.broadcast_to(jnp.sum(total, axis=0, keepdims=True), sum_out.shape)
     for copy in copies:
         copy.wait()
 
@@ -623,10 +619,11 @@
     )(*arguments)
 
 
-def norms_kernel(count, parts, out):
-    root = jnp.sqrt(jnp.sum(parts[...], axis=0, keepdims=True) * (1.0 / count))
-    out[0] = root[0, 0]
-    out[1] = root[0, 1]
+def norms_kernel(count, load_parts, residual_parts, out):
+    for k, parts in enumerate((load_parts, residual_parts)):
+        line = jnp.sum(parts[...], axis=0, keepdims=True)
+        total = jnp.sum(line, axis=1, keepdims=True)
+        out[k] = jnp.sqrt(total * (1.0 / count))[0, 0]
 
 
 def on_device(right_side, damage):
@@ -656,27 +653,27 @@
     z_pieces = swaps(*z_sends, GZ)
     field = (NP, 4, ROWS, 128)
     tails = (4, 4, ROWS, 128)
-    edges = (3, ROWS, 128)
-    pq, y3, columns = call(main_kernel, (field, field, (8, 128)), pieces, 12, (field,))
+    edges = (4, ROWS, 128)
+    pq, y3, by_cell = call(main_kernel, (field, field, (8, 128)), pieces, 12, (field,))
     tail, tail_pq, sums = call(
-        first_kernel, (tails, tails, (n, 128)), (columns, *z_sends, *z_pieces), 8
+        first_kernel, (tails, tails, (n, 128)), (by_cell, *z_sends, *z_pieces), 8
     )
     every = lax.all_to_all(sums, ALL, 0, 0, tiled=True)
-    displacement, partial_sums = call(
+    displacement, partial_sums, load_sums = call(
         second_kernel,
-        (right_side.shape, (n, 128)),
+        (right_side.shape, (n, 128), (8, n)),
         (every, y3, tail, pq, tail_pq, f),
         20,
         (
             *(field, field, tails, tails),
-            *((9, 4, ROWS, 128), (9, 4, ROWS, 128), edges),
+            *((12, 4, ROWS, 128), (12, 4, ROWS, 128), edges),
             pltpu.SemaphoreType.DMA((3,)),
         ),
-        target=(HBM, VMEM),
+        target=(HBM, VMEM, VMEM),
     )
     partial_sums = lax.all_to_all(partial_sums, ALL, 0, 0, tiled=True)
     (norms,) = call(
-        functools.partial(norms_kernel, right_side.size * n), ((2,),), (partial_sums,), 2, target=SMEM
+        functools.partial(norms_kernel, right_side.size * n), ((2,),), (load_sums, partial_sums), 2, target=SMEM
     )
     return (displacement, norms)
 

time: 76 us -> 75.8 us (level)
  transfers between devices with their start and end apart: 6 -> 6, of which waited for: 4 -> 3; matrix products, arithmetic and copies ran while one was open for 0% -> 0% of each run, Pallas kernels for 4% -> 5%
where the time goes in v5:
time: 75.8 us; the launch traced here: 75.6 us
  blocking collectives  45.7 us (60%)
  starting transfers between devices  13.2 us (17%)
  Pallas kernels  11 us (15%)
  waiting for transfers between devices  5.01 us (7%)
    all_to_all x1, blocking collectives, on_device(): every = lax.all_to_all(sums, ALL, 0, 0, tiled=True)  27.4 us
    all_to_all x1, blocking collectives, on_device(): partial_sums = lax.all_to_all(partial_sums, ALL, 0, 0, tiled=True)  18.3 us
    pallas_call x8, Pallas kernels, call(): pl.pallas_call(kernel, out_shape=tuple(shapes), in_specs=[source] * len(a...  11 us
    ppermute x3, starting transfers between devices, swaps(): lax.ppermute(far_send, axis, far)  10.3 us
    ppermute x3, starting transfers between devices, swaps(): lax.ppermute(near_send, axis, near)  2.87 us
    ppermute x3, waiting for transfers between devices, swaps(): lax.ppermute(far_send, axis, far)  2.76 us
    ppermute x3, waiting for transfers between devices, swaps(): lax.ppermute(near_send, axis, near)  2.25 us
  transfers between devices with their start and end apart: 6, of which 3 were waited for; matrix products, arithmetic and copies ran while one was open for 0% of the time, Pallas kernels for 5%

profile of v5, /device:TPU:1, one launch (start us, length us, event | category | flops | bytes accessed | tf_op | source)
XLA Modules:
  0.0 75.6 jit_solution(5624698176554491788)
XLA Ops:
  0.6 1.1 %shard_map.41 = (f32[4,16,16,128]{3,2,1,0:T(8,128)S(1)}, f32[4,4,16,128]{3,2,1,0:T(8,128)S(1)}, f32[4,4,16,128]{3,2,1,0:T(8,128)S(1)}) custom-call(f32[3,16,16,128]{3,2,1,0:T(8,128)} %load.1, s32[16,16,128]{2,1,0:T(8,128)} %damage.1), custom_call_target="tpu_custom_call" | custom-call | tf_op jit(solution)/shard_map/pallas_call | solution.py:612
  1.7 4.5 %collective-permute-start = (f32[4,4,16,128]{3,2,1,0:T(8,128)S(1)}, f32[4,4,16,128]{3,2,1,0:T(8,128)S(1)}, u32[]{:S(2)}, u32[]{:S(2)}) collective-permute-start(f32[4,4,16,128]{3,2,1,0:T(8,128)S(1)} %get-tuple-element.21), channel_id=1, source_target_pairs={{0,224},{32,64},{64,32},{96,128},{128,96},{160,192},{192,160},{224... | collective-permute-start | bytes 393224 | tf_op jit(solution)/shard_map/ppermute | solution.py:602
  6.2 2.9 %collective-permute-start.1 = (f32[4,4,16,128]{3,2,1,0:T(8,128)S(1)}, f32[4,4,16,128]{3,2,1,0:T(8,128)S(1)}, u32[]{:S(2)}, u32[]{:S(2)}) collective-permute-start(f32[4,4,16,128]{3,2,1,0:T(8,128)S(1)} %get-tuple-element.22), channel_id=1, source_target_pairs={{0,32},{32,0},{64,96},{96,64},{128,160},{160,128},{192,224},{224,1... | collective-permute-start | bytes 393224 | tf_op jit(solution)/shard_map/ppermute | solution.py:602
  9.0 0.0 collective-permute-done.xfar
  9.0 1.0 %collective-permute-done.1.xnear = f32[4,4,16,128]{3,2,1,0:T(8,128)S(1)} collective-permute-done((f32[4,4,16,128]{3,2,1,0:T(8,128)S(1)}, f32[4,4,16,128]{3,2,1,0:T(8,128)S(1)}, u32[]{:S(2)}, u32[]{:S(2)}) %collective-permute-start.1) | collective-permute-done | bytes 131104 | tf_op jit(solution)/shard_map/ppermute | solution.py:602
  10.0 0.1 shard_map.42
  10.1 2.6 %collective-permute-start.2 = (f32[4,12,8,128]{3,2,1,0:T(8,128)S(1)}, f32[4,12,8,128]{3,2,1,0:T(8,128)S(1)}, u32[]{:S(2)}, u32[]{:S(2)}) collective-permute-start(f32[4,12,8,128]{3,2,1,0:T(8,128)S(1)} %get-tuple-element.23), channel_id=1, source_target_pairs={{0,24},{8,16},{16,8},{24,0},{1,25},{9,17},{17,9},{25,1},{2,26},{10... | collective-permute-start | bytes 589832 | tf_op jit(solution)/shard_map/ppermute | solution.py:602
  12.6 0.0 collective-permute-start.3
  12.7 0.5 shard_map.44
  13.1 2.8 %collective-permute-done.2.yfar = f32[4,12,8,128]{3,2,1,0:T(8,128)S(1)} collective-permute-done((f32[4,12,8,128]{3,2,1,0:T(8,128)S(1)}, f32[4,12,8,128]{3,2,1,0:T(8,128)S(1)}, u32[]{:S(2)}, u32[]{:S(2)}) %collective-permute-start.2) | collective-permute-done | bytes 196640 | tf_op jit(solution)/shard_map/ppermute | solution.py:602
  15.9 1.3 %collective-permute-done.3.ynear = f32[4,12,8,128]{3,2,1,0:T(8,128)S(1)} collective-permute-done((f32[4,12,8,128]{3,2,1,0:T(8,128)S(1)}, f32[4,12,8,128]{3,2,1,0:T(8,128)S(1)}, u32[]{:S(2)}, u32[]{:S(2)}) %collective-permute-start.3) | collective-permute-done | bytes 196640 | tf_op jit(solution)/shard_map/ppermute | solution.py:602
  17.2 0.3 shard_map.45
  17.4 3.3 %collective-permute-start.4 = (f32[4,24,128]{2,1,0:T(8,128)S(1)}, f32[4,24,128]{2,1,0:T(8,128)S(1)}, u32[]{:S(2)}, u32[]{:S(2)}) collective-permute-start(f32[4,24,128]{2,1,0:T(8,128)S(1)} %get-tuple-element.28.zfar_own), channel_id=1, source_target_pairs={{0,7},{1,2},{2,1},{3,4},{4,3},{5,6},{6,5},{7,0},{8,15},{9,10},{10,... | collective-permute-start | bytes 147464 | tf_op jit(solution)/shard_map/ppermute | solution.py:602
  20.7 0.0 collective-permute-start.5
  20.7 3.0 %shard_map.43 = (f32[24,4,40,128]{3,2,1,0:T(8,128)S(1)}, f32[24,4,40,128]{3,2,1,0:T(8,128)S(1)}, f32[8,128]{1,0:T(8,128)S(1)}) custom-call(f32[4,16,16,128]{3,2,1,0:T(8,128)S(1)} %get-tuple-element.20.f, f32[4,4,16,128]{3,2,1,0:T(8,128)S(1)} %collective-permute-done.xfar, f32[4,4,16,128]{3,2,1,0:T(8,128)S(1)} %collective-permute-done.1.xnear, ...), custom_call_target="tpu_custom_call" | custom-call | tf_op jit(solution)/shard_map/pallas_call | solution.py:612
  23.7 0.0 collective-permute-done.4.zfar
  23.7 0.0 collective-permute-done.5.znear
  23.8 0.7 shard_map.46
  24.5 27.4 %all_to_all.22 = f32[256,1,128]{2,1,0:T(1,128)S(1)} all-to-all(f32[256,1,128]{2,1,0:T(1,128)S(1)} %bitcast.11), channel_id=1, replica_groups=mesh['gx_0'=4,'gx_1'=2,'gy'=4,'gz_0'=2,'gz_1'=4] {'gx_0','gx_1','gy','gz..., dimensions={0} | all-to-all | bytes 262144 | tf_op jit(solution)/shard_map/all_to_all | solution.py:661
  51.9 4.7 %shard_map.47 = (f32[3,16,16,128]{3,2,1,0:T(8,128)}, f32[256,128]{1,0:T(8,128)S(1)}, f32[8,256]{1,0:T(8,128)S(1)}) custom-call(f32[256,128]{1,0:T(8,128)S(1)} %bitcast.8, f32[24,4,40,128]{3,2,1,0:T(8,128)S(1)} %get-tuple-element.31.y3, f32[4,4,40,128]{3,2,1,0:T(8,128)S(1)} %get-tuple-element.32.tail2, f32[24,4,40,128]{3,2,1,0:T(8,128)S(1)} %get-tuple-element.33.pq, ...), custom_call_target="tpu_custom_call" | custom-call | tf_op jit(solution)/shard_map/pallas_call | solution.py:612
  56.7 18.3 %all_to_all.23 = f32[256,1,128]{2,1,0:T(1,128)S(1)} all-to-all(f32[256,1,128]{2,1,0:T(1,128)S(1)} %bitcast.10), channel_id=1, replica_groups=mesh['gx_0'=4,'gx_1'=2,'gy'=4,'gz_0'=2,'gz_1'=4] {'gx_0','gx_1','gy','gz..., dimensions={0} | all-to-all | bytes 262144 | tf_op jit(solution)/shard_map/all_to_all | solution.py:674
  74.9 0.7 shard_map.48
Async XLA Ops:
  1.7 7.3 %collective-permute-start = (f32[4,4,16,128]{3,2,1,0:T(8,128)S(1)}, f32[4,4,16,128]{3,2,1,0:T(8,128)S(1)}, u32[]{:S(2)}, u32[]{:S(2)}) collective-permute-start(f32[4,4,16,128]{3,2,1,0:T(8,128)S(1)} %get-tuple-element.21), channel_id=1, source_target_pairs={{0,224},{32,64},{64,32},{96,128},{128,96},{160,192},{192,160},{224... | collective-permute-start | bytes 393224 | tf_op jit(solution)/shard_map/ppermute | solution.py:602
  6.2 3.9 %collective-permute-start.1 = (f32[4,4,16,128]{3,2,1,0:T(8,128)S(1)}, f32[4,4,16,128]{3,2,1,0:T(8,128)S(1)}, u32[]{:S(2)}, u32[]{:S(2)}) collective-permute-start(f32[4,4,16,128]{3,2,1,0:T(8,128)S(1)} %get-tuple-element.22), channel_id=1, source_target_pairs={{0,32},{32,0},{64,96},{96,64},{128,160},{160,128},{192,224},{224,1... | collective-permute-start | bytes 393224 | tf_op jit(solution)/shard_map/ppermute | solution.py:602
  10.1 5.8 %collective-permute-start.2 = (f32[4,12,8,128]{3,2,1,0:T(8,128)S(1)}, f32[4,12,8,128]{3,2,1,0:T(8,128)S(1)}, u32[]{:S(2)}, u32[]{:S(2)}) collective-permute-start(f32[4,12,8,128]{3,2,1,0:T(8,128)S(1)} %get-tuple-element.23), channel_id=1, source_target_pairs={{0,24},{8,16},{16,8},{24,0},{1,25},{9,17},{17,9},{25,1},{2,26},{10... | collective-permute-start | bytes 589832 | tf_op jit(solution)/shard_map/ppermute | solution.py:602
  12.6 4.5 %collective-permute-start.3 = (f32[4,12,8,128]{3,2,1,0:T(8,128)S(1)}, f32[4,12,8,128]{3,2,1,0:T(8,128)S(1)}, u32[]{:S(2)}, u32[]{:S(2)}) collective-permute-start(f32[4,12,8,128]{3,2,1,0:T(8,128)S(1)} %get-tuple-element.24), channel_id=1, source_target_pairs={{0,8},{8,0},{16,24},{24,16},{1,9},{9,1},{17,25},{25,17},{2,10},{10... | collective-permute-start | bytes 589832 | tf_op jit(solution)/shard_map/ppermute | solution.py:602
  17.4 6.3 %collective-permute-start.4 = (f32[4,24,128]{2,1,0:T(8,128)S(1)}, f32[4,24,128]{2,1,0:T(8,128)S(1)}, u32[]{:S(2)}, u32[]{:S(2)}) collective-permute-start(f32[4,24,128]{2,1,0:T(8,128)S(1)} %get-tuple-element.28.zfar_own), channel_id=1, source_target_pairs={{0,7},{1,2},{2,1},{3,4},{4,3},{5,6},{6,5},{7,0},{8,15},{9,10},{10,... | collective-permute-start | bytes 147464 | tf_op jit(solution)/shard_map/ppermute | solution.py:602
  20.7 3.0 %collective-permute-start.5 = (f32[4,24,128]{2,1,0:T(8,128)S(1)}, f32[4,24,128]{2,1,0:T(8,128)S(1)}, u32[]{:S(2)}, u32[]{:S(2)}) collective-permute-start(f32[4,24,128]{2,1,0:T(8,128)S(1)} %get-tuple-element.29.znear_own), channel_id=1, source_target_pairs={{0,1},{1,0},{2,3},{3,2},{4,5},{5,4},{6,7},{7,6},{8,9},{9,8},{10,11... | collective-permute-start | bytes 147464 | tf_op jit(solution)/shard_map/ppermute | solution.py:602

commit v6 on v5

--- a/solution.py
+++ b/solution.py
@@ -468,7 +468,10 @@
             out.append(KEEP * w[a] + p[a] + q * (total + MIX * (up - down)))
         return tuple(out)
 
-    return lax.fori_loop(0, COARSE - 1, step, tuple(p))
+    w = tuple(p)
+    for k in range(COARSE - 1):
+        w = step(k, w)
+    return w
 
 
 def second_kernel(
@@ -589,7 +592,7 @@
                 total += r * r
         return total
 
-    total = planes(W, W + 16, residual, jnp.zeros((8, 128), F32))
+    total = planes(W, W + 16, residual, jnp.zeros((8, 128), F32), step=8)
     sum_out[...] = jnp.broadcast_to(jnp.sum(total, axis=0, keepdims=True), sum_out.shape)
     for copy in copies:
         copy.wait()

time: 75.8 us -> 75.6 us (level)
  no operation moved by 1% of the time
where the time goes in v6:
time: 75.6 us; the launch traced here: 75.4 us
  blocking collectives  45.7 us (60%)
  starting transfers between devices  13.2 us (17%)
  Pallas kernels  10.8 us (14%)
  waiting for transfers between devices  5.01 us (7%)
    all_to_all x1, blocking collectives, on_device(): every = lax.all_to_all(sums, ALL, 0, 0, tiled=True)  27.4 us
    all_to_all x1, blocking collectives, on_device(): partial_sums = lax.all_to_all(partial_sums, ALL, 0, 0, tiled=True)  18.3 us
    pallas_call x8, Pallas kernels, call(): pl.pallas_call(kernel, out_shape=tuple(shapes), in_specs=[source] * len(a...  10.8 us
    ppermute x3, starting transfers between devices, swaps(): lax.ppermute(far_send, axis, far)  10.3 us
    ppermute x3, starting transfers between devices, swaps(): lax.ppermute(near_send, axis, near)  2.87 us
    ppermute x3, waiting for transfers between devices, swaps(): lax.ppermute(far_send, axis, far)  2.76 us
    ppermute x3, waiting for transfers between devices, swaps(): lax.ppermute(near_send, axis, near)  2.25 us
  transfers between devices with their start and end apart: 6, of which 3 were waited for; matrix products, arithmetic and copies ran while one was open for 0% of the time, Pallas kernels for 5%

profile of v6, /device:TPU:1, one launch (start us, length us, event | category | flops | bytes accessed | tf_op | source)
XLA Modules:
  0.0 75.4 jit_solution(15416341077448158527)
XLA Ops:
  0.6 1.1 %shard_map.41 = (f32[4,16,16,128]{3,2,1,0:T(8,128)S(1)}, f32[4,4,16,128]{3,2,1,0:T(8,128)S(1)}, f32[4,4,16,128]{3,2,1,0:T(8,128)S(1)}) custom-call(f32[3,16,16,128]{3,2,1,0:T(8,128)} %load.1, s32[16,16,128]{2,1,0:T(8,128)} %damage.1), custom_call_target="tpu_custom_call" | custom-call | tf_op jit(solution)/shard_map/pallas_call | solution.py:615
  1.7 4.5 %collective-permute-start = (f32[4,4,16,128]{3,2,1,0:T(8,128)S(1)}, f32[4,4,16,128]{3,2,1,0:T(8,128)S(1)}, u32[]{:S(2)}, u32[]{:S(2)}) collective-permute-start(f32[4,4,16,128]{3,2,1,0:T(8,128)S(1)} %get-tuple-element.21), channel_id=1, source_target_pairs={{0,224},{32,64},{64,32},{96,128},{128,96},{160,192},{192,160},{224... | collective-permute-start | bytes 393224 | tf_op jit(solution)/shard_map/ppermute | solution.py:605
  6.2 2.9 %collective-permute-start.1 = (f32[4,4,16,128]{3,2,1,0:T(8,128)S(1)}, f32[4,4,16,128]{3,2,1,0:T(8,128)S(1)}, u32[]{:S(2)}, u32[]{:S(2)}) collective-permute-start(f32[4,4,16,128]{3,2,1,0:T(8,128)S(1)} %get-tuple-element.22), channel_id=1, source_target_pairs={{0,32},{32,0},{64,96},{96,64},{128,160},{160,128},{192,224},{224,1... | collective-permute-start | bytes 393224 | tf_op jit(solution)/shard_map/ppermute | solution.py:605
  9.0 0.0 collective-permute-done.xfar
  9.0 1.0 %collective-permute-done.1.xnear = f32[4,4,16,128]{3,2,1,0:T(8,128)S(1)} collective-permute-done((f32[4,4,16,128]{3,2,1,0:T(8,128)S(1)}, f32[4,4,16,128]{3,2,1,0:T(8,128)S(1)}, u32[]{:S(2)}, u32[]{:S(2)}) %collective-permute-start.1) | collective-permute-done | bytes 131104 | tf_op jit(solution)/shard_map/ppermute | solution.py:605
  10.0 0.1 shard_map.42
  10.1 2.6 %collective-permute-start.2 = (f32[4,12,8,128]{3,2,1,0:T(8,128)S(1)}, f32[4,12,8,128]{3,2,1,0:T(8,128)S(1)}, u32[]{:S(2)}, u32[]{:S(2)}) collective-permute-start(f32[4,12,8,128]{3,2,1,0:T(8,128)S(1)} %get-tuple-element.23), channel_id=1, source_target_pairs={{0,24},{8,16},{16,8},{24,0},{1,25},{9,17},{17,9},{25,1},{2,26},{10... | collective-permute-start | bytes 589832 | tf_op jit(solution)/shard_map/ppermute | solution.py:605
  12.6 0.0 collective-permute-start.3
  12.7 0.5 shard_map.44
  13.1 2.8 %collective-permute-done.2.yfar = f32[4,12,8,128]{3,2,1,0:T(8,128)S(1)} collective-permute-done((f32[4,12,8,128]{3,2,1,0:T(8,128)S(1)}, f32[4,12,8,128]{3,2,1,0:T(8,128)S(1)}, u32[]{:S(2)}, u32[]{:S(2)}) %collective-permute-start.2) | collective-permute-done | bytes 196640 | tf_op jit(solution)/shard_map/ppermute | solution.py:605
  15.9 1.3 %collective-permute-done.3.ynear = f32[4,12,8,128]{3,2,1,0:T(8,128)S(1)} collective-permute-done((f32[4,12,8,128]{3,2,1,0:T(8,128)S(1)}, f32[4,12,8,128]{3,2,1,0:T(8,128)S(1)}, u32[]{:S(2)}, u32[]{:S(2)}) %collective-permute-start.3) | collective-permute-done | bytes 196640 | tf_op jit(solution)/shard_map/ppermute | solution.py:605
  17.2 0.3 shard_map.45
  17.4 3.3 %collective-permute-start.4 = (f32[4,24,128]{2,1,0:T(8,128)S(1)}, f32[4,24,128]{2,1,0:T(8,128)S(1)}, u32[]{:S(2)}, u32[]{:S(2)}) collective-permute-start(f32[4,24,128]{2,1,0:T(8,128)S(1)} %get-tuple-element.28.zfar_own), channel_id=1, source_target_pairs={{0,7},{1,2},{2,1},{3,4},{4,3},{5,6},{6,5},{7,0},{8,15},{9,10},{10,... | collective-permute-start | bytes 147464 | tf_op jit(solution)/shard_map/ppermute | solution.py:605
  20.7 0.0 collective-permute-start.5
  20.7 3.0 %shard_map.43 = (f32[24,4,40,128]{3,2,1,0:T(8,128)S(1)}, f32[24,4,40,128]{3,2,1,0:T(8,128)S(1)}, f32[8,128]{1,0:T(8,128)S(1)}) custom-call(f32[4,16,16,128]{3,2,1,0:T(8,128)S(1)} %get-tuple-element.20.f, f32[4,4,16,128]{3,2,1,0:T(8,128)S(1)} %collective-permute-done.xfar, f32[4,4,16,128]{3,2,1,0:T(8,128)S(1)} %collective-permute-done.1.xnear, ...), custom_call_target="tpu_custom_call" | custom-call | tf_op jit(solution)/shard_map/pallas_call | solution.py:615
  23.7 0.0 collective-permute-done.4.zfar
  23.7 0.0 collective-permute-done.5.znear
  23.8 0.7 shard_map.46
  24.5 27.4 %all_to_all.22 = f32[256,1,128]{2,1,0:T(1,128)S(1)} all-to-all(f32[256,1,128]{2,1,0:T(1,128)S(1)} %bitcast.11), channel_id=1, replica_groups=mesh['gx_0'=4,'gx_1'=2,'gy'=4,'gz_0'=2,'gz_1'=4] {'gx_0','gx_1','gy','gz..., dimensions={0} | all-to-all | bytes 262144 | tf_op jit(solution)/shard_map/all_to_all | solution.py:664
  51.9 4.5 %shard_map.47 = (f32[3,16,16,128]{3,2,1,0:T(8,128)}, f32[256,128]{1,0:T(8,128)S(1)}, f32[8,256]{1,0:T(8,128)S(1)}) custom-call(f32[256,128]{1,0:T(8,128)S(1)} %bitcast.8, f32[24,4,40,128]{3,2,1,0:T(8,128)S(1)} %get-tuple-element.31.y3, f32[4,4,40,128]{3,2,1,0:T(8,128)S(1)} %get-tuple-element.32.tail2, f32[24,4,40,128]{3,2,1,0:T(8,128)S(1)} %get-tuple-element.33.pq, ...), custom_call_target="tpu_custom_call" | custom-call | tf_op jit(solution)/shard_map/pallas_call | solution.py:615
  56.4 18.3 %all_to_all.23 = f32[256,1,128]{2,1,0:T(1,128)S(1)} all-to-all(f32[256,1,128]{2,1,0:T(1,128)S(1)} %bitcast.10), channel_id=1, replica_groups=mesh['gx_0'=4,'gx_1'=2,'gy'=4,'gz_0'=2,'gz_1'=4] {'gx_0','gx_1','gy','gz..., dimensions={0} | all-to-all | bytes 262144 | tf_op jit(solution)/shard_map/all_to_all | solution.py:677
  74.7 0.7 shard_map.48
Async XLA Ops:
  1.7 7.3 %collective-permute-start = (f32[4,4,16,128]{3,2,1,0:T(8,128)S(1)}, f32[4,4,16,128]{3,2,1,0:T(8,128)S(1)}, u32[]{:S(2)}, u32[]{:S(2)}) collective-permute-start(f32[4,4,16,128]{3,2,1,0:T(8,128)S(1)} %get-tuple-element.21), channel_id=1, source_target_pairs={{0,224},{32,64},{64,32},{96,128},{128,96},{160,192},{192,160},{224... | collective-permute-start | bytes 393224 | tf_op jit(solution)/shard_map/ppermute | solution.py:605
  6.2 3.9 %collective-permute-start.1 = (f32[4,4,16,128]{3,2,1,0:T(8,128)S(1)}, f32[4,4,16,128]{3,2,1,0:T(8,128)S(1)}, u32[]{:S(2)}, u32[]{:S(2)}) collective-permute-start(f32[4,4,16,128]{3,2,1,0:T(8,128)S(1)} %get-tuple-element.22), channel_id=1, source_target_pairs={{0,32},{32,0},{64,96},{96,64},{128,160},{160,128},{192,224},{224,1... | collective-permute-start | bytes 393224 | tf_op jit(solution)/shard_map/ppermute | solution.py:605
  10.1 5.8 %collective-permute-start.2 = (f32[4,12,8,128]{3,2,1,0:T(8,128)S(1)}, f32[4,12,8,128]{3,2,1,0:T(8,128)S(1)}, u32[]{:S(2)}, u32[]{:S(2)}) collective-permute-start(f32[4,12,8,128]{3,2,1,0:T(8,128)S(1)} %get-tuple-element.23), channel_id=1, source_target_pairs={{0,24},{8,16},{16,8},{24,0},{1,25},{9,17},{17,9},{25,1},{2,26},{10... | collective-permute-start | bytes 589832 | tf_op jit(solution)/shard_map/ppermute | solution.py:605
  12.6 4.5 %collective-permute-start.3 = (f32[4,12,8,128]{3,2,1,0:T(8,128)S(1)}, f32[4,12,8,128]{3,2,1,0:T(8,128)S(1)}, u32[]{:S(2)}, u32[]{:S(2)}) collective-permute-start(f32[4,12,8,128]{3,2,1,0:T(8,128)S(1)} %get-tuple-element.24), channel_id=1, source_target_pairs={{0,8},{8,0},{16,24},{24,16},{1,9},{9,1},{17,25},{25,17},{2,10},{10... | collective-permute-start | bytes 589832 | tf_op jit(solution)/shard_map/ppermute | solution.py:605
  17.4 6.3 %collective-permute-start.4 = (f32[4,24,128]{2,1,0:T(8,128)S(1)}, f32[4,24,128]{2,1,0:T(8,128)S(1)}, u32[]{:S(2)}, u32[]{:S(2)}) collective-permute-start(f32[4,24,128]{2,1,0:T(8,128)S(1)} %get-tuple-element.28.zfar_own), channel_id=1, source_target_pairs={{0,7},{1,2},{2,1},{3,4},{4,3},{5,6},{6,5},{7,0},{8,15},{9,10},{10,... | collective-permute-start | bytes 147464 | tf_op jit(solution)/shard_map/ppermute | solution.py:605
  20.7 3.0 %collective-permute-start.5 = (f32[4,24,128]{2,1,0:T(8,128)S(1)}, f32[4,24,128]{2,1,0:T(8,128)S(1)}, u32[]{:S(2)}, u32[]{:S(2)}) collective-permute-start(f32[4,24,128]{2,1,0:T(8,128)S(1)} %get-tuple-element.29.znear_own), channel_id=1, source_target_pairs={{0,1},{1,0},{2,3},{3,2},{4,5},{5,4},{6,7},{7,6},{8,9},{9,8},{10,11... | collective-permute-start | bytes 147464 | tf_op jit(solution)/shard_map/ppermute | solution.py:605

commit v7 on v6

--- a/solution.py
+++ b/solution.py
@@ -325,7 +325,7 @@
         return carry
 
     lax.fori_loop(0, NP // 2, beside_y, 0)
-    sweep(pq, x2, pq, None, 1, NP - 1)
+    sweep(pq, x2, pq, None, 1, NP - 1, 11)
     lane = lanes_of((8, 128))
     row8 = rows_of((8, 128))
 
@@ -344,7 +344,7 @@
         return tuple(totals)
 
     zero = jnp.zeros((8, 128), F32)
-    totals = planes(W, W + 16, residual, (zero,) * 5)
+    totals = planes(W, W + 16, residual, (zero,) * 5, step=8)
     stacked = zero
     inner = (lane >= 2) & (lane < 126)
     for c in range(5):
@@ -355,7 +355,7 @@
     by_cell[...] = jnp.dot(
         stacked, gather, precision=lax.Precision.HIGHEST, preferred_element_type=F32
     )
-    sweep(x2, y3, pq, None, 2, NP - 2)
+    sweep(x2, y3, pq, None, 2, NP - 2, 10)
 
 
 def first_kernel(by_cell, zfar_own, znear_own, zfar, znear, tail, tail_pq, sums_out):

time: 75.6 us -> 75.6 us (level)
  transfers between devices with their start and end apart: 6 -> 6, of which waited for: 3 -> 4; matrix products, arithmetic and copies ran while one was open for 0% -> 0% of each run, Pallas kernels for 5% -> 4%
where the time goes in v7:
time: 75.6 us; the launch traced here: 75.4 us
  blocking collectives  45.8 us (61%)
  starting transfers between devices  13.2 us (17%)
  Pallas kernels  10.3 us (14%)
  waiting for transfers between devices  5.44 us (7%)
    all_to_all x1, blocking collectives, on_device(): every = lax.all_to_all(sums, ALL, 0, 0, tiled=True)  27.5 us
    all_to_all x1, blocking collectives, on_device(): partial_sums = lax.all_to_all(partial_sums, ALL, 0, 0, tiled=True)  18.3 us
    ppermute x3, starting transfers between devices, swaps(): lax.ppermute(far_send, axis, far)  10.3 us
    pallas_call x8, Pallas kernels, call(): pl.pallas_call(kernel, out_shape=tuple(shapes), in_specs=[source] * len(a...  10.3 us
    ppermute x3, starting transfers between devices, swaps(): lax.ppermute(near_send, axis, near)  2.87 us
    ppermute x3, waiting for transfers between devices, swaps(): lax.ppermute(far_send, axis, far)  2.76 us
    ppermute x3, waiting for transfers between devices, swaps(): lax.ppermute(near_send, axis, near)  2.68 us
  transfers between devices with their start and end apart: 6, of which 4 were waited for; matrix products, arithmetic and copies ran while one was open for 0% of the time, Pallas kernels for 4%

profile of v7, /device:TPU:1, one launch (start us, length us, event | category | flops | bytes accessed | tf_op | source)
XLA Modules:
  0.0 75.4 jit_solution(15820292108737142932)
XLA Ops:
  0.6 1.1 %shard_map.41 = (f32[4,16,16,128]{3,2,1,0:T(8,128)S(1)}, f32[4,4,16,128]{3,2,1,0:T(8,128)S(1)}, f32[4,4,16,128]{3,2,1,0:T(8,128)S(1)}) custom-call(f32[3,16,16,128]{3,2,1,0:T(8,128)} %load.1, s32[16,16,128]{2,1,0:T(8,128)} %damage.1), custom_call_target="tpu_custom_call" | custom-call | tf_op jit(solution)/shard_map/pallas_call | solution.py:615
  1.7 4.5 %collective-permute-start = (f32[4,4,16,128]{3,2,1,0:T(8,128)S(1)}, f32[4,4,16,128]{3,2,1,0:T(8,128)S(1)}, u32[]{:S(2)}, u32[]{:S(2)}) collective-permute-start(f32[4,4,16,128]{3,2,1,0:T(8,128)S(1)} %get-tuple-element.21), channel_id=1, source_target_pairs={{0,224},{32,64},{64,32},{96,128},{128,96},{160,192},{192,160},{224... | collective-permute-start | bytes 393224 | tf_op jit(solution)/shard_map/ppermute | solution.py:605
  6.2 2.9 %collective-permute-start.1 = (f32[4,4,16,128]{3,2,1,0:T(8,128)S(1)}, f32[4,4,16,128]{3,2,1,0:T(8,128)S(1)}, u32[]{:S(2)}, u32[]{:S(2)}) collective-permute-start(f32[4,4,16,128]{3,2,1,0:T(8,128)S(1)} %get-tuple-element.22), channel_id=1, source_target_pairs={{0,32},{32,0},{64,96},{96,64},{128,160},{160,128},{192,224},{224,1... | collective-permute-start | bytes 393224 | tf_op jit(solution)/shard_map/ppermute | solution.py:605
  9.0 0.0 collective-permute-done.xfar
  9.0 1.0 %collective-permute-done.1.xnear = f32[4,4,16,128]{3,2,1,0:T(8,128)S(1)} collective-permute-done((f32[4,4,16,128]{3,2,1,0:T(8,128)S(1)}, f32[4,4,16,128]{3,2,1,0:T(8,128)S(1)}, u32[]{:S(2)}, u32[]{:S(2)}) %collective-permute-start.1) | collective-permute-done | bytes 131104 | tf_op jit(solution)/shard_map/ppermute | solution.py:605
  10.0 0.1 shard_map.42
  10.1 2.6 %collective-permute-start.2 = (f32[4,12,8,128]{3,2,1,0:T(8,128)S(1)}, f32[4,12,8,128]{3,2,1,0:T(8,128)S(1)}, u32[]{:S(2)}, u32[]{:S(2)}) collective-permute-start(f32[4,12,8,128]{3,2,1,0:T(8,128)S(1)} %get-tuple-element.23), channel_id=1, source_target_pairs={{0,24},{8,16},{16,8},{24,0},{1,25},{9,17},{17,9},{25,1},{2,26},{10... | collective-permute-start | bytes 589832 | tf_op jit(solution)/shard_map/ppermute | solution.py:605
  12.6 0.0 collective-permute-start.3
  12.7 0.5 shard_map.44
  13.1 2.8 %collective-permute-done.2.yfar = f32[4,12,8,128]{3,2,1,0:T(8,128)S(1)} collective-permute-done((f32[4,12,8,128]{3,2,1,0:T(8,128)S(1)}, f32[4,12,8,128]{3,2,1,0:T(8,128)S(1)}, u32[]{:S(2)}, u32[]{:S(2)}) %collective-permute-start.2) | collective-permute-done | bytes 196640 | tf_op jit(solution)/shard_map/ppermute | solution.py:605
  15.9 1.3 %collective-permute-done.3.ynear = f32[4,12,8,128]{3,2,1,0:T(8,128)S(1)} collective-permute-done((f32[4,12,8,128]{3,2,1,0:T(8,128)S(1)}, f32[4,12,8,128]{3,2,1,0:T(8,128)S(1)}, u32[]{:S(2)}, u32[]{:S(2)}) %collective-permute-start.3) | collective-permute-done | bytes 196640 | tf_op jit(solution)/shard_map/ppermute | solution.py:605
  17.2 0.3 shard_map.45
  17.4 3.3 %collective-permute-start.4 = (f32[4,24,128]{2,1,0:T(8,128)S(1)}, f32[4,24,128]{2,1,0:T(8,128)S(1)}, u32[]{:S(2)}, u32[]{:S(2)}) collective-permute-start(f32[4,24,128]{2,1,0:T(8,128)S(1)} %get-tuple-element.28.zfar_own), channel_id=1, source_target_pairs={{0,7},{1,2},{2,1},{3,4},{4,3},{5,6},{6,5},{7,0},{8,15},{9,10},{10,... | collective-permute-start | bytes 147464 | tf_op jit(solution)/shard_map/ppermute | solution.py:605
  20.7 0.0 collective-permute-start.5
  20.7 2.5 %shard_map.43 = (f32[24,4,40,128]{3,2,1,0:T(8,128)S(1)}, f32[24,4,40,128]{3,2,1,0:T(8,128)S(1)}, f32[8,128]{1,0:T(8,128)S(1)}) custom-call(f32[4,16,16,128]{3,2,1,0:T(8,128)S(1)} %get-tuple-element.20.f, f32[4,4,16,128]{3,2,1,0:T(8,128)S(1)} %collective-permute-done.xfar, f32[4,4,16,128]{3,2,1,0:T(8,128)S(1)} %collective-permute-done.1.xnear, ...), custom_call_target="tpu_custom_call" | custom-call | tf_op jit(solution)/shard_map/pallas_call | solution.py:615
  23.2 0.0 collective-permute-done.4.zfar
  23.2 0.4 collective-permute-done.5.znear
  23.7 0.7 shard_map.46
  24.4 27.5 %all_to_all.22 = f32[256,1,128]{2,1,0:T(1,128)S(1)} all-to-all(f32[256,1,128]{2,1,0:T(1,128)S(1)} %bitcast.11), channel_id=1, replica_groups=mesh['gx_0'=4,'gx_1'=2,'gy'=4,'gz_0'=2,'gz_1'=4] {'gx_0','gx_1','gy','gz..., dimensions={0} | all-to-all | bytes 262144 | tf_op jit(solution)/shard_map/all_to_all | solution.py:664
  51.9 4.5 %shard_map.47 = (f32[3,16,16,128]{3,2,1,0:T(8,128)}, f32[256,128]{1,0:T(8,128)S(1)}, f32[8,256]{1,0:T(8,128)S(1)}) custom-call(f32[256,128]{1,0:T(8,128)S(1)} %bitcast.8, f32[24,4,40,128]{3,2,1,0:T(8,128)S(1)} %get-tuple-element.31.y3, f32[4,4,40,128]{3,2,1,0:T(8,128)S(1)} %get-tuple-element.32.tail2, f32[24,4,40,128]{3,2,1,0:T(8,128)S(1)} %get-tuple-element.33.pq, ...), custom_call_target="tpu_custom_call" | custom-call | tf_op jit(solution)/shard_map/pallas_call | solution.py:615
  56.4 18.3 %all_to_all.23 = f32[256,1,128]{2,1,0:T(1,128)S(1)} all-to-all(f32[256,1,128]{2,1,0:T(1,128)S(1)} %bitcast.10), channel_id=1, replica_groups=mesh['gx_0'=4,'gx_1'=2,'gy'=4,'gz_0'=2,'gz_1'=4] {'gx_0','gx_1','gy','gz..., dimensions={0} | all-to-all | bytes 262144 | tf_op jit(solution)/shard_map/all_to_all | solution.py:677
  74.7 0.7 shard_map.48
Async XLA Ops:
  1.7 7.3 %collective-permute-start = (f32[4,4,16,128]{3,2,1,0:T(8,128)S(1)}, f32[4,4,16,128]{3,2,1,0:T(8,128)S(1)}, u32[]{:S(2)}, u32[]{:S(2)}) collective-permute-start(f32[4,4,16,128]{3,2,1,0:T(8,128)S(1)} %get-tuple-element.21), channel_id=1, source_target_pairs={{0,224},{32,64},{64,32},{96,128},{128,96},{160,192},{192,160},{224... | collective-permute-start | bytes 393224 | tf_op jit(solution)/shard_map/ppermute | solution.py:605
  6.2 3.9 %collective-permute-start.1 = (f32[4,4,16,128]{3,2,1,0:T(8,128)S(1)}, f32[4,4,16,128]{3,2,1,0:T(8,128)S(1)}, u32[]{:S(2)}, u32[]{:S(2)}) collective-permute-start(f32[4,4,16,128]{3,2,1,0:T(8,128)S(1)} %get-tuple-element.22), channel_id=1, source_target_pairs={{0,32},{32,0},{64,96},{96,64},{128,160},{160,128},{192,224},{224,1... | collective-permute-start | bytes 393224 | tf_op jit(solution)/shard_map/ppermute | solution.py:605
  10.1 5.8 %collective-permute-start.2 = (f32[4,12,8,128]{3,2,1,0:T(8,128)S(1)}, f32[4,12,8,128]{3,2,1,0:T(8,128)S(1)}, u32[]{:S(2)}, u32[]{:S(2)}) collective-permute-start(f32[4,12,8,128]{3,2,1,0:T(8,128)S(1)} %get-tuple-element.23), channel_id=1, source_target_pairs={{0,24},{8,16},{16,8},{24,0},{1,25},{9,17},{17,9},{25,1},{2,26},{10... | collective-permute-start | bytes 589832 | tf_op jit(solution)/shard_map/ppermute | solution.py:605
  12.6 4.5 %collective-permute-start.3 = (f32[4,12,8,128]{3,2,1,0:T(8,128)S(1)}, f32[4,12,8,128]{3,2,1,0:T(8,128)S(1)}, u32[]{:S(2)}, u32[]{:S(2)}) collective-permute-start(f32[4,12,8,128]{3,2,1,0:T(8,128)S(1)} %get-tuple-element.24), channel_id=1, source_target_pairs={{0,8},{8,0},{16,24},{24,16},{1,9},{9,1},{17,25},{25,17},{2,10},{10... | collective-permute-start | bytes 589832 | tf_op jit(solution)/shard_map/ppermute | solution.py:605
  17.4 5.8 %collective-permute-start.4 = (f32[4,24,128]{2,1,0:T(8,128)S(1)}, f32[4,24,128]{2,1,0:T(8,128)S(1)}, u32[]{:S(2)}, u32[]{:S(2)}) collective-permute-start(f32[4,24,128]{2,1,0:T(8,128)S(1)} %get-tuple-element.28.zfar_own), channel_id=1, source_target_pairs={{0,7},{1,2},{2,1},{3,4},{4,3},{5,6},{6,5},{7,0},{8,15},{9,10},{10,... | collective-permute-start | bytes 147464 | tf_op jit(solution)/shard_map/ppermute | solution.py:605
  20.7 2.9 %collective-permute-start.5 = (f32[4,24,128]{2,1,0:T(8,128)S(1)}, f32[4,24,128]{2,1,0:T(8,128)S(1)}, u32[]{:S(2)}, u32[]{:S(2)}) collective-permute-start(f32[4,24,128]{2,1,0:T(8,128)S(1)} %get-tuple-element.29.znear_own), channel_id=1, source_target_pairs={{0,1},{1,0},{2,3},{3,2},{4,5},{5,4},{6,7},{7,6},{8,9},{9,8},{10,11... | collective-permute-start | bytes 147464 | tf_op jit(solution)/shard_map/ppermute | solution.py:605
